TPU v7x, 32 devices: a whole 2x2x4 slice. The times are simulated.
32 devices in a mesh: gx: 4 (over z), gy: 2 (over core), gz: 4 (over y, x).
Axes of the slice: x: 2, y: 2, z: 4, core: 2. Of those that a mesh axis runs over, the one named last changes fastest.
Arguments:
- pair: bfloat16 [128, 512, 512], P('gz', 'gx', 'gy'), may hold values from -6 to 6
- pair_mask: int32 [512, 512], P('gx', 'gy'), may hold values from 0 to 1, as said below
- input_gain: float32 [128], replicated, may hold values from 0.1 to 1.9
- input_weights: bfloat16 [4, 128, 128], replicated, may hold values from -0.5 to 0.5
- out_gate_weight: bfloat16 [128, 128], replicated, may hold values from -0.5 to 0.5
- hidden_gain: float32 [128], replicated, may hold values from 0.1 to 1.9
- out_weight: bfloat16 [128, 128], replicated, may hold values from -0.5 to 0.5
Outputs:
- update: bfloat16 [128, 512, 512], P('gz', 'gx', 'gy')
Inputs may be any that keep to these rules, and one draw needn't show every extreme that they name: pair_mask[r, s] = m[r] * m[s] for a 0/1 residue mask m of the draw that is 0 for all r >= L, for one crop length L with 256 < L <= 512; residues below L may also be 0.
All inputs are finite; a program needn't handle non-finite values.
Results may differ from a plain program's by a relative error of at most 0.011.
Values may be sent and summed in bfloat16 or wider, within the bound.
No kernel may reach another device: no remote copies, remote signals or barrier semaphores. Data moves between devices by JAX's collectives and lax.ppermute only.
A program may use at most 64 MiB of HBM per device.

v0:
```python
import jax
import jax.numpy as jnp
from jax import lax
from jax.sharding import PartitionSpec as P

EPSILON = 1e-05


def block_order(own, count, width, first, size):
    blocks = own ^ jnp.arange(count)
    return (blocks[:, None] * width + first + jnp.arange(size)[None, :]).reshape(-1)


def take_exact(order, matrix, axis):
    size = matrix.shape[axis]
    hot = (order[:, None] == jnp.arange(size)[None, :]).astype(matrix.dtype)
    moved = jnp.moveaxis(matrix, axis, -1)
    out = jnp.einsum("...c,ac->...a", moved, hot, preferred_element_type=jnp.float32)
    return jnp.moveaxis(out.astype(matrix.dtype), -1, axis)


def take_vector(order, vector):
    hot = order[:, None] == jnp.arange(vector.shape[0])[None, :]
    return jnp.sum(jnp.where(hot, vector[None, :], 0.0), axis=1)


def after(value, *others):
    return lax.optimization_barrier((value, *others))[0]


def shards(pair, pair_mask, input_gain, input_weights, out_gate_weight, hidden_gain, out_weight):
    bf16, f32 = jnp.bfloat16, jnp.float32
    local_channels, rows, columns = pair.shape
    channels, hidden = input_gain.shape[0], hidden_gain.shape[0]
    depth, planes = lax.axis_size("gx"), lax.axis_size("gz")
    half_depth = depth // 2
    group = half_depth * planes
    sub_rows = rows // planes
    sub_hidden = hidden // group
    z, core, g = lax.axis_index("gx"), lax.axis_index("gy"), lax.axis_index("gz")
    half, inner = z // half_depth, z % half_depth
    place = inner * planes + g
    chunks = [(0, sub_hidden // 2, 1), (sub_hidden // 2, sub_hidden // 2, 2)]
    pieces = 2

    def across_gz(block, m):
        return lax.ppermute(block, "gz", [(i, i ^ m) for i in range(planes)]) if m else block

    def across_group(block, m):
        if not m:
            return block
        pairs = []
        for a in range(depth):
            for b in range(planes):
                to = (a % half_depth * planes + b) ^ m
                pairs.append((a * planes + b, (a // half_depth * half_depth + to // planes) * planes + to % planes))
        return lax.ppermute(block, ("gx", "gz"), pairs)

    def across_halves(block):
        return lax.ppermute(block, "gx", [(i, (i + half_depth) % depth) for i in range(depth)])

    by_row = jnp.transpose(pair, (1, 0, 2))
    row_block = lambda m: lax.dynamic_slice_in_dim(by_row, (g ^ m) * sub_rows, sub_rows, 0)
    received = [across_gz(row_block(m), m) for m in range(planes)]
    channel_order = block_order(g, planes, local_channels, 0, local_channels)
    gains = take_vector(channel_order, input_gain)
    values = jnp.concatenate(received, axis=1).astype(f32)
    centred = values - jnp.mean(values, axis=1, keepdims=True)
    spread = jnp.mean(centred * centred, axis=1, keepdims=True)
    normed = (centred * lax.rsqrt(spread + EPSILON) * gains[None, :, None]).astype(bf16)
    own_mask = lax.dynamic_slice_in_dim(pair_mask, g * sub_rows, sub_rows, 0).astype(f32)
    own_weights = take_exact(channel_order, input_weights, 1)
    mine = core == half
    hidden_order = jnp.concatenate([block_order(place, group, sub_hidden, first, size) for first, size, _ in chunks])
    hidden_gains = take_vector(hidden_order, hidden_gain)
    projection = take_exact(hidden_order, take_exact(channel_order, out_weight, 1), 0)
    gate_weights = take_exact(channel_order, take_exact(channel_order, out_gate_weight, 0), 1)
    turned = normed
    last_sent = None
    pending = []
    for first, size, split in chunks:
        order = block_order(place, group, sub_hidden, first, size)
        weights = take_exact(order, own_weights, 2)
        gates, sides = (
            jnp.concatenate(
                [weights[a].reshape(channels, group, 1, size), weights[a + 2].reshape(channels, group, 1, size)], 2
            ).reshape(channels, 2 * group * size)
            for a in (0, 1)
        )
        product = lambda w: jnp.einsum("ck,rcs->krs", w, turned, preferred_element_type=f32)
        both = (own_mask[None] * jax.nn.sigmoid(product(gates)) * product(sides)).astype(bf16)
        both = both.reshape(group, 2, size, sub_rows, columns)
        collected = [across_group(both[m], m) for m in range(group)]
        turned = after(turned, both)
        if last_sent is not None:
            collected = [after(c, last_sent) for c in collected]
        left = jnp.concatenate([b[0] for b in collected], axis=1)
        right = jnp.concatenate([b[1] for b in collected], axis=1)
        other_left = lax.ppermute(left, "gy", [(0, 1), (1, 0)])
        near = jnp.where(mine, left, other_left)
        far = jnp.where(mine, other_left, left)
        width = columns // split
        for at in range(split):
            piece = right[:, :, at * width : (at + 1) * width]
            partial = lambda l: jnp.einsum("hki,hkj->hij", l, piece, preferred_element_type=f32)
            sent = partial(far).astype(bf16)
            last_sent = sent
            arrived = across_halves(sent)
            kept = after(partial(near))
            pending.append((kept, arrived))

    def back(at, *earlier):
        kept, arrived = pending[at]
        triangle = (kept + after(arrived, last_sent, *earlier).astype(f32)).astype(bf16)
        tri_block = lambda m: lax.dynamic_slice_in_dim(triangle, (place ^ m) * sub_rows, sub_rows, 1)
        return [across_group(tri_block(m), m) for m in range(group)]

    gate = jax.nn.sigmoid(jnp.einsum("dc,rds->rcs", gate_weights, turned, preferred_element_type=f32))
    gate = own_mask[:, None, :] * gate
    step = columns // pieces
    first_back = back(0)
    update = None
    blocks = []
    for at in range(pieces):
        got = back(at + 1) if update is None else back(at + 1, update)
        got = [b[:, :, at * step : (at + 1) * step] for b in first_back] + got
        hidden_values = jnp.concatenate(got, axis=0).astype(f32)
        hidden_centred = hidden_values - jnp.mean(hidden_values, axis=0)
        hidden_spread = jnp.mean(hidden_centred * hidden_centred, axis=0)
        hidden_normed = (
            hidden_centred * lax.rsqrt(hidden_spread + EPSILON) * hidden_gains[:, None, None]
        ).astype(bf16)
        projected = jnp.einsum("hc,hrs->rcs", projection, hidden_normed, preferred_element_type=f32)
        update = (gate[:, :, at * step : (at + 1) * step] * projected).astype(bf16)
        blocks.append([across_gz(update[:, m * local_channels : (m + 1) * local_channels], m) for m in range(planes)])
    out = jnp.zeros((rows, local_channels, columns), bf16)
    for at in range(pieces):
        for m in range(planes):
            out = lax.dynamic_update_slice(out, blocks[at][m], ((g ^ m) * sub_rows, 0, at * step))
    return jnp.transpose(out, (1, 0, 2))


def solution(mesh):
    placed = (P("gz", "gx", "gy"), P("gx", "gy"), P(), P(), P(), P(), P())

    return jax.shard_map(shards, mesh=mesh, in_specs=placed, out_specs=P("gz", "gx", "gy"), check_vma=False)
```

profile of v0, /device:TPU:0, one launch (start us, length us, event | category | flops | bytes accessed | tf_op | source)
XLA Modules:
  0.0 262.5 jit_solution(16692377341869026411)
XLA Ops:
  0.0 2.7 %dynamic-slice_bitcast_fusion.3 = (bf16[32,32,256]{2,0,1:T(8,128)(2,1)S(1)}, bf16[32,32,256]{2,0,1:T(8,128)(2,1)}, bf16[32,32,256]{2,0,1:T(8,128)(2,1)S(1)}, bf16[32,32,256]{2,0,1:T(8,128)(2,1)S(1)}) fusion(bf16[32,128,256]{2,1,0:T(8,128)(2,1)} %param.7, s32[]{:T(128)S(6)} %select_n.99, s32[]{:T(128)S(6)} %select_n.100, s32[]{:T(128)S(6)} %select_n.102, ...), kind=kLoop, calls=%fused_computation.66 | loop fusion | bytes 4194320 | tf_op jit(solution)/shard_map/dynamic_slice | solution.py:63
  2.7 3.0 %collective-permute-start = (bf16[32,32,256]{2,0,1:T(8,128)(2,1)}, bf16[32,32,256]{2,0,1:T(8,128)(2,1)S(1)}, u32[]{:S(2)}, u32[]{:S(2)}) collective-permute-start(bf16[32,32,256]{2,0,1:T(8,128)(2,1)} %get-tuple-element.49), channel_id=1, source_target_pairs={{0,1},{1,0},{2,3},{3,2},{4,5},{5,4},{6,7},{7,6},{8,9},{9,8},{10,11... | collective-permute-start | bytes 1572872 | tf_op jit(solution)/shard_map/ppermute | solution.py:47
  5.7 1.5 collective-permute-start.1
  10.5 8.2 %collective-permute-done = bf16[32,32,256]{2,0,1:T(8,128)(2,1)S(1)} collective-permute-done((bf16[32,32,256]{2,0,1:T(8,128)(2,1)}, bf16[32,32,256]{2,0,1:T(8,128)(2,1)S(1)}, u32[]{:S(2)}, u32[]{:S(2)}) %collective-permute-start) | collective-permute-done | bytes 524320 | tf_op jit(solution)/shard_map/ppermute | solution.py:47
  18.7 10.7 %collective-permute-done.1 = bf16[32,32,256]{2,0,1:T(8,128)(2,1)S(1)} collective-permute-done((bf16[32,32,256]{2,0,1:T(8,128)(2,1)S(1)}, bf16[32,32,256]{2,0,1:T(8,128)(2,1)S(1)}, u32[]{:S(2)}, u32[]{:S(2)}) %collective-permute-start.1) | collective-permute-done | bytes 524320 | tf_op jit(solution)/shard_map/ppermute | solution.py:47
  31.3 4.5 %fusion.4 = bf16[32,128,256]{2,0,1:T(8,128)(2,1)S(1)} fusion(f32[128]{0:T(128)S(1)} %select_reduce_fusion.1, f32[32,256]{1,0:T(8,128)S(1)} %add_rsqrt_fusion, f32[32,256]{1,0:T(8,128)S(1)} %broadcast_multiply_fusion, bf16[32,32,256]{2,0,1:T(8,128)(2,1)S(1)} %collective-permute-done.2, bf16[32,32,256]{2,0,1:T(8,128)(2,1)S(1)} %collective-permute-done.1, ...), kind=kLoop, calls=%fused_computation.6 | loop fusion | flops 8388608 | bytes 4260352 | tf_op jit(solution)/shard_map/convert_element_type | solution.py:70
  35.7 1.6 fusion.22
  37.4 2.3 multiply_convert_fusion.1
  39.8 1.5 collective-permute-start.3
  42.0 1.6 fusion.19
  43.7 1.5 collective-permute-start.5
  45.2 1.6 collective-permute-start.6
  46.9 1.4 collective-permute-start.7
  48.4 2.0 collective-permute-start.8
  50.4 1.5 collective-permute-done.4
  51.9 1.4 collective-permute-start.9
  53.3 2.7 %collective-permute-done.5 = bf16[2,8,32,256]{3,1,2,0:T(8,128)(2,1)S(1)} collective-permute-done((bf16[2,8,32,256]{3,1,2,0:T(8,128)(2,1)S(1)}, bf16[2,8,32,256]{3,1,2,0:T(8,128)(2,1)S(1)}, u32[]{:S(2)}, u32[]{:S(2)}) %collective-permute-start.5) | collective-permute-done | bytes 262176 | tf_op jit(solution)/shard_map/ppermute | solution.py:57
  56.0 5.0 %collective-permute-done.7 = bf16[2,8,32,256]{3,1,2,0:T(8,128)(2,1)S(1)} collective-permute-done((bf16[2,8,32,256]{3,1,2,0:T(8,128)(2,1)S(1)}, bf16[2,8,32,256]{3,1,2,0:T(8,128)(2,1)S(1)}, u32[]{:S(2)}, u32[]{:S(2)}) %collective-permute-start.7) | collective-permute-done | bytes 262176 | tf_op jit(solution)/shard_map/ppermute | solution.py:57
  61.0 5.2 %collective-permute-done.8 = bf16[2,8,32,256]{3,1,2,0:T(8,128)(2,1)S(1)} collective-permute-done((bf16[2,8,32,256]{3,1,2,0:T(8,128)(2,1)S(1)}, bf16[2,8,32,256]{3,1,2,0:T(8,128)(2,1)S(1)}, u32[]{:S(2)}, u32[]{:S(2)}) %collective-permute-start.8) | collective-permute-done | bytes 262176 | tf_op jit(solution)/shard_map/ppermute | solution.py:57
  66.2 3.2 %collective-permute-done.9 = bf16[2,8,32,256]{3,1,2,0:T(8,128)(2,1)S(1)} collective-permute-done((bf16[2,8,32,256]{3,1,2,0:T(8,128)(2,1)S(1)}, bf16[2,8,32,256]{3,1,2,0:T(8,128)(2,1)S(1)}, u32[]{:S(2)}, u32[]{:S(2)}) %collective-permute-start.9) | collective-permute-done | bytes 262176 | tf_op jit(solution)/shard_map/ppermute | solution.py:57
  69.5 2.2 multiply_convert_fusion
  72.0 2.5 collective-permute-start.18
  75.1 2.5 collective-permute-start.16
  78.3 1.5 collective-permute-start.14
  80.0 4.1 %collective-permute-done.18 = bf16[2,8,32,256]{3,1,2,0:T(8,128)(2,1)S(1)} collective-permute-done((bf16[2,8,32,256]{3,1,2,0:T(8,128)(2,1)S(1)}, bf16[2,8,32,256]{3,1,2,0:T(8,128)(2,1)S(1)}, u32[]{:S(2)}, u32[]{:S(2)}) %collective-permute-start.18) | collective-permute-done | bytes 262176 | tf_op jit(solution)/shard_map/ppermute | solution.py:57
  84.0 1.4 collective-permute-start.13
  85.5 7.5 %collective-permute-done.17 = bf16[2,8,32,256]{3,1,2,0:T(8,128)(2,1)S(1)} collective-permute-done((bf16[2,8,32,256]{3,1,2,0:T(8,128)(2,1)S(1)}, bf16[2,8,32,256]{3,1,2,0:T(8,128)(2,1)S(1)}, u32[]{:S(2)}, u32[]{:S(2)}) %collective-permute-start.17) | collective-permute-done | bytes 262176 | tf_op jit(solution)/shard_map/ppermute | solution.py:57
  93.0 1.4 collective-permute-start.12
  94.4 1.7 convolution_convert_fusion
  96.1 2.4 collective-permute-done.16
  98.5 4.3 %collective-permute-done.15 = bf16[2,8,32,256]{3,1,2,0:T(8,128)(2,1)S(1)} collective-permute-done((bf16[2,8,32,256]{3,1,2,0:T(8,128)(2,1)S(1)}, bf16[2,8,32,256]{3,1,2,0:T(8,128)(2,1)S(1)}, u32[]{:S(2)}, u32[]{:S(2)}) %collective-permute-start.15) | collective-permute-done | bytes 262176 | tf_op jit(solution)/shard_map/ppermute | solution.py:57
  102.7 1.4 collective-permute-done.12
  104.6 4.4 %multiply_bitcast_fusion = f32[32,128,256]{2,1,0:T(8,128)} fusion(bf16[128,128,1]{0,1,2:T(8,128)(2,1)S(1)} %fusion.25, bf16[32,128,256]{2,0,1:T(8,128)(2,1)S(1)} %fusion.4, f32[32,256]{1,0:T(8,128)S(1)} %dynamic-slice_convert_fusion), kind=kOutput, calls=%fused_computation.7 | convolution fusion | flops 272629760 | bytes 6356992 | tf_op jit(solution)/shard_map/dc,rds->rcs/dot_general | solution.py:118
  109.0 2.6 collective-permute-start.11
  113.3 1.5 broadcast_select_fusion
  114.8 1.6 copy.85
  116.5 2.3 convolution_convert_fusion.2
  119.1 50.9 %collective-permute-done.11 = bf16[8,256,256]{2,1,0:T(8,128)(2,1)} collective-permute-done((bf16[8,256,256]{2,1,0:T(8,128)(2,1)}, bf16[8,256,256]{2,1,0:T(8,128)(2,1)}, u32[]{:S(2)}, u32[]{:S(2)}) %collective-permute-start.11) | collective-permute-done | bytes 1048608 | tf_op jit(solution)/shard_map/ppermute | solution.py:60
  170.0 1.5 add_convert_fusion
  173.0 2.8 %collective-permute-start.22 = (bf16[8,32,256]{2,1,0:T(8,128)(2,1)}, bf16[8,32,256]{2,1,0:T(8,128)(2,1)}, u32[]{:S(2)}, u32[]{:S(2)}) collective-permute-start(bf16[8,32,256]{2,1,0:T(8,128)(2,1)} %get-tuple-element.68), channel_id=1, source_target_pairs={{0,3},{1,2},{2,1},{3,0},{8,11},{9,10},{10,9},{11,8},{16,19},{17,18... | collective-permute-start | bytes 393224 | tf_op jit(solution)/shard_map/ppermute | solution.py:57
  178.6 1.4 collective-permute-start.24
  182.4 3.9 %collective-permute-start.26 = (bf16[8,32,256]{2,1,0:T(8,128)(2,1)S(1)}, bf16[8,32,256]{2,1,0:T(8,128)(2,1)S(1)}, u32[]{:S(2)}, u32[]{:S(2)}) collective-permute-start(bf16[8,32,256]{2,1,0:T(8,128)(2,1)S(1)} %get-tuple-element.64), channel_id=1, source_target_pairs={{0,11},{1,10},{2,9},{3,8},{8,3},{9,2},{10,1},{11,0},{16,27},{17,26... | collective-permute-start | bytes 393224 | tf_op jit(solution)/shard_map/ppermute | solution.py:57
  187.2 2.2 collective-permute-start.27
  190.3 1.4 collective-permute-done.25
  191.8 4.5 %collective-permute-done.26 = bf16[8,32,256]{2,1,0:T(8,128)(2,1)S(1)} collective-permute-done((bf16[8,32,256]{2,1,0:T(8,128)(2,1)S(1)}, bf16[8,32,256]{2,1,0:T(8,128)(2,1)S(1)}, u32[]{:S(2)}, u32[]{:S(2)}) %collective-permute-start.26) | collective-permute-done | bytes 131104 | tf_op jit(solution)/shard_map/ppermute | solution.py:57
  196.3 14.3 %collective-permute-done.27 = bf16[8,256,128]{2,1,0:T(8,128)(2,1)S(1)} collective-permute-done((bf16[8,256,128]{2,1,0:T(8,128)(2,1)S(1)}, bf16[8,256,128]{2,1,0:T(8,128)(2,1)S(1)}, u32[]{:S(2)}, u32[]{:S(2)}) %collective-permute-start.27) | collective-permute-done | bytes 524320 | tf_op jit(solution)/shard_map/ppermute | solution.py:60
  212.4 2.4 collective-permute-start.30
  215.6 1.3 collective-permute-start.32
  218.2 2.6 collective-permute-start.34
  222.1 2.2 collective-permute-done.34
  225.3 1.2 copy-done.6
  228.5 1.5 collective-permute-start.39
  232.8 2.1 collective-permute-start.43
  235.3 1.8 collective-permute-start.44
  237.1 1.3 collective-permute-start.45
  238.4 1.5 collective-permute-start.35
  240.0 1.2 collective-permute-start.36
  242.2 1.2 collective-permute-done.45
  246.5 1.6 collective-permute-done.35
  248.2 1.5 collective-permute-start.48
  250.5 4.2 %collective-permute-done.37 = bf16[32,32,128]{2,1,0:T(8,128)(2,1)S(1)} collective-permute-done((bf16[32,32,128]{2,1,0:T(8,128)(2,1)S(1)}, bf16[32,32,128]{2,1,0:T(8,128)(2,1)S(1)}, u32[]{:S(2)}, u32[]{:S(2)}) %collective-permute-start.37) | collective-permute-done | bytes 262176 | tf_op jit(solution)/shard_map/ppermute | solution.py:47
  255.0 2.8 %collective-permute-done.46 = bf16[32,32,128]{2,1,0:T(8,128)(2,1)S(1)} collective-permute-done((bf16[32,32,128]{2,1,0:T(8,128)(2,1)S(1)}, bf16[32,32,128]{2,1,0:T(8,128)(2,1)S(1)}, u32[]{:S(2)}, u32[]{:S(2)}) %collective-permute-start.46) | collective-permute-done | bytes 262176 | tf_op jit(solution)/shard_map/ppermute | solution.py:47
  258.2 2.7 %collective-permute-done.48 = bf16[32,32,128]{2,1,0:T(8,128)(2,1)S(1)} collective-permute-done((bf16[32,32,128]{2,1,0:T(8,128)(2,1)S(1)}, bf16[32,32,128]{2,1,0:T(8,128)(2,1)S(1)}, u32[]{:S(2)}, u32[]{:S(2)}) %collective-permute-start.48) | collective-permute-done | bytes 262176 | tf_op jit(solution)/shard_map/ppermute | solution.py:47
  261.2 1.3 copy-done.8
  (196 shorter events, 36.0 us)
Async XLA Ops:
  0.0 7.6 %copy-start = (bf16[4,128,128]{2,1,0:T(8,128)(2,1)S(1)}, bf16[4,128,128]{2,1,0:T(8,128)(2,1)}, u32[]{:S(2)}) copy-start(bf16[4,128,128]{2,1,0:T(8,128)(2,1)} %param.10) | copy-start | bytes 393220
  0.0 9.4 %copy-start.12 = (f32[128]{0:T(128)S(1)}, f32[128]{0:T(128)}, u32[]{:S(2)}) copy-start(f32[128]{0:T(128)} %param.9) | copy-start | bytes 1540
  0.0 9.6 %copy-start.13 = (f32[128]{0:T(128)S(1)}, f32[128]{0:T(128)}, u32[]{:S(2)}) copy-start(f32[128]{0:T(128)} %param.12) | copy-start | bytes 1540
  0.0 9.8 %copy-start.10 = (bf16[128,128]{1,0:T(8,128)(2,1)S(1)}, bf16[128,128]{1,0:T(8,128)(2,1)}, u32[]{:S(2)}) copy-start(bf16[128,128]{1,0:T(8,128)(2,1)} %param.11) | copy-start | bytes 98308
  0.0 10.1 %copy-start.11 = (bf16[128,128]{1,0:T(8,128)(2,1)S(1)}, bf16[128,128]{1,0:T(8,128)(2,1)}, u32[]{:S(2)}) copy-start(bf16[128,128]{1,0:T(8,128)(2,1)} %param.13) | copy-start | bytes 98308
  2.7 15.9 %collective-permute-start = (bf16[32,32,256]{2,0,1:T(8,128)(2,1)}, bf16[32,32,256]{2,0,1:T(8,128)(2,1)S(1)}, u32[]{:S(2)}, u32[]{:S(2)}) collective-permute-start(bf16[32,32,256]{2,0,1:T(8,128)(2,1)} %get-tuple-element.49), channel_id=1, source_target_pairs={{0,1},{1,0},{2,3},{3,2},{4,5},{5,4},{6,7},{7,6},{8,9},{9,8},{10,11... | collective-permute-start | bytes 1572872 | tf_op jit(solution)/shard_map/ppermute | solution.py:47
  5.7 23.7 %collective-permute-start.1 = (bf16[32,32,256]{2,0,1:T(8,128)(2,1)S(1)}, bf16[32,32,256]{2,0,1:T(8,128)(2,1)S(1)}, u32[]{:S(2)}, u32[]{:S(2)}) collective-permute-start(bf16[32,32,256]{2,0,1:T(8,128)(2,1)S(1)} %get-tuple-element.51), channel_id=1, source_target_pairs={{0,2},{1,3},{2,0},{3,1},{4,6},{5,7},{6,4},{7,5},{8,10},{9,11},{10,... | collective-permute-start | bytes 1572872 | tf_op jit(solution)/shard_map/ppermute | solution.py:47
  7.2 23.1 %collective-permute-start.2 = (bf16[32,32,256]{2,0,1:T(8,128)(2,1)S(1)}, bf16[32,32,256]{2,0,1:T(8,128)(2,1)S(1)}, u32[]{:S(2)}, u32[]{:S(2)}) collective-permute-start(bf16[32,32,256]{2,0,1:T(8,128)(2,1)S(1)} %get-tuple-element.50), channel_id=1, source_target_pairs={{0,3},{1,2},{2,1},{3,0},{4,7},{5,6},{6,5},{7,4},{8,11},{9,10},{10,... | collective-permute-start | bytes 1572872 | tf_op jit(solution)/shard_map/ppermute | solution.py:47
  39.8 8.6 %collective-permute-start.3 = (bf16[2,8,32,256]{3,1,2,0:T(8,128)(2,1)S(1)}, bf16[2,8,32,256]{3,1,2,0:T(8,128)(2,1)S(1)}, u32[]{:S(2)}, u32[]{:S(2)}) collective-permute-start(bf16[2,8,32,256]{3,1,2,0:T(8,128)(2,1)S(1)} %copy.47), channel_id=1, source_target_pairs={{0,1},{1,0},{2,3},{3,2},{8,9},{9,8},{10,11},{11,10},{16,17},{17,16... | collective-permute-start | bytes 786440 | tf_op jit(solution)/shard_map/ppermute | solution.py:57
  41.3 10.5 %collective-permute-start.4 = (bf16[2,8,32,256]{3,1,2,0:T(8,128)(2,1)S(1)}, bf16[2,8,32,256]{3,1,2,0:T(8,128)(2,1)S(1)}, u32[]{:S(2)}, u32[]{:S(2)}) collective-permute-start(bf16[2,8,32,256]{3,1,2,0:T(8,128)(2,1)S(1)} %copy.49), channel_id=1, source_target_pairs={{0,2},{1,3},{2,0},{3,1},{8,10},{9,11},{10,8},{11,9},{16,18},{17,19... | collective-permute-start | bytes 786440 | tf_op jit(solution)/shard_map/ppermute | solution.py:57
  43.7 12.2 %collective-permute-start.5 = (bf16[2,8,32,256]{3,1,2,0:T(8,128)(2,1)S(1)}, bf16[2,8,32,256]{3,1,2,0:T(8,128)(2,1)S(1)}, u32[]{:S(2)}, u32[]{:S(2)}) collective-permute-start(bf16[2,8,32,256]{3,1,2,0:T(8,128)(2,1)S(1)} %copy.51), channel_id=1, source_target_pairs={{0,3},{1,2},{2,1},{3,0},{8,11},{9,10},{10,9},{11,8},{16,19},{17,18... | collective-permute-start | bytes 786440 | tf_op jit(solution)/shard_map/ppermute | solution.py:57
  45.2 10.7 %collective-permute-start.6 = (bf16[2,8,32,256]{3,1,2,0:T(8,128)(2,1)S(1)}, bf16[2,8,32,256]{3,1,2,0:T(8,128)(2,1)S(1)}, u32[]{:S(2)}, u32[]{:S(2)}) collective-permute-start(bf16[2,8,32,256]{3,1,2,0:T(8,128)(2,1)S(1)} %copy.53), channel_id=1, source_target_pairs={{0,8},{1,9},{2,10},{3,11},{8,0},{9,1},{10,2},{11,3},{16,24},{17,25... | collective-permute-start | bytes 786440 | tf_op jit(solution)/shard_map/ppermute | solution.py:57
  46.9 14.1 %collective-permute-start.7 = (bf16[2,8,32,256]{3,1,2,0:T(8,128)(2,1)S(1)}, bf16[2,8,32,256]{3,1,2,0:T(8,128)(2,1)S(1)}, u32[]{:S(2)}, u32[]{:S(2)}) collective-permute-start(bf16[2,8,32,256]{3,1,2,0:T(8,128)(2,1)S(1)} %copy.55), channel_id=1, source_target_pairs={{0,9},{1,8},{2,11},{3,10},{8,1},{9,0},{10,3},{11,2},{16,25},{17,24... | collective-permute-start | bytes 786440 | tf_op jit(solution)/shard_map/ppermute | solution.py:57
  48.4 17.8 %collective-permute-start.8 = (bf16[2,8,32,256]{3,1,2,0:T(8,128)(2,1)S(1)}, bf16[2,8,32,256]{3,1,2,0:T(8,128)(2,1)S(1)}, u32[]{:S(2)}, u32[]{:S(2)}) collective-permute-start(bf16[2,8,32,256]{3,1,2,0:T(8,128)(2,1)S(1)} %copy.57), channel_id=1, source_target_pairs={{0,10},{1,11},{2,8},{3,9},{8,2},{9,3},{10,0},{11,1},{16,26},{17,27... | collective-permute-start | bytes 786440 | tf_op jit(solution)/shard_map/ppermute | solution.py:57
  51.9 17.6 %collective-permute-start.9 = (bf16[2,8,32,256]{3,1,2,0:T(8,128)(2,1)S(1)}, bf16[2,8,32,256]{3,1,2,0:T(8,128)(2,1)S(1)}, u32[]{:S(2)}, u32[]{:S(2)}) collective-permute-start(bf16[2,8,32,256]{3,1,2,0:T(8,128)(2,1)S(1)} %copy.59), channel_id=1, source_target_pairs={{0,11},{1,10},{2,9},{3,8},{8,3},{9,2},{10,1},{11,0},{16,27},{17,26... | collective-permute-start | bytes 786440 | tf_op jit(solution)/shard_map/ppermute | solution.py:57
  69.4 8.9 %collective-permute-start.10 = (bf16[8,256,256]{2,0,1:T(8,128)(2,1)S(1)}, bf16[8,256,256]{2,0,1:T(8,128)(2,1)S(1)}, u32[]{:S(2)}, u32[]{:S(2)}) collective-permute-start(bf16[8,256,256]{2,0,1:T(8,128)(2,1)S(1)} %get-tuple-element.104), channel_id=1, source_target_pairs={{0,4},{4,0},{1,5},{5,1},{2,6},{6,2},{3,7},{7,3},{8,12},{12,8},{9,1... | collective-permute-start | bytes 3145736 | tf_op jit(solution)/shard_map/ppermute | solution.py:99
  72.0 12.1 %collective-permute-start.18 = (bf16[2,8,32,256]{3,1,2,0:T(8,128)(2,1)S(1)}, bf16[2,8,32,256]{3,1,2,0:T(8,128)(2,1)S(1)}, u32[]{:S(2)}, u32[]{:S(2)}) collective-permute-start(bf16[2,8,32,256]{3,1,2,0:T(8,128)(2,1)S(1)} %copy.83), channel_id=1, source_target_pairs={{0,11},{1,10},{2,9},{3,8},{8,3},{9,2},{10,1},{11,0},{16,27},{17,26... | collective-permute-start | bytes 786440 | tf_op jit(solution)/shard_map/ppermute | solution.py:57
  74.5 18.5 %collective-permute-start.17 = (bf16[2,8,32,256]{3,1,2,0:T(8,128)(2,1)S(1)}, bf16[2,8,32,256]{3,1,2,0:T(8,128)(2,1)S(1)}, u32[]{:S(2)}, u32[]{:S(2)}) collective-permute-start(bf16[2,8,32,256]{3,1,2,0:T(8,128)(2,1)S(1)} %copy.81), channel_id=1, source_target_pairs={{0,10},{1,11},{2,8},{3,9},{8,2},{9,3},{10,0},{11,1},{16,26},{17,27... | collective-permute-start | bytes 786440 | tf_op jit(solution)/shard_map/ppermute | solution.py:57
  75.1 23.4 %collective-permute-start.16 = (bf16[2,8,32,256]{3,1,2,0:T(8,128)(2,1)S(1)}, bf16[2,8,32,256]{3,1,2,0:T(8,128)(2,1)S(1)}, u32[]{:S(2)}, u32[]{:S(2)}) collective-permute-start(bf16[2,8,32,256]{3,1,2,0:T(8,128)(2,1)S(1)} %copy.79), channel_id=1, source_target_pairs={{0,9},{1,8},{2,11},{3,10},{8,1},{9,0},{10,3},{11,2},{16,25},{17,24... | collective-permute-start | bytes 786440 | tf_op jit(solution)/shard_map/ppermute | solution.py:57
  77.6 25.1 %collective-permute-start.15 = (bf16[2,8,32,256]{3,1,2,0:T(8,128)(2,1)S(1)}, bf16[2,8,32,256]{3,1,2,0:T(8,128)(2,1)S(1)}, u32[]{:S(2)}, u32[]{:S(2)}) collective-permute-start(bf16[2,8,32,256]{3,1,2,0:T(8,128)(2,1)S(1)} %copy.77), channel_id=1, source_target_pairs={{0,8},{1,9},{2,10},{3,11},{8,0},{9,1},{10,2},{11,3},{16,24},{17,25... | collective-permute-start | bytes 786440 | tf_op jit(solution)/shard_map/ppermute | solution.py:57
  78.3 24.4 %collective-permute-start.14 = (bf16[2,8,32,256]{3,1,2,0:T(8,128)(2,1)S(1)}, bf16[2,8,32,256]{3,1,2,0:T(8,128)(2,1)S(1)}, u32[]{:S(2)}, u32[]{:S(2)}) collective-permute-start(bf16[2,8,32,256]{3,1,2,0:T(8,128)(2,1)S(1)} %copy.75), channel_id=1, source_target_pairs={{0,3},{1,2},{2,1},{3,0},{8,11},{9,10},{10,9},{11,8},{16,19},{17,18... | collective-permute-start | bytes 786440 | tf_op jit(solution)/shard_map/ppermute | solution.py:57
  84.0 18.7 %collective-permute-start.13 = (bf16[2,8,32,256]{3,1,2,0:T(8,128)(2,1)S(1)}, bf16[2,8,32,256]{3,1,2,0:T(8,128)(2,1)S(1)}, u32[]{:S(2)}, u32[]{:S(2)}) collective-permute-start(bf16[2,8,32,256]{3,1,2,0:T(8,128)(2,1)S(1)} %copy.73), channel_id=1, source_target_pairs={{0,2},{1,3},{2,0},{3,1},{8,10},{9,11},{10,8},{11,9},{16,18},{17,19... | collective-permute-start | bytes 786440 | tf_op jit(solution)/shard_map/ppermute | solution.py:57
  93.0 11.2 %collective-permute-start.12 = (bf16[2,8,32,256]{3,1,2,0:T(8,128)(2,1)S(1)}, bf16[2,8,32,256]{3,1,2,0:T(8,128)(2,1)S(1)}, u32[]{:S(2)}, u32[]{:S(2)}) collective-permute-start(bf16[2,8,32,256]{3,1,2,0:T(8,128)(2,1)S(1)} %copy.71), channel_id=1, source_target_pairs={{0,1},{1,0},{2,3},{3,2},{8,9},{9,8},{10,11},{11,10},{16,17},{17,16... | collective-permute-start | bytes 786440 | tf_op jit(solution)/shard_map/ppermute | solution.py:57
  104.6 8.8 %collective-permute-start.19 = (bf16[8,256,256]{2,0,1:T(8,128)(2,1)S(1)}, bf16[8,256,256]{2,0,1:T(8,128)(2,1)S(1)}, u32[]{:S(2)}, u32[]{:S(2)}) collective-permute-start(bf16[8,256,256]{2,0,1:T(8,128)(2,1)S(1)} %get-tuple-element.88), channel_id=1, source_target_pairs={{0,4},{4,0},{1,5},{5,1},{2,6},{6,2},{3,7},{7,3},{8,12},{12,8},{9,1... | collective-permute-start | bytes 3145736 | tf_op jit(solution)/shard_map/ppermute | solution.py:99
  109.0 61.0 %collective-permute-start.11 = (bf16[8,256,256]{2,1,0:T(8,128)(2,1)}, bf16[8,256,256]{2,1,0:T(8,128)(2,1)}, u32[]{:S(2)}, u32[]{:S(2)}) collective-permute-start(bf16[8,256,256]{2,1,0:T(8,128)(2,1)} %convolution_convert_fusion), channel_id=1, source_target_pairs={{0,16},{8,24},{16,0},{24,8},{1,17},{9,25},{17,1},{25,9},{2,18},{10... | collective-permute-start | bytes 3145736 | tf_op jit(solution)/shard_map/ppermute | solution.py:60
  118.7 57.3 %copy-start.3 = (bf16[8,256,128]{2,0,1:T(8,128)(2,1)S(1)}, bf16[8,256,128]{2,0,1:T(8,128)(2,1)}, u32[]{:S(2)}) copy-start(bf16[8,256,128]{2,0,1:T(8,128)(2,1)} %get-tuple-element.62) | copy-start | bytes 1572868
  118.7 108.5 %collective-permute-start.38 = (bf16[8,256,128]{2,1,0:T(8,128)(2,1)}, bf16[8,256,128]{2,1,0:T(8,128)(2,1)}, u32[]{:S(2)}, u32[]{:S(2)}) collective-permute-start(bf16[8,256,128]{2,1,0:T(8,128)(2,1)} %convolution_convert_fusion.2), channel_id=1, source_target_pairs={{0,16},{8,24},{16,0},{24,8},{1,17},{9,25},{17,1},{25,9},{2,18},{10... | collective-permute-start | bytes 1572872 | tf_op jit(solution)/shard_map/ppermute | solution.py:60
  171.4 5.0 %copy-start.7 = (bf16[8,256,256]{2,1,0:T(8,128)(2,1)}, bf16[8,256,256]{2,1,0:T(8,128)(2,1)S(1)}, u32[]{:S(2)}) copy-start(bf16[8,256,256]{2,1,0:T(8,128)(2,1)S(1)} %add_convert_fusion) | copy-start | bytes 3145732
  171.5 5.0 %copy-start.5 = (bf16[8,256,256]{2,0,1:T(8,128)(2,1)S(1)}, bf16[8,256,256]{2,0,1:T(8,128)(2,1)}, u32[]{:S(2)}) copy-start(bf16[8,256,256]{2,0,1:T(8,128)(2,1)} %get-tuple-element.27) | copy-start | bytes 3145732
  172.3 6.3 %collective-permute-start.20 = (bf16[8,32,256]{2,1,0:T(8,128)(2,1)}, bf16[8,32,256]{2,1,0:T(8,128)(2,1)}, u32[]{:S(2)}, u32[]{:S(2)}) collective-permute-start(bf16[8,32,256]{2,1,0:T(8,128)(2,1)} %get-tuple-element.70), channel_id=1, source_target_pairs={{0,1},{1,0},{2,3},{3,2},{8,9},{9,8},{10,11},{11,10},{16,17},{17,16... | collective-permute-start | bytes 393224 | tf_op jit(solution)/shard_map/ppermute | solution.py:57
  172.4 8.5 %collective-permute-start.21 = (bf16[8,32,256]{2,1,0:T(8,128)(2,1)}, bf16[8,32,256]{2,1,0:T(8,128)(2,1)}, u32[]{:S(2)}, u32[]{:S(2)}) collective-permute-start(bf16[8,32,256]{2,1,0:T(8,128)(2,1)} %get-tuple-element.69), channel_id=1, source_target_pairs={{0,2},{1,3},{2,0},{3,1},{8,10},{9,11},{10,8},{11,9},{16,18},{17,19... | collective-permute-start | bytes 393224 | tf_op jit(solution)/shard_map/ppermute | solution.py:57
  173.0 9.4 %collective-permute-start.22 = (bf16[8,32,256]{2,1,0:T(8,128)(2,1)}, bf16[8,32,256]{2,1,0:T(8,128)(2,1)}, u32[]{:S(2)}, u32[]{:S(2)}) collective-permute-start(bf16[8,32,256]{2,1,0:T(8,128)(2,1)} %get-tuple-element.68), channel_id=1, source_target_pairs={{0,3},{1,2},{2,1},{3,0},{8,11},{9,10},{10,9},{11,8},{16,19},{17,18... | collective-permute-start | bytes 393224 | tf_op jit(solution)/shard_map/ppermute | solution.py:57
  175.8 11.4 %collective-permute-start.23 = (bf16[8,32,256]{2,1,0:T(8,128)(2,1)}, bf16[8,32,256]{2,1,0:T(8,128)(2,1)}, u32[]{:S(2)}, u32[]{:S(2)}) collective-permute-start(bf16[8,32,256]{2,1,0:T(8,128)(2,1)} %get-tuple-element.67), channel_id=1, source_target_pairs={{0,8},{1,9},{2,10},{3,11},{8,0},{9,1},{10,2},{11,3},{16,24},{17,25... | collective-permute-start | bytes 393224 | tf_op jit(solution)/shard_map/ppermute | solution.py:57
  176.0 1.2 copy-start.4
  177.3 1.3 copy-start.9
  178.6 11.7 %collective-permute-start.24 = (bf16[8,32,256]{2,1,0:T(8,128)(2,1)S(1)}, bf16[8,32,256]{2,1,0:T(8,128)(2,1)S(1)}, u32[]{:S(2)}, u32[]{:S(2)}) collective-permute-start(bf16[8,32,256]{2,1,0:T(8,128)(2,1)S(1)} %copy-done.9), channel_id=1, source_target_pairs={{0,9},{1,8},{2,11},{3,10},{8,1},{9,0},{10,3},{11,2},{16,25},{17,24... | collective-permute-start | bytes 393224 | tf_op jit(solution)/shard_map/ppermute | solution.py:57
  180.9 10.8 %collective-permute-start.25 = (bf16[8,32,256]{2,1,0:T(8,128)(2,1)S(1)}, bf16[8,32,256]{2,1,0:T(8,128)(2,1)S(1)}, u32[]{:S(2)}, u32[]{:S(2)}) collective-permute-start(bf16[8,32,256]{2,1,0:T(8,128)(2,1)S(1)} %get-tuple-element.65), channel_id=1, source_target_pairs={{0,10},{1,11},{2,8},{3,9},{8,2},{9,3},{10,0},{11,1},{16,26},{17,27... | collective-permute-start | bytes 393224 | tf_op jit(solution)/shard_map/ppermute | solution.py:57
  182.4 13.9 %collective-permute-start.26 = (bf16[8,32,256]{2,1,0:T(8,128)(2,1)S(1)}, bf16[8,32,256]{2,1,0:T(8,128)(2,1)S(1)}, u32[]{:S(2)}, u32[]{:S(2)}) collective-permute-start(bf16[8,32,256]{2,1,0:T(8,128)(2,1)S(1)} %get-tuple-element.64), channel_id=1, source_target_pairs={{0,11},{1,10},{2,9},{3,8},{8,3},{9,2},{10,1},{11,0},{16,27},{17,26... | collective-permute-start | bytes 393224 | tf_op jit(solution)/shard_map/ppermute | solution.py:57
  187.2 23.4 %collective-permute-start.27 = (bf16[8,256,128]{2,1,0:T(8,128)(2,1)S(1)}, bf16[8,256,128]{2,1,0:T(8,128)(2,1)S(1)}, u32[]{:S(2)}, u32[]{:S(2)}) collective-permute-start(bf16[8,256,128]{2,1,0:T(8,128)(2,1)S(1)} %convolution_convert_fusion.1), channel_id=1, source_target_pairs={{0,16},{8,24},{16,0},{24,8},{1,17},{9,25},{17,1},{25,9},{2,18},{10... | collective-permute-start | bytes 1572872 | tf_op jit(solution)/shard_map/ppermute | solution.py:60
  189.3 22.1 %copy-start.2 = (bf16[8,256,128]{2,0,1:T(8,128)(2,1)S(1)}, bf16[8,256,128]{2,0,1:T(8,128)(2,1)}, u32[]{:S(2)}) copy-start(bf16[8,256,128]{2,0,1:T(8,128)(2,1)} %get-tuple-element.63) | copy-start | bytes 1572868
  210.7 4.8 %collective-permute-start.28 = (bf16[8,32,128]{2,1,0:T(8,128)(2,1)S(1)}, bf16[8,32,128]{2,1,0:T(8,128)(2,1)S(1)}, u32[]{:S(2)}, u32[]{:S(2)}) collective-permute-start(bf16[8,32,128]{2,1,0:T(8,128)(2,1)S(1)} %get-tuple-element.85), channel_id=1, source_target_pairs={{0,1},{1,0},{2,3},{3,2},{8,9},{9,8},{10,11},{11,10},{16,17},{17,16... | collective-permute-start | bytes 196616 | tf_op jit(solution)/shard_map/ppermute | solution.py:57
  211.8 5.0 %collective-permute-start.29 = (bf16[8,32,128]{2,1,0:T(8,128)(2,1)S(1)}, bf16[8,32,128]{2,1,0:T(8,128)(2,1)S(1)}, u32[]{:S(2)}, u32[]{:S(2)}) collective-permute-start(bf16[8,32,128]{2,1,0:T(8,128)(2,1)S(1)} %get-tuple-element.84), channel_id=1, source_target_pairs={{0,2},{1,3},{2,0},{3,1},{8,10},{9,11},{10,8},{11,9},{16,18},{17,19... | collective-permute-start | bytes 196616 | tf_op jit(solution)/shard_map/ppermute | solution.py:57
  212.4 5.8 %collective-permute-start.30 = (bf16[8,32,128]{2,1,0:T(8,128)(2,1)S(1)}, bf16[8,32,128]{2,1,0:T(8,128)(2,1)S(1)}, u32[]{:S(2)}, u32[]{:S(2)}) collective-permute-start(bf16[8,32,128]{2,1,0:T(8,128)(2,1)S(1)} %get-tuple-element.83), channel_id=1, source_target_pairs={{0,3},{1,2},{2,1},{3,0},{8,11},{9,10},{10,9},{11,8},{16,19},{17,18... | collective-permute-start | bytes 196616 | tf_op jit(solution)/shard_map/ppermute | solution.py:57
  214.8 6.0 %collective-permute-start.31 = (bf16[8,32,128]{2,1,0:T(8,128)(2,1)S(1)}, bf16[8,32,128]{2,1,0:T(8,128)(2,1)S(1)}, u32[]{:S(2)}, u32[]{:S(2)}) collective-permute-start(bf16[8,32,128]{2,1,0:T(8,128)(2,1)S(1)} %get-tuple-element.82), channel_id=1, source_target_pairs={{0,8},{1,9},{2,10},{3,11},{8,0},{9,1},{10,2},{11,3},{16,24},{17,25... | collective-permute-start | bytes 196616 | tf_op jit(solution)/shard_map/ppermute | solution.py:57
  215.6 5.3 %collective-permute-start.32 = (bf16[8,32,128]{2,1,0:T(8,128)(2,1)S(1)}, bf16[8,32,128]{2,1,0:T(8,128)(2,1)S(1)}, u32[]{:S(2)}, u32[]{:S(2)}) collective-permute-start(bf16[8,32,128]{2,1,0:T(8,128)(2,1)S(1)} %get-tuple-element.81), channel_id=1, source_target_pairs={{0,9},{1,8},{2,11},{3,10},{8,1},{9,0},{10,3},{11,2},{16,25},{17,24... | collective-permute-start | bytes 196616 | tf_op jit(solution)/shard_map/ppermute | solution.py:57
  216.9 5.2 %collective-permute-start.33 = (bf16[8,32,128]{2,1,0:T(8,128)(2,1)S(1)}, bf16[8,32,128]{2,1,0:T(8,128)(2,1)S(1)}, u32[]{:S(2)}, u32[]{:S(2)}) collective-permute-start(bf16[8,32,128]{2,1,0:T(8,128)(2,1)S(1)} %get-tuple-element.80), channel_id=1, source_target_pairs={{0,10},{1,11},{2,8},{3,9},{8,2},{9,3},{10,0},{11,1},{16,26},{17,27... | collective-permute-start | bytes 196616 | tf_op jit(solution)/shard_map/ppermute | solution.py:57
  218.2 6.1 %collective-permute-start.34 = (bf16[8,32,128]{2,1,0:T(8,128)(2,1)S(1)}, bf16[8,32,128]{2,1,0:T(8,128)(2,1)S(1)}, u32[]{:S(2)}, u32[]{:S(2)}) collective-permute-start(bf16[8,32,128]{2,1,0:T(8,128)(2,1)S(1)} %get-tuple-element.79), channel_id=1, source_target_pairs={{0,11},{1,10},{2,9},{3,8},{8,3},{9,2},{10,1},{11,0},{16,27},{17,26... | collective-permute-start | bytes 196616 | tf_op jit(solution)/shard_map/ppermute | solution.py:57
  224.3 2.2 copy-start.6
  228.5 6.8 %collective-permute-start.39 = (bf16[8,32,128]{2,1,0:T(8,128)(2,1)S(1)}, bf16[8,32,128]{2,1,0:T(8,128)(2,1)S(1)}, u32[]{:S(2)}, u32[]{:S(2)}) collective-permute-start(bf16[8,32,128]{2,1,0:T(8,128)(2,1)S(1)} %get-tuple-element.77), channel_id=1, source_target_pairs={{0,1},{1,0},{2,3},{3,2},{8,9},{9,8},{10,11},{11,10},{16,17},{17,16... | collective-permute-start | bytes 196616 | tf_op jit(solution)/shard_map/ppermute | solution.py:57
  230.0 7.2 %collective-permute-start.40 = (bf16[8,32,128]{2,1,0:T(8,128)(2,1)S(1)}, bf16[8,32,128]{2,1,0:T(8,128)(2,1)S(1)}, u32[]{:S(2)}, u32[]{:S(2)}) collective-permute-start(bf16[8,32,128]{2,1,0:T(8,128)(2,1)S(1)} %get-tuple-element.76), channel_id=1, source_target_pairs={{0,2},{1,3},{2,0},{3,1},{8,10},{9,11},{10,8},{11,9},{16,18},{17,19... | collective-permute-start | bytes 196616 | tf_op jit(solution)/shard_map/ppermute | solution.py:57
  231.1 7.4 %collective-permute-start.41 = (bf16[8,32,128]{2,1,0:T(8,128)(2,1)S(1)}, bf16[8,32,128]{2,1,0:T(8,128)(2,1)S(1)}, u32[]{:S(2)}, u32[]{:S(2)}) collective-permute-start(bf16[8,32,128]{2,1,0:T(8,128)(2,1)S(1)} %get-tuple-element.75), channel_id=1, source_target_pairs={{0,3},{1,2},{2,1},{3,0},{8,11},{9,10},{10,9},{11,8},{16,19},{17,18... | collective-permute-start | bytes 196616 | tf_op jit(solution)/shard_map/ppermute | solution.py:57
  232.0 8.0 %collective-permute-start.42 = (bf16[8,32,128]{2,1,0:T(8,128)(2,1)S(1)}, bf16[8,32,128]{2,1,0:T(8,128)(2,1)S(1)}, u32[]{:S(2)}, u32[]{:S(2)}) collective-permute-start(bf16[8,32,128]{2,1,0:T(8,128)(2,1)S(1)} %get-tuple-element.74), channel_id=1, source_target_pairs={{0,8},{1,9},{2,10},{3,11},{8,0},{9,1},{10,2},{11,3},{16,24},{17,25... | collective-permute-start | bytes 196616 | tf_op jit(solution)/shard_map/ppermute | solution.py:57
  232.8 8.4 %collective-permute-start.43 = (bf16[8,32,128]{2,1,0:T(8,128)(2,1)S(1)}, bf16[8,32,128]{2,1,0:T(8,128)(2,1)S(1)}, u32[]{:S(2)}, u32[]{:S(2)}) collective-permute-start(bf16[8,32,128]{2,1,0:T(8,128)(2,1)S(1)} %get-tuple-element.73), channel_id=1, source_target_pairs={{0,9},{1,8},{2,11},{3,10},{8,1},{9,0},{10,3},{11,2},{16,25},{17,24... | collective-permute-start | bytes 196616 | tf_op jit(solution)/shard_map/ppermute | solution.py:57
  235.3 6.9 %collective-permute-start.44 = (bf16[8,32,128]{2,1,0:T(8,128)(2,1)S(1)}, bf16[8,32,128]{2,1,0:T(8,128)(2,1)S(1)}, u32[]{:S(2)}, u32[]{:S(2)}) collective-permute-start(bf16[8,32,128]{2,1,0:T(8,128)(2,1)S(1)} %get-tuple-element.72), channel_id=1, source_target_pairs={{0,10},{1,11},{2,8},{3,9},{8,2},{9,3},{10,0},{11,1},{16,26},{17,27... | collective-permute-start | bytes 196616 | tf_op jit(solution)/shard_map/ppermute | solution.py:57
  237.1 6.3 %collective-permute-start.45 = (bf16[8,32,128]{2,1,0:T(8,128)(2,1)S(1)}, bf16[8,32,128]{2,1,0:T(8,128)(2,1)S(1)}, u32[]{:S(2)}, u32[]{:S(2)}) collective-permute-start(bf16[8,32,128]{2,1,0:T(8,128)(2,1)S(1)} %get-tuple-element.71), channel_id=1, source_target_pairs={{0,11},{1,10},{2,9},{3,8},{8,3},{9,2},{10,1},{11,0},{16,27},{17,26... | collective-permute-start | bytes 196616 | tf_op jit(solution)/shard_map/ppermute | solution.py:57
  238.4 9.7 %collective-permute-start.35 = (bf16[32,32,128]{2,1,0:T(8,128)(2,1)S(1)}, bf16[32,32,128]{2,1,0:T(8,128)(2,1)S(1)}, u32[]{:S(2)}, u32[]{:S(2)}) collective-permute-start(bf16[32,32,128]{2,1,0:T(8,128)(2,1)S(1)} %get-tuple-element.60), channel_id=1, source_target_pairs={{0,1},{1,0},{2,3},{3,2},{4,5},{5,4},{6,7},{7,6},{8,9},{9,8},{10,11... | collective-permute-start | bytes 786440 | tf_op jit(solution)/shard_map/ppermute | solution.py:47
  240.0 10.4 %collective-permute-start.36 = (bf16[32,32,128]{2,1,0:T(8,128)(2,1)S(1)}, bf16[32,32,128]{2,1,0:T(8,128)(2,1)S(1)}, u32[]{:S(2)}, u32[]{:S(2)}) collective-permute-start(bf16[32,32,128]{2,1,0:T(8,128)(2,1)S(1)} %get-tuple-element.59), channel_id=1, source_target_pairs={{0,2},{1,3},{2,0},{3,1},{4,6},{5,7},{6,4},{7,5},{8,10},{9,11},{10,... | collective-permute-start | bytes 786440 | tf_op jit(solution)/shard_map/ppermute | solution.py:47
  241.2 13.5 %collective-permute-start.37 = (bf16[32,32,128]{2,1,0:T(8,128)(2,1)S(1)}, bf16[32,32,128]{2,1,0:T(8,128)(2,1)S(1)}, u32[]{:S(2)}, u32[]{:S(2)}) collective-permute-start(bf16[32,32,128]{2,1,0:T(8,128)(2,1)S(1)} %get-tuple-element.58), channel_id=1, source_target_pairs={{0,3},{1,2},{2,1},{3,0},{4,7},{5,6},{6,5},{7,4},{8,11},{9,10},{10,... | collective-permute-start | bytes 786440 | tf_op jit(solution)/shard_map/ppermute | solution.py:47
  245.0 17.5 %copy-start.1 = (bf16[4,128,128]{2,1,0:T(8,128)(2,1)S(1)}, bf16[4,128,128]{2,1,0:T(8,128)(2,1)}, u32[]{:S(2)}) copy-start(bf16[4,128,128]{2,1,0:T(8,128)(2,1)} %param.10) | copy-start | bytes 393220
  245.1 12.7 %collective-permute-start.46 = (bf16[32,32,128]{2,1,0:T(8,128)(2,1)S(1)}, bf16[32,32,128]{2,1,0:T(8,128)(2,1)S(1)}, u32[]{:S(2)}, u32[]{:S(2)}) collective-permute-start(bf16[32,32,128]{2,1,0:T(8,128)(2,1)S(1)} %get-tuple-element.54), channel_id=1, source_target_pairs={{0,1},{1,0},{2,3},{3,2},{4,5},{5,4},{6,7},{7,6},{8,9},{9,8},{10,11... | collective-permute-start | bytes 786440 | tf_op jit(solution)/shard_map/ppermute | solution.py:47
  245.7 12.4 %collective-permute-start.47 = (bf16[32,32,128]{2,1,0:T(8,128)(2,1)S(1)}, bf16[32,32,128]{2,1,0:T(8,128)(2,1)S(1)}, u32[]{:S(2)}, u32[]{:S(2)}) collective-permute-start(bf16[32,32,128]{2,1,0:T(8,128)(2,1)S(1)} %get-tuple-element.53), channel_id=1, source_target_pairs={{0,2},{1,3},{2,0},{3,1},{4,6},{5,7},{6,4},{7,5},{8,10},{9,11},{10,... | collective-permute-start | bytes 786440 | tf_op jit(solution)/shard_map/ppermute | solution.py:47
  248.2 12.8 %collective-permute-start.48 = (bf16[32,32,128]{2,1,0:T(8,128)(2,1)S(1)}, bf16[32,32,128]{2,1,0:T(8,128)(2,1)S(1)}, u32[]{:S(2)}, u32[]{:S(2)}) collective-permute-start(bf16[32,32,128]{2,1,0:T(8,128)(2,1)S(1)} %get-tuple-element.52), channel_id=1, source_target_pairs={{0,3},{1,2},{2,1},{3,0},{4,7},{5,6},{6,5},{7,4},{8,11},{9,10},{10,... | collective-permute-start | bytes 786440 | tf_op jit(solution)/shard_map/ppermute | solution.py:47
  261.1 1.3 copy-start.8
where the time goes:
time: 263 us; the launch traced here: 262 us
  waiting for transfers between devices  145 us (55%)
  starting transfers between devices  65 us (25%)
  matrix products  20.5 us (8%)
  local copies, waits for them, and re-layouts  17.6 us (7%)
  other arithmetic  13.1 us (5%)
    ppermute x3, waiting for transfers between devices, across_halves(): lax.ppermute(block, 'gx', [(i, (i + half_depth) % depth) for i in range(d...  65.1 us
    ppermute x35, starting transfers between devices, across_group(): return lax.ppermute(block, ('gx', 'gz'), pairs)  48.6 us
    ppermute x35, waiting for transfers between devices, across_group(): return lax.ppermute(block, ('gx', 'gz'), pairs)  48.4 us
    ppermute x9, waiting for transfers between devices, across_gz(): lax.ppermute(block, 'gz', [(i, i ^ m) for i in range(planes)])  31.8 us
    ppermute x9, starting transfers between devices, across_gz(): lax.ppermute(block, 'gz', [(i, i ^ m) for i in range(planes)])  11.1 us
    dot_general x4, matrix products, shards(): jnp.einsum('ck,rcs->krs', w, turned, preferred_element_type=f32)  7.77 us
    unnamed x62, local copies, waits for them, and re-layouts  7.65 us
    dot_general x6, matrix products, shards(): jnp.einsum('hki,hkj->hij', l, piece, preferred_element_type=f32)  5.81 us
  transfers between devices with their start and end apart: 49, of which 27 were waited for; matrix products, arithmetic and copies ran while one was open for 13% of the time, Pallas kernels for 0%

commit v1 on v0

--- a/solution.py
+++ b/solution.py
@@ -38,10 +38,12 @@
     sub_rows = rows // planes
     sub_hidden = hidden // group
     z, core, g = lax.axis_index("gx"), lax.axis_index("gy"), lax.axis_index("gz")
-    half, inner = z // half_depth, z % half_depth
+    half = z // half_depth
+    inner = jnp.where(half == 0, z, depth - 1 - z)
     place = inner * planes + g
     chunks = [(0, sub_hidden // 2, 1), (sub_hidden // 2, sub_hidden // 2, 2)]
     pieces = 2
+    step = sub_rows // pieces
 
     def across_gz(block, m):
         return lax.ppermute(block, "gz", [(i, i ^ m) for i in range(planes)]) if m else block
@@ -50,14 +52,30 @@
         if not m:
             return block
         pairs = []
-        for a in range(depth):
+        for a in range(half_depth):
             for b in range(planes):
-                to = (a % half_depth * planes + b) ^ m
-                pairs.append((a * planes + b, (a // half_depth * half_depth + to // planes) * planes + to % planes))
+                to, at = divmod((a * planes + b) ^ m, planes)
+                pairs.append((a * planes + b, to * planes + at))
+                pairs.append(((depth - 1 - a) * planes + b, (depth - 1 - to) * planes + at))
         return lax.ppermute(block, ("gx", "gz"), pairs)
 
-    def across_halves(block):
-        return lax.ppermute(block, "gx", [(i, (i + half_depth) % depth) for i in range(depth)])
+    middle = (half_depth - 1, half_depth)
+
+    outer = [i for i in range(depth) if i not in middle]
+
+    def across_halves(block, whose):
+        return lax.ppermute(block, "gx", [(i, depth - 1 - i) for i in whose])
+
+    def to_plane(block, e, far):
+        pairs = []
+        for i in range(half_depth):
+            to = i ^ e
+            ends = ((i, depth - 1 - to), (depth - 1 - i, to)) if far else ((i, to), (depth - 1 - i, depth - 1 - to))
+            pairs += ends
+        return lax.ppermute(block, "gx", pairs)
+
+    def level(which, index):
+        return jnp.where(which == 0, index, half_depth - 1 - index)
 
     by_row = jnp.transpose(pair, (1, 0, 2))
     row_block = lambda m: lax.dynamic_slice_in_dim(by_row, (g ^ m) * sub_rows, sub_rows, 0)
@@ -75,10 +93,10 @@
     hidden_gains = take_vector(hidden_order, hidden_gain)
     projection = take_exact(hidden_order, take_exact(channel_order, out_weight, 1), 0)
     gate_weights = take_exact(channel_order, take_exact(channel_order, out_gate_weight, 0), 1)
-    turned = normed
+    turned = after(normed, projection)
     last_sent = None
     pending = []
-    for first, size, split in chunks:
+    for at_chunk, (first, size, split) in enumerate(chunks):
         order = block_order(place, group, sub_hidden, first, size)
         weights = take_exact(order, own_weights, 2)
         gates, sides = (
@@ -87,43 +105,69 @@
             ).reshape(channels, 2 * group * size)
             for a in (0, 1)
         )
-        product = lambda w: jnp.einsum("ck,rcs->krs", w, turned, preferred_element_type=f32)
-        both = (own_mask[None] * jax.nn.sigmoid(product(gates)) * product(sides)).astype(bf16)
-        both = both.reshape(group, 2, size, sub_rows, columns)
-        collected = [across_group(both[m], m) for m in range(group)]
+        product = lambda w: jnp.einsum("ck,rcs->rks", w, turned, preferred_element_type=f32)
+        both = (own_mask[:, None, :] * jax.nn.sigmoid(product(gates)) * product(sides)).astype(bf16)
+        block_of = lambda m: both[:, m * 2 * size : (m + 1) * 2 * size]
+        collected = [across_group(block_of(m), m) for m in range(group)]
         turned = after(turned, both)
         if last_sent is not None:
-            collected = [after(c, last_sent) for c in collected]
-        left = jnp.concatenate([b[0] for b in collected], axis=1)
-        right = jnp.concatenate([b[1] for b in collected], axis=1)
+            collected = [after(c, last_sent, gate_weights) for c in collected]
+        operands = jnp.concatenate(collected, axis=0)
+        left, right = operands[:, :size], operands[:, size:]
         other_left = lax.ppermute(left, "gy", [(0, 1), (1, 0)])
         near = jnp.where(mine, left, other_left)
         far = jnp.where(mine, other_left, left)
-        width = columns // split
+        partial = lambda l: jnp.einsum("khi,khj->hij", l, right, preferred_element_type=f32)
+        last_sent = partial(far).astype(bf16)
+        kept = after(partial(near))
+        if not at_chunk:
+            from_middle = across_halves(last_sent, middle)
+            from_outer = across_halves(last_sent, outer)
+            pending.append([(kept, jnp.where(inner == half_depth - 1, from_middle, from_outer))])
+            continue
         for at in range(split):
-            piece = right[:, :, at * width : (at + 1) * width]
-            partial = lambda l: jnp.einsum("hki,hkj->hij", l, piece, preferred_element_type=f32)
-            sent = partial(far).astype(bf16)
-            last_sent = sent
-            arrived = across_halves(sent)
-            kept = after(partial(near))
-            pending.append((kept, arrived))
+            height = sub_rows // split
+
+            def share_of(sums, which):
+                planewise = sums.reshape(size, half_depth, planes, sub_rows, columns)[:, :, :, at * height : (at + 1) * height]
+                return lax.dynamic_index_in_dim(planewise, which, 1, False)
+
+            sums = []
+            for e in range(half_depth):
+                arrived = to_plane(share_of(last_sent, level(1 - half, inner ^ e)), e, True)
+                own = share_of(kept, level(half, inner ^ e))
+                if e:
+                    own = to_plane(own.astype(bf16), e, False)
+                sums.append((own, arrived))
+            pending.append(sums)
 
     def back(at, *earlier):
-        kept, arrived = pending[at]
-        triangle = (kept + after(arrived, last_sent, *earlier).astype(f32)).astype(bf16)
-        tri_block = lambda m: lax.dynamic_slice_in_dim(triangle, (place ^ m) * sub_rows, sub_rows, 1)
-        return [across_group(tri_block(m), m) for m in range(group)]
+        triangle = jnp.stack(
+            [
+                (own.astype(f32) + after(arrived, last_sent, *earlier).astype(f32)).astype(bf16)
+                for own, arrived in pending[at]
+            ]
+        )
+        if at:
+            tri_block = lambda m: lax.dynamic_index_in_dim(triangle, g ^ m, 2, False)
+            got = [across_gz(tri_block(m), m) for m in range(planes)]
+            return [block[e] for e in range(half_depth) for block in got]
+        triangle = triangle.reshape(-1, half_depth, planes, sub_rows, columns)
+
+        def far_block(m):
+            to = place ^ m
+            flat = triangle.reshape(-1, group, sub_rows, columns)
+            return lax.dynamic_index_in_dim(flat, level(half, to // planes) * planes + to % planes, 1, False)
+
+        return [across_group(far_block(m), m) for m in range(group)]
 
     gate = jax.nn.sigmoid(jnp.einsum("dc,rds->rcs", gate_weights, turned, preferred_element_type=f32))
     gate = own_mask[:, None, :] * gate
-    step = columns // pieces
     first_back = back(0)
-    update = None
     blocks = []
     for at in range(pieces):
-        got = back(at + 1) if update is None else back(at + 1, update)
-        got = [b[:, :, at * step : (at + 1) * step] for b in first_back] + got
+        got = back(at + 1)
+        got = [b[:, at * step : (at + 1) * step] for b in first_back] + got
         hidden_values = jnp.concatenate(got, axis=0).astype(f32)
         hidden_centred = hidden_values - jnp.mean(hidden_values, axis=0)
         hidden_spread = jnp.mean(hidden_centred * hidden_centred, axis=0)
@@ -131,12 +175,12 @@
             hidden_centred * lax.rsqrt(hidden_spread + EPSILON) * hidden_gains[:, None, None]
         ).astype(bf16)
         projected = jnp.einsum("hc,hrs->rcs", projection, hidden_normed, preferred_element_type=f32)
-        update = (gate[:, :, at * step : (at + 1) * step] * projected).astype(bf16)
+        update = (gate[at * step : (at + 1) * step] * projected).astype(bf16)
         blocks.append([across_gz(update[:, m * local_channels : (m + 1) * local_channels], m) for m in range(planes)])
     out = jnp.zeros((rows, local_channels, columns), bf16)
     for at in range(pieces):
         for m in range(planes):
-            out = lax.dynamic_update_slice(out, blocks[at][m], ((g ^ m) * sub_rows, 0, at * step))
+            out = lax.dynamic_update_slice(out, blocks[at][m], ((g ^ m) * sub_rows + at * step, 0, 0))
     return jnp.transpose(out, (1, 0, 2))
 
 

time: 263 us -> 247 us (0.939)
  waiting for transfers between devices: 145 us -> 104 us
  starting transfers between devices: 65 us -> 101 us
  local copies, waits for them, and re-layouts: 17.6 us -> 12.4 us
  matrix products: 20.5 us -> 16.3 us
  other arithmetic: 13.1 us -> 10.1 us
    ppermute x3 -> x8, waiting for transfers between devices: 65.1 us -> 25.3 us  [the longest x2 14.5 us: across_halves(): return lax.ppermute(block, 'gx', [(i, depth - 1 - i) for i in whose])]
    ppermute x35 -> x21, starting transfers between devices: 48.6 us -> 64.8 us  [across_group(): return lax.ppermute(block, ('gx', 'gz'), pairs)]
    ppermute x3 -> x8, starting transfers between devices: 5.08 us -> 16.2 us  [the longest x6 9.94 us: to_plane(): return lax.ppermute(block, 'gx', pairs)]
    ppermute x9 -> x15, starting transfers between devices: 11.1 us -> 20.3 us  [across_gz(): lax.ppermute(block, 'gz', [(i, i ^ m) for i in range(planes)])]
    ppermute x35 -> x21, waiting for transfers between devices: 48.4 us -> 44.5 us  [across_group(): return lax.ppermute(block, ('gx', 'gz'), pairs)]
    unnamed x62 -> x65, local copies, waits for them, and re-layouts: 7.65 us -> 4.32 us
    convert_element_type x5 -> x1, other arithmetic: 3.54 us -> 0.36 us  [back(): (own.astype(f32) + after(arrived, last_sent, *earlier).astype(f32)).astyp...]
    ppermute x9 -> x15, waiting for transfers between devices: 31.8 us -> 34.1 us  [across_gz(): lax.ppermute(block, 'gz', [(i, i ^ m) for i in range(planes)])]
  transfers between devices with their start and end apart: 49 -> 46, of which waited for: 27 -> 25; matrix products, arithmetic and copies ran while one was open for 13% -> 8% of each run, Pallas kernels for 0% -> 0%
where the time goes in v1:
time: 247 us; the launch traced here: 245 us
  waiting for transfers between devices  104 us (42%)
  starting transfers between devices  101 us (41%)
  matrix products  16.3 us (7%)
  local copies, waits for them, and re-layouts  12.4 us (5%)
  other arithmetic  10.1 us (4%)
    ppermute x21, starting transfers between devices, across_group(): return lax.ppermute(block, ('gx', 'gz'), pairs)  64.8 us
    ppermute x21, waiting for transfers between devices, across_group(): return lax.ppermute(block, ('gx', 'gz'), pairs)  44.5 us
    ppermute x15, waiting for transfers between devices, across_gz(): lax.ppermute(block, 'gz', [(i, i ^ m) for i in range(planes)])  34.1 us
    ppermute x15, starting transfers between devices, across_gz(): lax.ppermute(block, 'gz', [(i, i ^ m) for i in range(planes)])  20.3 us
    ppermute x2, waiting for transfers between devices, across_halves(): return lax.ppermute(block, 'gx', [(i, depth - 1 - i) for i in whose])  14.5 us
    ppermute x6, waiting for transfers between devices, to_plane(): return lax.ppermute(block, 'gx', pairs)  10.8 us
    ppermute x6, starting transfers between devices, to_plane(): return lax.ppermute(block, 'gx', pairs)  9.94 us
    dot_general x4, matrix products, shards(): jnp.einsum('ck,rcs->rks', w, turned, preferred_element_type=f32)  7.86 us
  transfers between devices with their start and end apart: 46, of which 25 were waited for; matrix products, arithmetic and copies ran while one was open for 8% of the time, Pallas kernels for 0%

profile of v1, /device:TPU:0, one launch (start us, length us, event | category | flops | bytes accessed | tf_op | source)
XLA Modules:
  0.0 245.4 jit_solution(7358565056924713867)
XLA Ops:
  0.0 2.8 %dynamic-slice_bitcast_fusion.3 = (bf16[32,32,256]{2,0,1:T(8,128)(2,1)S(1)}, bf16[32,32,256]{2,0,1:T(8,128)(2,1)}, bf16[32,32,256]{2,0,1:T(8,128)(2,1)S(1)}, bf16[32,32,256]{2,0,1:T(8,128)(2,1)}) fusion(bf16[32,128,256]{2,1,0:T(8,128)(2,1)} %param.7, s32[]{:T(128)S(6)} %select_n.230, s32[]{:T(128)S(6)} %select_n.231, s32[]{:T(128)S(6)} %select_n.233, ...), kind=kLoop, calls=%fused_computation.100 | loop fusion | bytes 4194320 | tf_op jit(solution)/shard_map/dynamic_slice | solution.py:81
  2.8 3.0 %collective-permute-start = (bf16[32,32,256]{2,0,1:T(8,128)(2,1)}, bf16[32,32,256]{2,0,1:T(8,128)(2,1)S(1)}, u32[]{:S(2)}, u32[]{:S(2)}) collective-permute-start(bf16[32,32,256]{2,0,1:T(8,128)(2,1)} %get-tuple-element.60), channel_id=1, source_target_pairs={{0,1},{1,0},{2,3},{3,2},{4,5},{5,4},{6,7},{7,6},{8,9},{9,8},{10,11... | collective-permute-start | bytes 1572872 | tf_op jit(solution)/shard_map/ppermute | solution.py:49
  5.8 1.5 collective-permute-start.1
  10.3 8.5 %collective-permute-done = bf16[32,32,256]{2,0,1:T(8,128)(2,1)S(1)} collective-permute-done((bf16[32,32,256]{2,0,1:T(8,128)(2,1)}, bf16[32,32,256]{2,0,1:T(8,128)(2,1)S(1)}, u32[]{:S(2)}, u32[]{:S(2)}) %collective-permute-start) | collective-permute-done | bytes 524320 | tf_op jit(solution)/shard_map/ppermute | solution.py:49
  18.7 11.8 %collective-permute-done.1 = bf16[32,32,256]{2,0,1:T(8,128)(2,1)S(1)} collective-permute-done((bf16[32,32,256]{2,0,1:T(8,128)(2,1)}, bf16[32,32,256]{2,0,1:T(8,128)(2,1)S(1)}, u32[]{:S(2)}, u32[]{:S(2)}) %collective-permute-start.1) | collective-permute-done | bytes 524320 | tf_op jit(solution)/shard_map/ppermute | solution.py:49
  31.6 3.6 %fusion.4 = bf16[32,128,256]{2,0,1:T(8,128)(2,1)S(1)} fusion(f32[128]{0:T(128)S(1)} %select_reduce_fusion.1, f32[32,256]{1,0:T(8,128)S(1)} %add_rsqrt_fusion, f32[32,256]{1,0:T(8,128)S(1)} %broadcast_multiply_fusion, bf16[32,32,256]{2,0,1:T(8,128)(2,1)} %copy-done.5, bf16[32,32,256]{2,0,1:T(8,128)(2,1)} %copy-done.4, ...), kind=kLoop, calls=%fused_computation.6 | loop fusion | flops 8388608 | bytes 4260352 | tf_op jit(solution)/shard_map/convert_element_type | solution.py:88
  35.2 1.6 fusion.21
  36.9 2.3 fusion.24
  39.4 1.3 collective-permute-start.3
  41.5 1.4 collective-permute-start.5
  42.9 1.6 collective-permute-start.6
  44.5 1.1 collective-permute-start.7
  45.6 1.6 fusion.18
  47.3 2.9 %collective-permute-done.3 = bf16[32,16,256]{2,1,0:T(8,128)(2,1)S(1)} collective-permute-done((bf16[32,16,256]{2,1,0:T(8,128)(2,1)S(1)}, bf16[32,16,256]{2,1,0:T(8,128)(2,1)S(1)}, u32[]{:S(2)}, u32[]{:S(2)}) %collective-permute-start.3) | collective-permute-done | bytes 262176 | tf_op jit(solution)/shard_map/ppermute | solution.py:60
  50.1 2.9 %collective-permute-start.8 = (bf16[32,16,256]{2,1,0:T(8,128)(2,1)S(1)}, bf16[32,16,256]{2,1,0:T(8,128)(2,1)S(1)}, u32[]{:S(2)}, u32[]{:S(2)}) collective-permute-start(bf16[32,16,256]{2,1,0:T(8,128)(2,1)S(1)} %get-tuple-element.52), channel_id=1, source_target_pairs={{0,10},{24,18},{1,11},{25,19},{2,8},{26,16},{3,9},{27,17},{8,2},{1... | collective-permute-start | bytes 786440 | tf_op jit(solution)/shard_map/ppermute | solution.py:60
  53.1 1.6 collective-permute-start.9
  54.7 4.5 %collective-permute-done.5 = bf16[32,16,256]{2,1,0:T(8,128)(2,1)S(1)} collective-permute-done((bf16[32,16,256]{2,1,0:T(8,128)(2,1)S(1)}, bf16[32,16,256]{2,1,0:T(8,128)(2,1)S(1)}, u32[]{:S(2)}, u32[]{:S(2)}) %collective-permute-start.5) | collective-permute-done | bytes 262176 | tf_op jit(solution)/shard_map/ppermute | solution.py:60
  59.3 4.9 %collective-permute-done.8 = bf16[32,16,256]{2,1,0:T(8,128)(2,1)S(1)} collective-permute-done((bf16[32,16,256]{2,1,0:T(8,128)(2,1)S(1)}, bf16[32,16,256]{2,1,0:T(8,128)(2,1)S(1)}, u32[]{:S(2)}, u32[]{:S(2)}) %collective-permute-start.8) | collective-permute-done | bytes 262176 | tf_op jit(solution)/shard_map/ppermute | solution.py:60
  64.2 2.8 %collective-permute-done.9 = bf16[32,16,256]{2,1,0:T(8,128)(2,1)S(1)} collective-permute-done((bf16[32,16,256]{2,1,0:T(8,128)(2,1)S(1)}, bf16[32,16,256]{2,1,0:T(8,128)(2,1)S(1)}, u32[]{:S(2)}, u32[]{:S(2)}) %collective-permute-start.9) | collective-permute-done | bytes 262176 | tf_op jit(solution)/shard_map/ppermute | solution.py:60
  67.1 2.3 fusion.27
  69.7 2.5 %collective-permute-start.19 = (bf16[32,16,256]{2,1,0:T(8,128)(2,1)S(1)}, bf16[32,16,256]{2,1,0:T(8,128)(2,1)S(1)}, u32[]{:S(2)}, u32[]{:S(2)}) collective-permute-start(bf16[32,16,256]{2,1,0:T(8,128)(2,1)S(1)} %get-tuple-element.42), channel_id=1, source_target_pairs={{0,11},{24,19},{1,10},{25,18},{2,9},{26,17},{3,8},{27,16},{8,3},{1... | collective-permute-start | bytes 786440 | tf_op jit(solution)/shard_map/ppermute | solution.py:60
  72.2 1.2 collective-permute-start.18
  73.4 1.6 collective-permute-start.17
  75.6 1.5 collective-permute-start.15
  77.2 4.1 %collective-permute-done.19 = bf16[32,16,256]{2,1,0:T(8,128)(2,1)S(1)} collective-permute-done((bf16[32,16,256]{2,1,0:T(8,128)(2,1)S(1)}, bf16[32,16,256]{2,1,0:T(8,128)(2,1)S(1)}, u32[]{:S(2)}, u32[]{:S(2)}) %collective-permute-start.19) | collective-permute-done | bytes 262176 | tf_op jit(solution)/shard_map/ppermute | solution.py:60
  81.3 1.7 collective-permute-start.14
  83.0 8.3 %collective-permute-done.18 = bf16[32,16,256]{2,1,0:T(8,128)(2,1)S(1)} collective-permute-done((bf16[32,16,256]{2,1,0:T(8,128)(2,1)S(1)}, bf16[32,16,256]{2,1,0:T(8,128)(2,1)S(1)}, u32[]{:S(2)}, u32[]{:S(2)}) %collective-permute-start.18) | collective-permute-done | bytes 262176 | tf_op jit(solution)/shard_map/ppermute | solution.py:60
  92.1 1.6 convolution_convert_fusion.1
  93.7 2.3 collective-permute-done.17
  96.0 4.4 %collective-permute-done.16 = bf16[32,16,256]{2,1,0:T(8,128)(2,1)S(1)} collective-permute-done((bf16[32,16,256]{2,1,0:T(8,128)(2,1)S(1)}, bf16[32,16,256]{2,1,0:T(8,128)(2,1)S(1)}, u32[]{:S(2)}, u32[]{:S(2)}) %collective-permute-start.16) | collective-permute-done | bytes 262176 | tf_op jit(solution)/shard_map/ppermute | solution.py:60
  100.4 1.2 collective-permute-done.13
  101.8 1.3 copy-done.2
  104.8 2.3 multiply_bitcast_fusion
  107.9 5.5 %collective-permute-start.12 = (bf16[8,256,256]{2,1,0:T(8,128)(2,1)S(1)}, bf16[8,256,256]{2,1,0:T(8,128)(2,1)S(1)}, u32[]{:S(2)}, u32[]{:S(2)}) collective-permute-start(bf16[8,256,256]{2,1,0:T(8,128)(2,1)S(1)} %copy-done.9), channel_id=1, source_target_pairs={{0,24},{24,0},{1,25},{25,1},{2,26},{26,2},{3,27},{27,3},{4,28},{28... | collective-permute-start | bytes 3145736 | tf_op jit(solution)/shard_map/ppermute | solution.py:67
  115.0 1.5 broadcast_select_fusion.1
  119.6 3.7 %collective-permute-start.37 = (bf16[8,4,16,256]{3,0,2,1:T(8,128)(2,1)S(1)}, bf16[8,4,16,256]{3,0,2,1:T(8,128)(2,1)S(1)}, u32[]{:S(2)}, u32[]{:S(2)}) collective-permute-start(bf16[8,4,16,256]{3,0,2,1:T(8,128)(2,1)S(1)} %bitcast.227), channel_id=1, source_target_pairs={{0,24},{24,0},{8,16},{16,8},{1,25},{25,1},{9,17},{17,9},{2,26},{26... | collective-permute-start | bytes 786440 | tf_op jit(solution)/shard_map/ppermute | solution.py:75
  123.3 14.5 %collective-permute-done.12 = bf16[8,256,256]{2,1,0:T(8,128)(2,1)S(1)} collective-permute-done((bf16[8,256,256]{2,1,0:T(8,128)(2,1)S(1)}, bf16[8,256,256]{2,1,0:T(8,128)(2,1)S(1)}, u32[]{:S(2)}, u32[]{:S(2)}) %collective-permute-start.12) | collective-permute-done | bytes 1048608 | tf_op jit(solution)/shard_map/ppermute | solution.py:67
  139.1 1.7 collective-permute-start.22
  141.8 1.7 collective-permute-done.21
  143.6 1.5 collective-permute-start.23
  145.0 31.7 %collective-permute-start.24 = (bf16[8,32,256]{2,0,1:T(8,128)(2,1)S(1)}, bf16[8,32,256]{2,0,1:T(8,128)(2,1)S(1)}, u32[]{:S(2)}, u32[]{:S(2)}) collective-permute-start(bf16[8,32,256]{2,0,1:T(8,128)(2,1)S(1)} %bitcast.236), channel_id=1, source_target_pairs={{0,8},{24,16},{1,9},{25,17},{2,10},{26,18},{3,11},{27,19},{8,0},{1... | collective-permute-start | bytes 393224 | tf_op jit(solution)/shard_map/ppermute | solution.py:60
  176.7 5.1 %collective-permute-start.25 = (bf16[8,32,256]{2,0,1:T(8,128)(2,1)S(1)}, bf16[8,32,256]{2,0,1:T(8,128)(2,1)S(1)}, u32[]{:S(2)}, u32[]{:S(2)}) collective-permute-start(bf16[8,32,256]{2,0,1:T(8,128)(2,1)S(1)} %bitcast.235), channel_id=1, source_target_pairs={{0,9},{24,17},{1,8},{25,16},{2,11},{26,19},{3,10},{27,18},{8,1},{1... | collective-permute-start | bytes 393224 | tf_op jit(solution)/shard_map/ppermute | solution.py:60
  181.9 1.7 collective-permute-start.26
  183.7 1.9 collective-permute-done.25
  185.6 2.2 collective-permute-start.27
  187.7 1.5 collective-permute-done.26
  189.3 4.0 %collective-permute-done.27 = bf16[8,32,256]{2,0,1:T(8,128)(2,1)S(1)} collective-permute-done((bf16[8,32,256]{2,0,1:T(8,128)(2,1)S(1)}, bf16[8,32,256]{2,0,1:T(8,128)(2,1)S(1)}, u32[]{:S(2)}, u32[]{:S(2)}) %collective-permute-start.27) | collective-permute-done | bytes 131104 | tf_op jit(solution)/shard_map/ppermute | solution.py:60
  193.2 3.9 %collective-permute-start.30 = (bf16[8,4,16,256]{3,0,2,1:T(8,128)(2,1)S(1)}, bf16[8,4,16,256]{3,0,2,1:T(8,128)(2,1)S(1)}, u32[]{:S(2)}, u32[]{:S(2)}) collective-permute-start(bf16[8,4,16,256]{3,0,2,1:T(8,128)(2,1)S(1)} %bitcast.230), channel_id=1, source_target_pairs={{0,16},{24,8},{8,24},{16,0},{1,17},{25,9},{9,25},{17,1},{2,18},{26... | collective-permute-start | bytes 786440 | tf_op jit(solution)/shard_map/ppermute | solution.py:75
  197.2 1.4 collective-permute-start.28
  199.2 1.3 collective-permute-start.40
  200.4 1.1 collective-permute-start.41
  201.5 10.8 %collective-permute-done.30 = bf16[8,4,16,256]{3,0,2,1:T(8,128)(2,1)S(1)} collective-permute-done((bf16[8,4,16,256]{3,0,2,1:T(8,128)(2,1)S(1)}, bf16[8,4,16,256]{3,0,2,1:T(8,128)(2,1)S(1)}, u32[]{:S(2)}, u32[]{:S(2)}) %collective-permute-start.30) | collective-permute-done | bytes 262176 | tf_op jit(solution)/shard_map/ppermute | solution.py:75
  212.3 1.7 collective-permute-start.42
  216.4 1.8 collective-permute-start.33
  218.6 2.4 collective-permute-done.31
  222.3 1.8 collective-permute-done.33
  227.2 1.9 collective-permute-start.35
  230.8 1.9 collective-permute-start.44
  233.0 1.6 collective-permute-done.34
  234.7 1.5 collective-permute-start.45
  236.3 1.8 collective-permute-done.35
  238.6 1.7 collective-permute-done.43
  240.5 3.3 %collective-permute-done.44 = bf16[16,32,256]{2,1,0:T(8,128)(2,1)S(1)} collective-permute-done((bf16[16,32,256]{2,1,0:T(8,128)(2,1)S(1)}, bf16[16,32,256]{2,1,0:T(8,128)(2,1)S(1)}, u32[]{:S(2)}, u32[]{:S(2)}) %collective-permute-start.44) | collective-permute-done | bytes 262176 | tf_op jit(solution)/shard_map/ppermute | solution.py:49
  244.1 1.3 copy-done.8
  (195 shorter events, 26.5 us)
Async XLA Ops:
  0.0 7.6 %copy-start = (bf16[4,128,128]{2,1,0:T(8,128)(2,1)S(1)}, bf16[4,128,128]{2,1,0:T(8,128)(2,1)}, u32[]{:S(2)}) copy-start(bf16[4,128,128]{2,1,0:T(8,128)(2,1)} %param.10) | copy-start | bytes 393220
  0.0 9.4 %copy-start.12 = (f32[128]{0:T(128)S(1)}, f32[128]{0:T(128)}, u32[]{:S(2)}) copy-start(f32[128]{0:T(128)} %param.9) | copy-start | bytes 1540
  0.0 9.6 %copy-start.10 = (bf16[128,128]{1,0:T(8,128)(2,1)S(1)}, bf16[128,128]{1,0:T(8,128)(2,1)}, u32[]{:S(2)}) copy-start(bf16[128,128]{1,0:T(8,128)(2,1)} %param.13) | copy-start | bytes 98308
  0.0 9.9 %copy-start.11 = (bf16[128,128]{1,0:T(8,128)(2,1)S(1)}, bf16[128,128]{1,0:T(8,128)(2,1)}, u32[]{:S(2)}) copy-start(bf16[128,128]{1,0:T(8,128)(2,1)} %param.11) | copy-start | bytes 98308
  2.8 16.0 %collective-permute-start = (bf16[32,32,256]{2,0,1:T(8,128)(2,1)}, bf16[32,32,256]{2,0,1:T(8,128)(2,1)S(1)}, u32[]{:S(2)}, u32[]{:S(2)}) collective-permute-start(bf16[32,32,256]{2,0,1:T(8,128)(2,1)} %get-tuple-element.60), channel_id=1, source_target_pairs={{0,1},{1,0},{2,3},{3,2},{4,5},{5,4},{6,7},{7,6},{8,9},{9,8},{10,11... | collective-permute-start | bytes 1572872 | tf_op jit(solution)/shard_map/ppermute | solution.py:49
  5.8 24.8 %collective-permute-start.1 = (bf16[32,32,256]{2,0,1:T(8,128)(2,1)}, bf16[32,32,256]{2,0,1:T(8,128)(2,1)S(1)}, u32[]{:S(2)}, u32[]{:S(2)}) collective-permute-start(bf16[32,32,256]{2,0,1:T(8,128)(2,1)} %get-tuple-element.62), channel_id=1, source_target_pairs={{0,2},{1,3},{2,0},{3,1},{4,6},{5,7},{6,4},{7,5},{8,10},{9,11},{10,... | collective-permute-start | bytes 1572872 | tf_op jit(solution)/shard_map/ppermute | solution.py:49
  7.3 23.3 %collective-permute-start.2 = (bf16[32,32,256]{2,0,1:T(8,128)(2,1)S(1)}, bf16[32,32,256]{2,0,1:T(8,128)(2,1)S(1)}, u32[]{:S(2)}, u32[]{:S(2)}) collective-permute-start(bf16[32,32,256]{2,0,1:T(8,128)(2,1)S(1)} %get-tuple-element.61), channel_id=1, source_target_pairs={{0,3},{1,2},{2,1},{3,0},{4,7},{5,6},{6,5},{7,4},{8,11},{9,10},{10,... | collective-permute-start | bytes 1572872 | tf_op jit(solution)/shard_map/ppermute | solution.py:49
  30.6 1.0 copy-start.4
  30.6 1.0 copy-start.5
  39.4 10.7 %collective-permute-start.3 = (bf16[32,16,256]{2,1,0:T(8,128)(2,1)S(1)}, bf16[32,16,256]{2,1,0:T(8,128)(2,1)S(1)}, u32[]{:S(2)}, u32[]{:S(2)}) collective-permute-start(bf16[32,16,256]{2,1,0:T(8,128)(2,1)S(1)} %get-tuple-element.57), channel_id=1, source_target_pairs={{0,1},{24,25},{1,0},{25,24},{2,3},{26,27},{3,2},{27,26},{8,9},{16,... | collective-permute-start | bytes 786440 | tf_op jit(solution)/shard_map/ppermute | solution.py:60
  40.7 12.4 %collective-permute-start.4 = (bf16[32,16,256]{2,1,0:T(8,128)(2,1)S(1)}, bf16[32,16,256]{2,1,0:T(8,128)(2,1)S(1)}, u32[]{:S(2)}, u32[]{:S(2)}) collective-permute-start(bf16[32,16,256]{2,1,0:T(8,128)(2,1)S(1)} %get-tuple-element.56), channel_id=1, source_target_pairs={{0,2},{24,26},{1,3},{25,27},{2,0},{26,24},{3,1},{27,25},{8,10},{16... | collective-permute-start | bytes 786440 | tf_op jit(solution)/shard_map/ppermute | solution.py:60
  41.5 17.7 %collective-permute-start.5 = (bf16[32,16,256]{2,1,0:T(8,128)(2,1)S(1)}, bf16[32,16,256]{2,1,0:T(8,128)(2,1)S(1)}, u32[]{:S(2)}, u32[]{:S(2)}) collective-permute-start(bf16[32,16,256]{2,1,0:T(8,128)(2,1)S(1)} %get-tuple-element.55), channel_id=1, source_target_pairs={{0,3},{24,27},{1,2},{25,26},{2,1},{26,25},{3,0},{27,24},{8,11},{16... | collective-permute-start | bytes 786440 | tf_op jit(solution)/shard_map/ppermute | solution.py:60
  42.9 16.3 %collective-permute-start.6 = (bf16[32,16,256]{2,1,0:T(8,128)(2,1)S(1)}, bf16[32,16,256]{2,1,0:T(8,128)(2,1)S(1)}, u32[]{:S(2)}, u32[]{:S(2)}) collective-permute-start(bf16[32,16,256]{2,1,0:T(8,128)(2,1)S(1)} %get-tuple-element.54), channel_id=1, source_target_pairs={{0,8},{24,16},{1,9},{25,17},{2,10},{26,18},{3,11},{27,19},{8,0},{1... | collective-permute-start | bytes 786440 | tf_op jit(solution)/shard_map/ppermute | solution.py:60
  44.5 14.7 %collective-permute-start.7 = (bf16[32,16,256]{2,1,0:T(8,128)(2,1)S(1)}, bf16[32,16,256]{2,1,0:T(8,128)(2,1)S(1)}, u32[]{:S(2)}, u32[]{:S(2)}) collective-permute-start(bf16[32,16,256]{2,1,0:T(8,128)(2,1)S(1)} %get-tuple-element.53), channel_id=1, source_target_pairs={{0,9},{24,17},{1,8},{25,16},{2,11},{26,19},{3,10},{27,18},{8,1},{1... | collective-permute-start | bytes 786440 | tf_op jit(solution)/shard_map/ppermute | solution.py:60
  50.1 14.1 %collective-permute-start.8 = (bf16[32,16,256]{2,1,0:T(8,128)(2,1)S(1)}, bf16[32,16,256]{2,1,0:T(8,128)(2,1)S(1)}, u32[]{:S(2)}, u32[]{:S(2)}) collective-permute-start(bf16[32,16,256]{2,1,0:T(8,128)(2,1)S(1)} %get-tuple-element.52), channel_id=1, source_target_pairs={{0,10},{24,18},{1,11},{25,19},{2,8},{26,16},{3,9},{27,17},{8,2},{1... | collective-permute-start | bytes 786440 | tf_op jit(solution)/shard_map/ppermute | solution.py:60
  53.1 13.9 %collective-permute-start.9 = (bf16[32,16,256]{2,1,0:T(8,128)(2,1)S(1)}, bf16[32,16,256]{2,1,0:T(8,128)(2,1)S(1)}, u32[]{:S(2)}, u32[]{:S(2)}) collective-permute-start(bf16[32,16,256]{2,1,0:T(8,128)(2,1)S(1)} %get-tuple-element.51), channel_id=1, source_target_pairs={{0,11},{24,19},{1,10},{25,18},{2,9},{26,17},{3,8},{27,16},{8,3},{1... | collective-permute-start | bytes 786440 | tf_op jit(solution)/shard_map/ppermute | solution.py:60
  67.1 8.5 %collective-permute-start.10 = (bf16[256,8,256]{2,1,0:T(8,128)(2,1)S(1)}, bf16[256,8,256]{2,1,0:T(8,128)(2,1)S(1)}, u32[]{:S(2)}, u32[]{:S(2)}) collective-permute-start(bf16[256,8,256]{2,1,0:T(8,128)(2,1)S(1)} %slice.321), channel_id=1, source_target_pairs={{0,4},{4,0},{1,5},{5,1},{2,6},{6,2},{3,7},{7,3},{8,12},{12,8},{9,1... | collective-permute-start | bytes 3145736 | tf_op jit(solution)/shard_map/ppermute | solution.py:117
  69.7 11.7 %collective-permute-start.19 = (bf16[32,16,256]{2,1,0:T(8,128)(2,1)S(1)}, bf16[32,16,256]{2,1,0:T(8,128)(2,1)S(1)}, u32[]{:S(2)}, u32[]{:S(2)}) collective-permute-start(bf16[32,16,256]{2,1,0:T(8,128)(2,1)S(1)} %get-tuple-element.42), channel_id=1, source_target_pairs={{0,11},{24,19},{1,10},{25,18},{2,9},{26,17},{3,8},{27,16},{8,3},{1... | collective-permute-start | bytes 786440 | tf_op jit(solution)/shard_map/ppermute | solution.py:60
  72.2 19.2 %collective-permute-start.18 = (bf16[32,16,256]{2,1,0:T(8,128)(2,1)S(1)}, bf16[32,16,256]{2,1,0:T(8,128)(2,1)S(1)}, u32[]{:S(2)}, u32[]{:S(2)}) collective-permute-start(bf16[32,16,256]{2,1,0:T(8,128)(2,1)S(1)} %get-tuple-element.43), channel_id=1, source_target_pairs={{0,10},{24,18},{1,11},{25,19},{2,8},{26,16},{3,9},{27,17},{8,2},{1... | collective-permute-start | bytes 786440 | tf_op jit(solution)/shard_map/ppermute | solution.py:60
  73.4 22.6 %collective-permute-start.17 = (bf16[32,16,256]{2,1,0:T(8,128)(2,1)S(1)}, bf16[32,16,256]{2,1,0:T(8,128)(2,1)S(1)}, u32[]{:S(2)}, u32[]{:S(2)}) collective-permute-start(bf16[32,16,256]{2,1,0:T(8,128)(2,1)S(1)} %get-tuple-element.44), channel_id=1, source_target_pairs={{0,9},{24,17},{1,8},{25,16},{2,11},{26,19},{3,10},{27,18},{8,1},{1... | collective-permute-start | bytes 786440 | tf_op jit(solution)/shard_map/ppermute | solution.py:60
  75.0 25.4 %collective-permute-start.16 = (bf16[32,16,256]{2,1,0:T(8,128)(2,1)S(1)}, bf16[32,16,256]{2,1,0:T(8,128)(2,1)S(1)}, u32[]{:S(2)}, u32[]{:S(2)}) collective-permute-start(bf16[32,16,256]{2,1,0:T(8,128)(2,1)S(1)} %get-tuple-element.45), channel_id=1, source_target_pairs={{0,8},{24,16},{1,9},{25,17},{2,10},{26,18},{3,11},{27,19},{8,0},{1... | collective-permute-start | bytes 786440 | tf_op jit(solution)/shard_map/ppermute | solution.py:60
  75.6 24.8 %collective-permute-start.15 = (bf16[32,16,256]{2,1,0:T(8,128)(2,1)S(1)}, bf16[32,16,256]{2,1,0:T(8,128)(2,1)S(1)}, u32[]{:S(2)}, u32[]{:S(2)}) collective-permute-start(bf16[32,16,256]{2,1,0:T(8,128)(2,1)S(1)} %get-tuple-element.46), channel_id=1, source_target_pairs={{0,3},{24,27},{1,2},{25,26},{2,1},{26,25},{3,0},{27,24},{8,11},{16... | collective-permute-start | bytes 786440 | tf_op jit(solution)/shard_map/ppermute | solution.py:60
  77.2 24.4 %copy-start.6 = (bf16[256,8,256]{2,1,0:T(8,128)(2,1)}, bf16[256,8,256]{2,1,0:T(8,128)(2,1)S(1)}, u32[]{:S(2)}) copy-start(bf16[256,8,256]{2,1,0:T(8,128)(2,1)S(1)} %get-tuple-element.50) | copy-start | bytes 3145732
  81.3 19.1 %collective-permute-start.14 = (bf16[32,16,256]{2,1,0:T(8,128)(2,1)S(1)}, bf16[32,16,256]{2,1,0:T(8,128)(2,1)S(1)}, u32[]{:S(2)}, u32[]{:S(2)}) collective-permute-start(bf16[32,16,256]{2,1,0:T(8,128)(2,1)S(1)} %get-tuple-element.47), channel_id=1, source_target_pairs={{0,2},{24,26},{1,3},{25,27},{2,0},{26,24},{3,1},{27,25},{8,10},{16... | collective-permute-start | bytes 786440 | tf_op jit(solution)/shard_map/ppermute | solution.py:60
  91.3 10.3 %collective-permute-start.13 = (bf16[32,16,256]{2,1,0:T(8,128)(2,1)S(1)}, bf16[32,16,256]{2,1,0:T(8,128)(2,1)S(1)}, u32[]{:S(2)}, u32[]{:S(2)}) collective-permute-start(bf16[32,16,256]{2,1,0:T(8,128)(2,1)S(1)} %get-tuple-element.48), channel_id=1, source_target_pairs={{0,1},{24,25},{1,0},{25,24},{2,3},{26,27},{3,2},{27,26},{8,9},{16,... | collective-permute-start | bytes 786440 | tf_op jit(solution)/shard_map/ppermute | solution.py:60
  101.7 2.5 %copy-start.13 = (f32[128]{0:T(128)S(1)}, f32[128]{0:T(128)}, u32[]{:S(2)}) copy-start(f32[128]{0:T(128)} %param.12) | copy-start | bytes 1540
  101.8 1.3 copy-start.2
  104.2 9.8 %collective-permute-start.20 = (bf16[256,8,256]{2,1,0:T(8,128)(2,1)}, bf16[256,8,256]{2,1,0:T(8,128)(2,1)}, u32[]{:S(2)}, u32[]{:S(2)}) collective-permute-start(bf16[256,8,256]{2,1,0:T(8,128)(2,1)} %slice.331), channel_id=1, source_target_pairs={{0,4},{4,0},{1,5},{5,1},{2,6},{6,2},{3,7},{7,3},{8,12},{12,8},{9,1... | collective-permute-start | bytes 3145736 | tf_op jit(solution)/shard_map/ppermute | solution.py:117
  104.8 2.4 copy-start.9
  104.8 8.6 %copy-start.7 = (bf16[256,8,256]{2,1,0:T(8,128)(2,1)S(1)}, bf16[256,8,256]{2,1,0:T(8,128)(2,1)}, u32[]{:S(2)}) copy-start(bf16[256,8,256]{2,1,0:T(8,128)(2,1)} %copy-done.6) | copy-start | bytes 3145732
  107.1 16.1 %collective-permute-start.11 = (bf16[8,256,256]{2,1,0:T(8,128)(2,1)S(1)}, bf16[8,256,256]{2,1,0:T(8,128)(2,1)S(1)}, u32[]{:S(2)}, u32[]{:S(2)}) collective-permute-start(bf16[8,256,256]{2,1,0:T(8,128)(2,1)S(1)} %copy-done.9), channel_id=1, source_target_pairs={{8,16},{16,8},{9,17},{17,9},{10,18},{18,10},{11,19},{19,11},{12,20... | collective-permute-start | bytes 3145736 | tf_op jit(solution)/shard_map/ppermute | solution.py:67
  107.9 29.9 %collective-permute-start.12 = (bf16[8,256,256]{2,1,0:T(8,128)(2,1)S(1)}, bf16[8,256,256]{2,1,0:T(8,128)(2,1)S(1)}, u32[]{:S(2)}, u32[]{:S(2)}) collective-permute-start(bf16[8,256,256]{2,1,0:T(8,128)(2,1)S(1)} %copy-done.9), channel_id=1, source_target_pairs={{0,24},{24,0},{1,25},{25,1},{2,26},{26,2},{3,27},{27,3},{4,28},{28... | collective-permute-start | bytes 3145736 | tf_op jit(solution)/shard_map/ppermute | solution.py:67
  113.4 1.6 copy-start.3
  117.5 79.7 %collective-permute-start.39 = (bf16[8,4,16,256]{3,0,2,1:T(8,128)(2,1)S(1)}, bf16[8,4,16,256]{3,0,2,1:T(8,128)(2,1)S(1)}, u32[]{:S(2)}, u32[]{:S(2)}) collective-permute-start(bf16[8,4,16,256]{3,0,2,1:T(8,128)(2,1)S(1)} %bitcast.225), channel_id=1, source_target_pairs={{0,16},{24,8},{8,24},{16,0},{1,17},{25,9},{9,25},{17,1},{2,18},{26... | collective-permute-start | bytes 786440 | tf_op jit(solution)/shard_map/ppermute | solution.py:75
  118.6 80.4 %collective-permute-start.38 = (bf16[8,4,16,256]{3,0,2,1:T(8,128)(2,1)S(1)}, bf16[8,4,16,256]{3,0,2,1:T(8,128)(2,1)S(1)}, u32[]{:S(2)}, u32[]{:S(2)}) collective-permute-start(bf16[8,4,16,256]{3,0,2,1:T(8,128)(2,1)S(1)} %bitcast.226), channel_id=1, source_target_pairs={{0,8},{24,16},{8,0},{16,24},{1,9},{25,17},{9,1},{17,25},{2,10},{26... | collective-permute-start | bytes 786440 | tf_op jit(solution)/shard_map/ppermute | solution.py:75
  119.6 79.1 %collective-permute-start.37 = (bf16[8,4,16,256]{3,0,2,1:T(8,128)(2,1)S(1)}, bf16[8,4,16,256]{3,0,2,1:T(8,128)(2,1)S(1)}, u32[]{:S(2)}, u32[]{:S(2)}) collective-permute-start(bf16[8,4,16,256]{3,0,2,1:T(8,128)(2,1)S(1)} %bitcast.227), channel_id=1, source_target_pairs={{0,24},{24,0},{8,16},{16,8},{1,25},{25,1},{9,17},{17,9},{2,26},{26... | collective-permute-start | bytes 786440 | tf_op jit(solution)/shard_map/ppermute | solution.py:75
  138.5 5.0 %collective-permute-start.21 = (bf16[8,32,256]{2,0,1:T(8,128)(2,1)S(1)}, bf16[8,32,256]{2,0,1:T(8,128)(2,1)S(1)}, u32[]{:S(2)}, u32[]{:S(2)}) collective-permute-start(bf16[8,32,256]{2,0,1:T(8,128)(2,1)S(1)} %bitcast.239), channel_id=1, source_target_pairs={{0,1},{24,25},{1,0},{25,24},{2,3},{26,27},{3,2},{27,26},{8,9},{16,... | collective-permute-start | bytes 393224 | tf_op jit(solution)/shard_map/ppermute | solution.py:60
  139.1 6.0 %collective-permute-start.22 = (bf16[8,32,256]{2,0,1:T(8,128)(2,1)S(1)}, bf16[8,32,256]{2,0,1:T(8,128)(2,1)S(1)}, u32[]{:S(2)}, u32[]{:S(2)}) collective-permute-start(bf16[8,32,256]{2,0,1:T(8,128)(2,1)S(1)} %bitcast.237), channel_id=1, source_target_pairs={{0,2},{24,26},{1,3},{25,27},{2,0},{26,24},{3,1},{27,25},{8,10},{16... | collective-permute-start | bytes 393224 | tf_op jit(solution)/shard_map/ppermute | solution.py:60
  143.6 33.2 %collective-permute-start.23 = (bf16[8,32,256]{2,0,1:T(8,128)(2,1)S(1)}, bf16[8,32,256]{2,0,1:T(8,128)(2,1)S(1)}, u32[]{:S(2)}, u32[]{:S(2)}) collective-permute-start(bf16[8,32,256]{2,0,1:T(8,128)(2,1)S(1)} %bitcast.238), channel_id=1, source_target_pairs={{0,3},{24,27},{1,2},{25,26},{2,1},{26,25},{3,0},{27,24},{8,11},{16... | collective-permute-start | bytes 393224 | tf_op jit(solution)/shard_map/ppermute | solution.py:60
  145.0 36.8 %collective-permute-start.24 = (bf16[8,32,256]{2,0,1:T(8,128)(2,1)S(1)}, bf16[8,32,256]{2,0,1:T(8,128)(2,1)S(1)}, u32[]{:S(2)}, u32[]{:S(2)}) collective-permute-start(bf16[8,32,256]{2,0,1:T(8,128)(2,1)S(1)} %bitcast.236), channel_id=1, source_target_pairs={{0,8},{24,16},{1,9},{25,17},{2,10},{26,18},{3,11},{27,19},{8,0},{1... | collective-permute-start | bytes 393224 | tf_op jit(solution)/shard_map/ppermute | solution.py:60
  176.7 8.8 %collective-permute-start.25 = (bf16[8,32,256]{2,0,1:T(8,128)(2,1)S(1)}, bf16[8,32,256]{2,0,1:T(8,128)(2,1)S(1)}, u32[]{:S(2)}, u32[]{:S(2)}) collective-permute-start(bf16[8,32,256]{2,0,1:T(8,128)(2,1)S(1)} %bitcast.235), channel_id=1, source_target_pairs={{0,9},{24,17},{1,8},{25,16},{2,11},{26,19},{3,10},{27,18},{8,1},{1... | collective-permute-start | bytes 393224 | tf_op jit(solution)/shard_map/ppermute | solution.py:60
  181.9 7.3 %collective-permute-start.26 = (bf16[8,32,256]{2,0,1:T(8,128)(2,1)S(1)}, bf16[8,32,256]{2,0,1:T(8,128)(2,1)S(1)}, u32[]{:S(2)}, u32[]{:S(2)}) collective-permute-start(bf16[8,32,256]{2,0,1:T(8,128)(2,1)S(1)} %bitcast.234), channel_id=1, source_target_pairs={{0,10},{24,18},{1,11},{25,19},{2,8},{26,16},{3,9},{27,17},{8,2},{1... | collective-permute-start | bytes 393224 | tf_op jit(solution)/shard_map/ppermute | solution.py:60
  185.6 7.7 %collective-permute-start.27 = (bf16[8,32,256]{2,0,1:T(8,128)(2,1)S(1)}, bf16[8,32,256]{2,0,1:T(8,128)(2,1)S(1)}, u32[]{:S(2)}, u32[]{:S(2)}) collective-permute-start(bf16[8,32,256]{2,0,1:T(8,128)(2,1)S(1)} %bitcast.233), channel_id=1, source_target_pairs={{0,11},{24,19},{1,10},{25,18},{2,9},{26,17},{3,8},{27,16},{8,3},{1... | collective-permute-start | bytes 393224 | tf_op jit(solution)/shard_map/ppermute | solution.py:60
  189.2 25.2 %collective-permute-start.29 = (bf16[8,4,16,256]{3,0,2,1:T(8,128)(2,1)S(1)}, bf16[8,4,16,256]{3,0,2,1:T(8,128)(2,1)S(1)}, u32[]{:S(2)}, u32[]{:S(2)}) collective-permute-start(bf16[8,4,16,256]{3,0,2,1:T(8,128)(2,1)S(1)} %bitcast.228), channel_id=1, source_target_pairs={{0,8},{24,16},{8,0},{16,24},{1,9},{25,17},{9,1},{17,25},{2,10},{26... | collective-permute-start | bytes 786440 | tf_op jit(solution)/shard_map/ppermute | solution.py:75
  193.2 19.1 %collective-permute-start.30 = (bf16[8,4,16,256]{3,0,2,1:T(8,128)(2,1)S(1)}, bf16[8,4,16,256]{3,0,2,1:T(8,128)(2,1)S(1)}, u32[]{:S(2)}, u32[]{:S(2)}) collective-permute-start(bf16[8,4,16,256]{3,0,2,1:T(8,128)(2,1)S(1)} %bitcast.230), channel_id=1, source_target_pairs={{0,16},{24,8},{8,24},{16,0},{1,17},{25,9},{9,25},{17,1},{2,18},{26... | collective-permute-start | bytes 786440 | tf_op jit(solution)/shard_map/ppermute | solution.py:75
  197.2 16.8 %collective-permute-start.28 = (bf16[8,4,16,256]{3,0,2,1:T(8,128)(2,1)S(1)}, bf16[8,4,16,256]{3,0,2,1:T(8,128)(2,1)S(1)}, u32[]{:S(2)}, u32[]{:S(2)}) collective-permute-start(bf16[8,4,16,256]{3,0,2,1:T(8,128)(2,1)S(1)} %bitcast.229), channel_id=1, source_target_pairs={{0,24},{24,0},{8,16},{16,8},{1,25},{25,1},{9,17},{17,9},{2,26},{26... | collective-permute-start | bytes 786440 | tf_op jit(solution)/shard_map/ppermute | solution.py:75
  199.2 17.2 %collective-permute-start.40 = (bf16[2,8,16,256]{3,1,2,0:T(8,128)(2,1)S(1)}, bf16[2,8,16,256]{3,1,2,0:T(8,128)(2,1)S(1)}, u32[]{:S(2)}, u32[]{:S(2)}) collective-permute-start(bf16[2,8,16,256]{3,1,2,0:T(8,128)(2,1)S(1)} %get-tuple-element.83), channel_id=1, source_target_pairs={{0,1},{1,0},{2,3},{3,2},{4,5},{5,4},{6,7},{7,6},{8,9},{9,8},{10,11... | collective-permute-start | bytes 393224 | tf_op jit(solution)/shard_map/ppermute | solution.py:49
  200.4 17.8 %collective-permute-start.41 = (bf16[2,8,16,256]{3,1,2,0:T(8,128)(2,1)S(1)}, bf16[2,8,16,256]{3,1,2,0:T(8,128)(2,1)S(1)}, u32[]{:S(2)}, u32[]{:S(2)}) collective-permute-start(bf16[2,8,16,256]{3,1,2,0:T(8,128)(2,1)S(1)} %get-tuple-element.84), channel_id=1, source_target_pairs={{0,2},{1,3},{2,0},{3,1},{4,6},{5,7},{6,4},{7,5},{8,10},{9,11},{10,... | collective-permute-start | bytes 393224 | tf_op jit(solution)/shard_map/ppermute | solution.py:49
  212.3 6.1 %collective-permute-start.42 = (bf16[2,8,16,256]{3,1,2,0:T(8,128)(2,1)S(1)}, bf16[2,8,16,256]{3,1,2,0:T(8,128)(2,1)S(1)}, u32[]{:S(2)}, u32[]{:S(2)}) collective-permute-start(bf16[2,8,16,256]{3,1,2,0:T(8,128)(2,1)S(1)} %get-tuple-element.81), channel_id=1, source_target_pairs={{0,3},{1,2},{2,1},{3,0},{4,7},{5,6},{6,5},{7,4},{8,11},{9,10},{10,... | collective-permute-start | bytes 393224 | tf_op jit(solution)/shard_map/ppermute | solution.py:49
  214.6 6.4 %collective-permute-start.31 = (bf16[2,8,16,256]{3,1,2,0:T(8,128)(2,1)S(1)}, bf16[2,8,16,256]{3,1,2,0:T(8,128)(2,1)S(1)}, u32[]{:S(2)}, u32[]{:S(2)}) collective-permute-start(bf16[2,8,16,256]{3,1,2,0:T(8,128)(2,1)S(1)} %get-tuple-element.89), channel_id=1, source_target_pairs={{0,1},{1,0},{2,3},{3,2},{4,5},{5,4},{6,7},{7,6},{8,9},{9,8},{10,11... | collective-permute-start | bytes 393224 | tf_op jit(solution)/shard_map/ppermute | solution.py:49
  215.4 6.9 %collective-permute-start.32 = (bf16[2,8,16,256]{3,1,2,0:T(8,128)(2,1)S(1)}, bf16[2,8,16,256]{3,1,2,0:T(8,128)(2,1)S(1)}, u32[]{:S(2)}, u32[]{:S(2)}) collective-permute-start(bf16[2,8,16,256]{3,1,2,0:T(8,128)(2,1)S(1)} %get-tuple-element.90), channel_id=1, source_target_pairs={{0,2},{1,3},{2,0},{3,1},{4,6},{5,7},{6,4},{7,5},{8,10},{9,11},{10,... | collective-permute-start | bytes 393224 | tf_op jit(solution)/shard_map/ppermute | solution.py:49
  216.4 7.7 %collective-permute-start.33 = (bf16[2,8,16,256]{3,1,2,0:T(8,128)(2,1)S(1)}, bf16[2,8,16,256]{3,1,2,0:T(8,128)(2,1)S(1)}, u32[]{:S(2)}, u32[]{:S(2)}) collective-permute-start(bf16[2,8,16,256]{3,1,2,0:T(8,128)(2,1)S(1)} %get-tuple-element.87), channel_id=1, source_target_pairs={{0,3},{1,2},{2,1},{3,0},{4,7},{5,6},{6,5},{7,4},{8,11},{9,10},{10,... | collective-permute-start | bytes 393224 | tf_op jit(solution)/shard_map/ppermute | solution.py:49
  226.0 8.7 %collective-permute-start.34 = (bf16[16,32,256]{2,1,0:T(8,128)(2,1)S(1)}, bf16[16,32,256]{2,1,0:T(8,128)(2,1)S(1)}, u32[]{:S(2)}, u32[]{:S(2)}) collective-permute-start(bf16[16,32,256]{2,1,0:T(8,128)(2,1)S(1)} %get-tuple-element.71), channel_id=1, source_target_pairs={{0,1},{1,0},{2,3},{3,2},{4,5},{5,4},{6,7},{7,6},{8,9},{9,8},{10,11... | collective-permute-start | bytes 786440 | tf_op jit(solution)/shard_map/ppermute | solution.py:49
  227.2 10.9 %collective-permute-start.35 = (bf16[16,32,256]{2,1,0:T(8,128)(2,1)S(1)}, bf16[16,32,256]{2,1,0:T(8,128)(2,1)S(1)}, u32[]{:S(2)}, u32[]{:S(2)}) collective-permute-start(bf16[16,32,256]{2,1,0:T(8,128)(2,1)S(1)} %get-tuple-element.70), channel_id=1, source_target_pairs={{0,2},{1,3},{2,0},{3,1},{4,6},{5,7},{6,4},{7,5},{8,10},{9,11},{10,... | collective-permute-start | bytes 786440 | tf_op jit(solution)/shard_map/ppermute | solution.py:49
  229.1 9.2 %collective-permute-start.36 = (bf16[16,32,256]{2,1,0:T(8,128)(2,1)S(1)}, bf16[16,32,256]{2,1,0:T(8,128)(2,1)S(1)}, u32[]{:S(2)}, u32[]{:S(2)}) collective-permute-start(bf16[16,32,256]{2,1,0:T(8,128)(2,1)S(1)} %get-tuple-element.69), channel_id=1, source_target_pairs={{0,3},{1,2},{2,1},{3,0},{4,7},{5,6},{6,5},{7,4},{8,11},{9,10},{10,... | collective-permute-start | bytes 786440 | tf_op jit(solution)/shard_map/ppermute | solution.py:49
  229.7 10.6 %collective-permute-start.43 = (bf16[16,32,256]{2,1,0:T(8,128)(2,1)S(1)}, bf16[16,32,256]{2,1,0:T(8,128)(2,1)S(1)}, u32[]{:S(2)}, u32[]{:S(2)}) collective-permute-start(bf16[16,32,256]{2,1,0:T(8,128)(2,1)S(1)} %get-tuple-element.65), channel_id=1, source_target_pairs={{0,1},{1,0},{2,3},{3,2},{4,5},{5,4},{6,7},{7,6},{8,9},{9,8},{10,11... | collective-permute-start | bytes 786440 | tf_op jit(solution)/shard_map/ppermute | solution.py:49
  230.8 13.0 %collective-permute-start.44 = (bf16[16,32,256]{2,1,0:T(8,128)(2,1)S(1)}, bf16[16,32,256]{2,1,0:T(8,128)(2,1)S(1)}, u32[]{:S(2)}, u32[]{:S(2)}) collective-permute-start(bf16[16,32,256]{2,1,0:T(8,128)(2,1)S(1)} %get-tuple-element.64), channel_id=1, source_target_pairs={{0,2},{1,3},{2,0},{3,1},{4,6},{5,7},{6,4},{7,5},{8,10},{9,11},{10,... | collective-permute-start | bytes 786440 | tf_op jit(solution)/shard_map/ppermute | solution.py:49
  232.6 12.8 %copy-start.1 = (bf16[4,128,128]{2,1,0:T(8,128)(2,1)S(1)}, bf16[4,128,128]{2,1,0:T(8,128)(2,1)}, u32[]{:S(2)}) copy-start(bf16[4,128,128]{2,1,0:T(8,128)(2,1)} %param.10) | copy-start | bytes 393220
  234.7 9.2 %collective-permute-start.45 = (bf16[16,32,256]{2,1,0:T(8,128)(2,1)S(1)}, bf16[16,32,256]{2,1,0:T(8,128)(2,1)S(1)}, u32[]{:S(2)}, u32[]{:S(2)}) collective-permute-start(bf16[16,32,256]{2,1,0:T(8,128)(2,1)S(1)} %get-tuple-element.63), channel_id=1, source_target_pairs={{0,3},{1,2},{2,1},{3,0},{4,7},{5,6},{6,5},{7,4},{8,11},{9,10},{10,... | collective-permute-start | bytes 786440 | tf_op jit(solution)/shard_map/ppermute | solution.py:49
  244.1 1.3 copy-start.8

commit v2 on v1

--- a/solution.py
+++ b/solution.py
@@ -1,6 +1,7 @@
 import jax
 import jax.numpy as jnp
 from jax import lax
+from jax.experimental import pallas as pl
 from jax.sharding import PartitionSpec as P
 
 EPSILON = 1e-05
@@ -22,6 +23,45 @@
 def take_vector(order, vector):
     hot = order[:, None] == jnp.arange(vector.shape[0])[None, :]
     return jnp.sum(jnp.where(hot, vector[None, :], 0.0), axis=1)
+
+
+def norm_and_gate_kernel(count, *refs):
+    blocks, (mask, gains, gates, sides, normed, *parts) = refs[:count], refs[count:]
+    width = parts[0].shape[1]
+    for r in range(mask.shape[0]):
+        values = jnp.concatenate([block[r].astype(jnp.float32) for block in blocks], axis=0)
+        centred = values - jnp.mean(values, axis=0, keepdims=True)
+        spread = jnp.mean(centred * centred, axis=0, keepdims=True)
+        rounded = (centred * lax.rsqrt(spread + EPSILON) * gains[...]).astype(jnp.bfloat16)
+        normed[r] = rounded
+        left = jnp.dot(gates[...], rounded, preferred_element_type=jnp.float32)
+        right = jnp.dot(sides[...], rounded, preferred_element_type=jnp.float32)
+        both = (mask[r : r + 1, :] * jax.nn.sigmoid(left) * right).astype(jnp.bfloat16)
+        for at, part in enumerate(parts):
+            part[r] = both[at * width : (at + 1) * width]
+
+
+def norm_and_gate(blocks, mask, gains, gates, sides, count):
+    rows, width, columns = blocks[0].shape
+    channels, outputs = len(blocks) * width, gates.shape[0]
+    some = min(rows, 8)
+    tall = lambda n: pl.BlockSpec((some, n, columns), lambda i: (i, 0, 0))
+    whole = lambda a: pl.BlockSpec(a.shape, lambda i: (0, 0))
+    return pl.pallas_call(
+        lambda *refs: norm_and_gate_kernel(len(blocks), *refs),
+        grid=(rows // some,),
+        in_specs=[tall(width)] * len(blocks)
+        + [pl.BlockSpec((some, columns), lambda i: (i, 0)), whole(gains), whole(gates), whole(sides)],
+        out_specs=[tall(channels)] + [tall(outputs // count)] * count,
+        out_shape=[jax.ShapeDtypeStruct((rows, channels, columns), jnp.bfloat16)]
+        + [jax.ShapeDtypeStruct((rows, outputs // count, columns), jnp.bfloat16)] * count,
+        cost_estimate=pl.CostEstimate(
+            flops=4 * rows * columns * channels * outputs,
+            bytes_accessed=4 * rows * columns * (channels + outputs),
+            transcendentals=2 * rows * columns * outputs,
+        ),
+        name="norm_and_gate",
+    )(*blocks, mask, gains, gates, sides)
 
 
 def after(value, *others):
@@ -77,15 +117,15 @@
     def level(which, index):
         return jnp.where(which == 0, index, half_depth - 1 - index)
 
-    by_row = jnp.transpose(pair, (1, 0, 2))
-    row_block = lambda m: lax.dynamic_slice_in_dim(by_row, (g ^ m) * sub_rows, sub_rows, 0)
-    received = [across_gz(row_block(m), m) for m in range(planes)]
+    received = [None] * planes
+    block = None
+    for m in range(planes - 1, -1, -1):
+        start = (g ^ m) * sub_rows
+        start = start if block is None else after(start, block)
+        block = jnp.transpose(lax.dynamic_slice_in_dim(pair, start, sub_rows, 1), (1, 0, 2))
+        received[m] = across_gz(block, m)
     channel_order = block_order(g, planes, local_channels, 0, local_channels)
     gains = take_vector(channel_order, input_gain)
-    values = jnp.concatenate(received, axis=1).astype(f32)
-    centred = values - jnp.mean(values, axis=1, keepdims=True)
-    spread = jnp.mean(centred * centred, axis=1, keepdims=True)
-    normed = (centred * lax.rsqrt(spread + EPSILON) * gains[None, :, None]).astype(bf16)
     own_mask = lax.dynamic_slice_in_dim(pair_mask, g * sub_rows, sub_rows, 0).astype(f32)
     own_weights = take_exact(channel_order, input_weights, 1)
     mine = core == half
@@ -93,7 +133,7 @@
     hidden_gains = take_vector(hidden_order, hidden_gain)
     projection = take_exact(hidden_order, take_exact(channel_order, out_weight, 1), 0)
     gate_weights = take_exact(channel_order, take_exact(channel_order, out_gate_weight, 0), 1)
-    turned = after(normed, projection)
+    turned = None
     last_sent = None
     pending = []
     for at_chunk, (first, size, split) in enumerate(chunks):
@@ -105,11 +145,15 @@
             ).reshape(channels, 2 * group * size)
             for a in (0, 1)
         )
-        product = lambda w: jnp.einsum("ck,rcs->rks", w, turned, preferred_element_type=f32)
-        both = (own_mask[:, None, :] * jax.nn.sigmoid(product(gates)) * product(sides)).astype(bf16)
-        block_of = lambda m: both[:, m * 2 * size : (m + 1) * 2 * size]
-        collected = [across_group(block_of(m), m) for m in range(group)]
-        turned = after(turned, both)
+        if turned is None:
+            turned, *both = norm_and_gate(received, own_mask, gains[:, None], gates.T, sides.T, group)
+            turned = after(turned, projection)
+        else:
+            product = lambda w: jnp.einsum("ck,rcs->rks", w, turned, preferred_element_type=f32)
+            both = (own_mask[:, None, :] * jax.nn.sigmoid(product(gates)) * product(sides)).astype(bf16)
+            both = [both[:, m * 2 * size : (m + 1) * 2 * size] for m in range(group)]
+        collected = [across_group(both[m], m) for m in range(group)]
+        turned = after(turned, *both)
         if last_sent is not None:
             collected = [after(c, last_sent, gate_weights) for c in collected]
         operands = jnp.concatenate(collected, axis=0)

time: 247 us -> 241 us (0.976)
  matrix products: 16.3 us -> 10.3 us
  Pallas kernels: 0 us -> 5.41 us
  other arithmetic: 10.1 us -> 5.96 us
  waiting for transfers between devices: 104 us -> 101 us
    pallas_call x0 -> x1, Pallas kernels: none -> 5.41 us  [norm_and_gate(): pl.pallas_call(lambda *refs: norm_and_gate_kernel(len(blocks), *refs), gr...]
    ppermute x15, waiting for transfers between devices: 34.1 us -> 28.8 us  [across_gz(): lax.ppermute(block, 'gz', [(i, i ^ m) for i in range(planes)])]
    dot_general x4 -> x2, matrix products: 7.86 us -> 3.81 us  [shards(): jnp.einsum('ck,rcs->rks', w, turned, preferred_element_type=f32)]
    convert_element_type x1 -> x0, other arithmetic: 3.64 us -> none  [shards(): (centred * lax.rsqrt(spread + EPSILON) * gains[None, :, None]).astype(bf16)]
    ppermute x21, waiting for transfers between devices: 44.5 us -> 48.1 us  [across_group(): return lax.ppermute(block, ('gx', 'gz'), pairs)]
    ppermute x6, waiting for transfers between devices: 10.8 us -> 7.94 us  [to_plane(): return lax.ppermute(block, 'gx', pairs)]
    unnamed x65 -> x72, local copies, waits for them, and re-layouts: 4.32 us -> 6.84 us
  transfers between devices with their start and end apart: 46 -> 46, of which waited for: 25 -> 26; matrix products, arithmetic and copies ran while one was open for 8% -> 10% of each run, Pallas kernels for 0% -> 0%
where the time goes in v2:
time: 241 us; the launch traced here: 240 us
  starting transfers between devices  103 us (43%)
  waiting for transfers between devices  101 us (42%)
  local copies, waits for them, and re-layouts  12.6 us (5%)
  matrix products  10.3 us (4%)
  other arithmetic  5.96 us (2%)
  Pallas kernels  5.41 us (2%)
    ppermute x21, starting transfers between devices, across_group(): return lax.ppermute(block, ('gx', 'gz'), pairs)  66.8 us
    ppermute x21, waiting for transfers between devices, across_group(): return lax.ppermute(block, ('gx', 'gz'), pairs)  48.1 us
    ppermute x15, waiting for transfers between devices, across_gz(): lax.ppermute(block, 'gz', [(i, i ^ m) for i in range(planes)])  28.8 us
    ppermute x15, starting transfers between devices, across_gz(): lax.ppermute(block, 'gz', [(i, i ^ m) for i in range(planes)])  21 us
    ppermute x2, waiting for transfers between devices, across_halves(): return lax.ppermute(block, 'gx', [(i, depth - 1 - i) for i in whose])  16.5 us
    ppermute x6, starting transfers between devices, to_plane(): return lax.ppermute(block, 'gx', pairs)  9.05 us
    ppermute x6, waiting for transfers between devices, to_plane(): return lax.ppermute(block, 'gx', pairs)  7.94 us
    unnamed x72, local copies, waits for them, and re-layouts  6.84 us
  transfers between devices with their start and end apart: 46, of which 26 were waited for; matrix products, arithmetic and copies ran while one was open for 10% of the time, Pallas kernels for 0%

profile of v2, /device:TPU:0, one launch (start us, length us, event | category | flops | bytes accessed | tf_op | source)
XLA Modules:
  0.0 240.4 jit_solution(10328585707648807834)
XLA Ops:
  0.0 1.6 copy-done
  1.9 4.0 %collective-permute-start.2 = (bf16[32,32,256]{2,1,0:T(8,128)(2,1)S(1)}, bf16[32,32,256]{2,1,0:T(8,128)(2,1)}, u32[]{:S(2)}, u32[]{:S(2)}) collective-permute-start(bf16[32,32,256]{2,1,0:T(8,128)(2,1)S(1)} %bitcast.236), channel_id=1, source_target_pairs={{0,3},{1,2},{2,1},{3,0},{4,7},{5,6},{6,5},{7,4},{8,11},{9,10},{10,... | collective-permute-start | bytes 1572872 | tf_op jit(solution)/shard_map/ppermute | solution.py:89
  7.3 1.1 copy.125
  9.1 1.1 copy.124
  13.6 1.4 dynamic-slice_convert_fusion.refs_4_
  15.6 13.8 %collective-permute-done.refs_1_ = bf16[32,32,256]{2,1,0:T(8,128)(2,1)} collective-permute-done((bf16[32,32,256]{2,1,0:T(8,128)(2,1)}, bf16[32,32,256]{2,1,0:T(8,128)(2,1)}, u32[]{:S(2)}, u32[]{:S(2)}) %collective-permute-start) | collective-permute-done | bytes 524320 | tf_op jit(solution)/shard_map/ppermute | solution.py:89
  29.5 5.4 %norm_and_gate.1 = (bf16[32,128,256]{2,1,0:T(8,128)(2,1)}, bf16[32,16,256]{2,1,0:T(8,128)(2,1)}, bf16[32,16,256]{2,1,0:T(8,128)(2,1)}, bf16[32,16,256]{2,1,0:T(8...) custom-call(bf16[32,32,256]{2,1,0:T(8,128)(2,1)} %bitcast.238, ...), custom_call_target="tpu_custom_call" | custom-call | flops 536870912 | bytes 8388608 | tf_op jit(solution)/shard_map/norm_and_gate/pallas_call | solution.py:50
  34.9 1.6 collective-permute-start.3
  36.5 1.2 collective-permute-start.4
  38.5 2.4 fusion.78
  40.9 1.6 collective-permute-start.6
  42.6 1.4 collective-permute-start.7
  44.4 2.4 %collective-permute-start.8 = (bf16[32,16,256]{2,1,0:T(8,128)(2,1)S(1)}, bf16[32,16,256]{2,1,0:T(8,128)(2,1)S(1)}, u32[]{:S(2)}, u32[]{:S(2)}) collective-permute-start(bf16[32,16,256]{2,1,0:T(8,128)(2,1)S(1)} %copy-done.8), channel_id=1, source_target_pairs={{0,10},{24,18},{1,11},{25,19},{2,8},{26,16},{3,9},{27,17},{8,2},{1... | collective-permute-start | bytes 786440 | tf_op jit(solution)/shard_map/ppermute | solution.py:100
  46.8 1.6 collective-permute-done.4
  48.4 1.9 collective-permute-start.9
  50.3 2.1 collective-permute-done.5
  52.4 4.3 %collective-permute-done.7 = bf16[32,16,256]{2,1,0:T(8,128)(2,1)S(1)} collective-permute-done((bf16[32,16,256]{2,1,0:T(8,128)(2,1)S(1)}, bf16[32,16,256]{2,1,0:T(8,128)(2,1)S(1)}, u32[]{:S(2)}, u32[]{:S(2)}) %collective-permute-start.7) | collective-permute-done | bytes 262176 | tf_op jit(solution)/shard_map/ppermute | solution.py:100
  56.7 5.6 %collective-permute-done.8 = bf16[32,16,256]{2,1,0:T(8,128)(2,1)S(1)} collective-permute-done((bf16[32,16,256]{2,1,0:T(8,128)(2,1)S(1)}, bf16[32,16,256]{2,1,0:T(8,128)(2,1)S(1)}, u32[]{:S(2)}, u32[]{:S(2)}) %collective-permute-start.8) | collective-permute-done | bytes 262176 | tf_op jit(solution)/shard_map/ppermute | solution.py:100
  62.3 4.4 %collective-permute-done.9 = bf16[32,16,256]{2,1,0:T(8,128)(2,1)S(1)} collective-permute-done((bf16[32,16,256]{2,1,0:T(8,128)(2,1)S(1)}, bf16[32,16,256]{2,1,0:T(8,128)(2,1)S(1)}, u32[]{:S(2)}, u32[]{:S(2)}) %collective-permute-start.9) | collective-permute-done | bytes 262176 | tf_op jit(solution)/shard_map/ppermute | solution.py:100
  66.9 1.4 fusion.12
  68.6 1.9 collective-permute-start.19
  70.4 1.4 collective-permute-start.18
  71.8 2.3 collective-permute-start.17
  75.5 5.1 %collective-permute-done.19 = bf16[32,16,256]{2,1,0:T(8,128)(2,1)S(1)} collective-permute-done((bf16[32,16,256]{2,1,0:T(8,128)(2,1)S(1)}, bf16[32,16,256]{2,1,0:T(8,128)(2,1)S(1)}, u32[]{:S(2)}, u32[]{:S(2)}) %collective-permute-start.19) | collective-permute-done | bytes 262176 | tf_op jit(solution)/shard_map/ppermute | solution.py:100
  80.5 0.9 collective-permute-start.14
  81.4 8.4 %collective-permute-done.18 = bf16[32,16,256]{2,1,0:T(8,128)(2,1)S(1)} collective-permute-done((bf16[32,16,256]{2,1,0:T(8,128)(2,1)S(1)}, bf16[32,16,256]{2,1,0:T(8,128)(2,1)S(1)}, u32[]{:S(2)}, u32[]{:S(2)}) %collective-permute-start.18) | collective-permute-done | bytes 262176 | tf_op jit(solution)/shard_map/ppermute | solution.py:100
  89.8 1.2 collective-permute-start.13
  91.6 2.8 %collective-permute-done.17 = bf16[32,16,256]{2,1,0:T(8,128)(2,1)S(1)} collective-permute-done((bf16[32,16,256]{2,1,0:T(8,128)(2,1)S(1)}, bf16[32,16,256]{2,1,0:T(8,128)(2,1)S(1)}, u32[]{:S(2)}, u32[]{:S(2)}) %collective-permute-start.17) | collective-permute-done | bytes 262176 | tf_op jit(solution)/shard_map/ppermute | solution.py:100
  94.4 4.3 %collective-permute-done.16 = bf16[32,16,256]{2,1,0:T(8,128)(2,1)S(1)} collective-permute-done((bf16[32,16,256]{2,1,0:T(8,128)(2,1)S(1)}, bf16[32,16,256]{2,1,0:T(8,128)(2,1)S(1)}, u32[]{:S(2)}, u32[]{:S(2)}) %collective-permute-start.16) | collective-permute-done | bytes 262176 | tf_op jit(solution)/shard_map/ppermute | solution.py:100
  98.7 1.4 collective-permute-done.13
  101.0 1.5 multiply_bitcast_fusion
  103.2 5.7 %collective-permute-start.12 = (bf16[8,256,256]{2,1,0:T(8,128)(2,1)S(1)}, bf16[8,256,256]{2,1,0:T(8,128)(2,1)S(1)}, u32[]{:S(2)}, u32[]{:S(2)}) collective-permute-start(bf16[8,256,256]{2,1,0:T(8,128)(2,1)S(1)} %convolution_convert_fusion.1), channel_id=1, source_target_pairs={{0,24},{24,0},{1,25},{25,1},{2,26},{26,2},{3,27},{27,3},{4,28},{28... | collective-permute-start | bytes 3145736 | tf_op jit(solution)/shard_map/ppermute | solution.py:107
  111.9 0.8 collective-permute-start.38
  112.9 3.7 %collective-permute-start.37 = (bf16[8,4,16,256]{3,0,2,1:T(8,128)(2,1)S(1)}, bf16[8,4,16,256]{3,0,2,1:T(8,128)(2,1)S(1)}, u32[]{:S(2)}, u32[]{:S(2)}) collective-permute-start(bf16[8,4,16,256]{3,0,2,1:T(8,128)(2,1)S(1)} %bitcast.242), channel_id=1, source_target_pairs={{0,24},{24,0},{8,16},{16,8},{1,25},{25,1},{9,17},{17,9},{2,26},{26... | collective-permute-start | bytes 786440 | tf_op jit(solution)/shard_map/ppermute | solution.py:115
  116.6 16.5 %collective-permute-done.12 = bf16[8,256,256]{2,1,0:T(8,128)(2,1)S(1)} collective-permute-done((bf16[8,256,256]{2,1,0:T(8,128)(2,1)S(1)}, bf16[8,256,256]{2,1,0:T(8,128)(2,1)S(1)}, u32[]{:S(2)}, u32[]{:S(2)}) %collective-permute-start.12) | collective-permute-done | bytes 1048608 | tf_op jit(solution)/shard_map/ppermute | solution.py:107
  134.0 1.7 collective-permute-start.22
  136.8 2.0 collective-permute-done.21
  138.8 1.2 collective-permute-start.23
  140.0 32.7 %collective-permute-start.24 = (bf16[8,32,256]{2,0,1:T(8,128)(2,1)S(1)}, bf16[8,32,256]{2,0,1:T(8,128)(2,1)S(1)}, u32[]{:S(2)}, u32[]{:S(2)}) collective-permute-start(bf16[8,32,256]{2,0,1:T(8,128)(2,1)S(1)} %bitcast.250), channel_id=1, source_target_pairs={{0,8},{24,16},{1,9},{25,17},{2,10},{26,18},{3,11},{27,19},{8,0},{1... | collective-permute-start | bytes 393224 | tf_op jit(solution)/shard_map/ppermute | solution.py:100
  172.7 4.1 %collective-permute-start.25 = (bf16[8,32,256]{2,0,1:T(8,128)(2,1)S(1)}, bf16[8,32,256]{2,0,1:T(8,128)(2,1)S(1)}, u32[]{:S(2)}, u32[]{:S(2)}) collective-permute-start(bf16[8,32,256]{2,0,1:T(8,128)(2,1)S(1)} %bitcast.249), channel_id=1, source_target_pairs={{0,9},{24,17},{1,8},{25,16},{2,11},{26,19},{3,10},{27,18},{8,1},{1... | collective-permute-start | bytes 393224 | tf_op jit(solution)/shard_map/ppermute | solution.py:100
  177.1 2.3 collective-permute-start.26
  179.4 0.9 collective-permute-done.25
  180.3 5.1 %collective-permute-start.27 = (bf16[8,32,256]{2,0,1:T(8,128)(2,1)S(1)}, bf16[8,32,256]{2,0,1:T(8,128)(2,1)S(1)}, u32[]{:S(2)}, u32[]{:S(2)}) collective-permute-start(bf16[8,32,256]{2,0,1:T(8,128)(2,1)S(1)} %bitcast.247), channel_id=1, source_target_pairs={{0,11},{24,19},{1,10},{25,18},{2,9},{26,17},{3,8},{27,16},{8,3},{1... | collective-permute-start | bytes 393224 | tf_op jit(solution)/shard_map/ppermute | solution.py:100
  186.0 1.3 collective-permute-start.29
  187.3 4.1 %collective-permute-done.27 = bf16[8,32,256]{2,0,1:T(8,128)(2,1)S(1)} collective-permute-done((bf16[8,32,256]{2,0,1:T(8,128)(2,1)S(1)}, bf16[8,32,256]{2,0,1:T(8,128)(2,1)S(1)}, u32[]{:S(2)}, u32[]{:S(2)}) %collective-permute-start.27) | collective-permute-done | bytes 131104 | tf_op jit(solution)/shard_map/ppermute | solution.py:100
  191.4 1.7 collective-permute-start.30
  193.1 1.5 collective-permute-start.28
  195.1 1.6 collective-permute-start.40
  196.7 1.7 collective-permute-start.41
  198.4 7.9 %collective-permute-done.30 = bf16[8,4,16,256]{3,0,2,1:T(8,128)(2,1)S(1)} collective-permute-done((bf16[8,4,16,256]{3,0,2,1:T(8,128)(2,1)S(1)}, bf16[8,4,16,256]{3,0,2,1:T(8,128)(2,1)S(1)}, u32[]{:S(2)}, u32[]{:S(2)}) %collective-permute-start.30) | collective-permute-done | bytes 262176 | tf_op jit(solution)/shard_map/ppermute | solution.py:115
  206.3 2.2 collective-permute-start.42
  209.0 1.5 collective-permute-start.31
  210.7 1.9 collective-permute-start.33
  212.9 3.2 %collective-permute-done.31 = bf16[2,8,16,256]{3,1,2,0:T(8,128)(2,1)S(1)} collective-permute-done((bf16[2,8,16,256]{3,1,2,0:T(8,128)(2,1)S(1)}, bf16[2,8,16,256]{3,1,2,0:T(8,128)(2,1)S(1)}, u32[]{:S(2)}, u32[]{:S(2)}) %collective-permute-start.31) | collective-permute-done | bytes 131104 | tf_op jit(solution)/shard_map/ppermute | solution.py:89
  217.3 2.0 collective-permute-done.33
  221.2 2.1 collective-permute-start.34
  223.5 1.5 collective-permute-start.36
  224.9 2.0 collective-permute-start.43
  227.4 2.3 collective-permute-done.34
  229.7 1.6 collective-permute-start.45
  231.5 1.7 collective-permute-done.35
  233.6 1.8 collective-permute-done.43
  235.6 3.2 %collective-permute-done.44 = bf16[16,32,256]{2,1,0:T(8,128)(2,1)S(1)} collective-permute-done((bf16[16,32,256]{2,1,0:T(8,128)(2,1)S(1)}, bf16[16,32,256]{2,1,0:T(8,128)(2,1)S(1)}, u32[]{:S(2)}, u32[]{:S(2)}) %collective-permute-start.44) | collective-permute-done | bytes 262176 | tf_op jit(solution)/shard_map/ppermute | solution.py:89
  239.1 1.3 copy-done.3
  (197 shorter events, 23.2 us)
Async XLA Ops:
  0.0 1.6 copy-start
  1.9 27.6 %collective-permute-start.2 = (bf16[32,32,256]{2,1,0:T(8,128)(2,1)S(1)}, bf16[32,32,256]{2,1,0:T(8,128)(2,1)}, u32[]{:S(2)}, u32[]{:S(2)}) collective-permute-start(bf16[32,32,256]{2,1,0:T(8,128)(2,1)S(1)} %bitcast.236), channel_id=1, source_target_pairs={{0,3},{1,2},{2,1},{3,0},{4,7},{5,6},{6,5},{7,4},{8,11},{9,10},{10,... | collective-permute-start | bytes 1572872 | tf_op jit(solution)/shard_map/ppermute | solution.py:89
  6.5 23.0 %collective-permute-start.1 = (bf16[32,32,256]{2,1,0:T(8,128)(2,1)S(1)}, bf16[32,32,256]{2,1,0:T(8,128)(2,1)}, u32[]{:S(2)}, u32[]{:S(2)}) collective-permute-start(bf16[32,32,256]{2,1,0:T(8,128)(2,1)S(1)} %bitcast.237), channel_id=1, source_target_pairs={{0,2},{1,3},{2,0},{3,1},{4,6},{5,7},{6,4},{7,5},{8,10},{9,11},{10,... | collective-permute-start | bytes 1572872 | tf_op jit(solution)/shard_map/ppermute | solution.py:89
  7.3 3.2 %copy-start.5 = (bf16[4,128,128]{2,1,0:T(8,128)(2,1)S(1)}, bf16[4,128,128]{2,1,0:T(8,128)(2,1)}, u32[]{:S(2)}) copy-start(bf16[4,128,128]{2,1,0:T(8,128)(2,1)} %param.10) | copy-start | bytes 393220
  7.3 3.6 %copy-start.13 = (f32[128]{0:T(128)S(1)}, f32[128]{0:T(128)}, u32[]{:S(2)}) copy-start(f32[128]{0:T(128)} %param.9) | copy-start | bytes 1540
  8.4 6.6 %copy-start.11 = (bf16[128,128]{1,0:T(8,128)(2,1)S(1)}, bf16[128,128]{1,0:T(8,128)(2,1)}, u32[]{:S(2)}) copy-start(bf16[128,128]{1,0:T(8,128)(2,1)} %param.13) | copy-start | bytes 98308
  8.4 21.0 %collective-permute-start = (bf16[32,32,256]{2,1,0:T(8,128)(2,1)}, bf16[32,32,256]{2,1,0:T(8,128)(2,1)}, u32[]{:S(2)}, u32[]{:S(2)}) collective-permute-start(bf16[32,32,256]{2,1,0:T(8,128)(2,1)} %bitcast.216), channel_id=1, source_target_pairs={{0,1},{1,0},{2,3},{3,2},{4,5},{5,4},{6,7},{7,6},{8,9},{9,8},{10,11... | collective-permute-start | bytes 1572872 | tf_op jit(solution)/shard_map/ppermute | solution.py:89
  8.5 6.8 %copy-start.12 = (bf16[128,128]{1,0:T(8,128)(2,1)S(1)}, bf16[128,128]{1,0:T(8,128)(2,1)}, u32[]{:S(2)}) copy-start(bf16[128,128]{1,0:T(8,128)(2,1)} %param.11) | copy-start | bytes 98308
  34.9 9.5 %collective-permute-start.3 = (bf16[32,16,256]{2,1,0:T(8,128)(2,1)}, bf16[32,16,256]{2,1,0:T(8,128)(2,1)S(1)}, u32[]{:S(2)}, u32[]{:S(2)}) collective-permute-start(bf16[32,16,256]{2,1,0:T(8,128)(2,1)} %get-tuple-element.37), channel_id=1, source_target_pairs={{0,1},{24,25},{1,0},{25,24},{2,3},{26,27},{3,2},{27,26},{8,9},{16,... | collective-permute-start | bytes 786440 | tf_op jit(solution)/shard_map/ppermute | solution.py:100
  36.5 11.9 %collective-permute-start.4 = (bf16[32,16,256]{2,1,0:T(8,128)(2,1)}, bf16[32,16,256]{2,1,0:T(8,128)(2,1)S(1)}, u32[]{:S(2)}, u32[]{:S(2)}) collective-permute-start(bf16[32,16,256]{2,1,0:T(8,128)(2,1)} %get-tuple-element.38), channel_id=1, source_target_pairs={{0,2},{24,26},{1,3},{25,27},{2,0},{26,24},{3,1},{27,25},{8,10},{16... | collective-permute-start | bytes 786440 | tf_op jit(solution)/shard_map/ppermute | solution.py:100
  37.6 14.7 %collective-permute-start.5 = (bf16[32,16,256]{2,1,0:T(8,128)(2,1)}, bf16[32,16,256]{2,1,0:T(8,128)(2,1)S(1)}, u32[]{:S(2)}, u32[]{:S(2)}) collective-permute-start(bf16[32,16,256]{2,1,0:T(8,128)(2,1)} %get-tuple-element.39), channel_id=1, source_target_pairs={{0,3},{24,27},{1,2},{25,26},{2,1},{26,25},{3,0},{27,24},{8,11},{16... | collective-permute-start | bytes 786440 | tf_op jit(solution)/shard_map/ppermute | solution.py:100
  38.5 2.4 %copy-start.4 = (bf16[32,16,256]{2,1,0:T(8,128)(2,1)S(1)}, bf16[32,16,256]{2,1,0:T(8,128)(2,1)}, u32[]{:S(2)}) copy-start(bf16[32,16,256]{2,1,0:T(8,128)(2,1)} %get-tuple-element.36) | copy-start | bytes 786436
  38.5 2.4 %copy-start.10 = (bf16[32,16,256]{2,1,0:T(8,128)(2,1)S(1)}, bf16[32,16,256]{2,1,0:T(8,128)(2,1)}, u32[]{:S(2)}) copy-start(bf16[32,16,256]{2,1,0:T(8,128)(2,1)} %get-tuple-element.40) | copy-start | bytes 786436
  38.5 4.1 %copy-start.9 = (bf16[32,16,256]{2,1,0:T(8,128)(2,1)S(1)}, bf16[32,16,256]{2,1,0:T(8,128)(2,1)}, u32[]{:S(2)}) copy-start(bf16[32,16,256]{2,1,0:T(8,128)(2,1)} %get-tuple-element.41) | copy-start | bytes 786436
  38.5 5.9 %copy-start.8 = (bf16[32,16,256]{2,1,0:T(8,128)(2,1)S(1)}, bf16[32,16,256]{2,1,0:T(8,128)(2,1)}, u32[]{:S(2)}) copy-start(bf16[32,16,256]{2,1,0:T(8,128)(2,1)} %get-tuple-element.42) | copy-start | bytes 786436
  38.5 9.9 %copy-start.7 = (bf16[32,16,256]{2,1,0:T(8,128)(2,1)S(1)}, bf16[32,16,256]{2,1,0:T(8,128)(2,1)}, u32[]{:S(2)}) copy-start(bf16[32,16,256]{2,1,0:T(8,128)(2,1)} %get-tuple-element.43) | copy-start | bytes 786436
  40.9 11.5 %collective-permute-start.6 = (bf16[32,16,256]{2,1,0:T(8,128)(2,1)S(1)}, bf16[32,16,256]{2,1,0:T(8,128)(2,1)S(1)}, u32[]{:S(2)}, u32[]{:S(2)}) collective-permute-start(bf16[32,16,256]{2,1,0:T(8,128)(2,1)S(1)} %copy-done.10), channel_id=1, source_target_pairs={{0,8},{24,16},{1,9},{25,17},{2,10},{26,18},{3,11},{27,19},{8,0},{1... | collective-permute-start | bytes 786440 | tf_op jit(solution)/shard_map/ppermute | solution.py:100
  42.6 14.1 %collective-permute-start.7 = (bf16[32,16,256]{2,1,0:T(8,128)(2,1)S(1)}, bf16[32,16,256]{2,1,0:T(8,128)(2,1)S(1)}, u32[]{:S(2)}, u32[]{:S(2)}) collective-permute-start(bf16[32,16,256]{2,1,0:T(8,128)(2,1)S(1)} %copy-done.9), channel_id=1, source_target_pairs={{0,9},{24,17},{1,8},{25,16},{2,11},{26,19},{3,10},{27,18},{8,1},{1... | collective-permute-start | bytes 786440 | tf_op jit(solution)/shard_map/ppermute | solution.py:100
  44.4 17.9 %collective-permute-start.8 = (bf16[32,16,256]{2,1,0:T(8,128)(2,1)S(1)}, bf16[32,16,256]{2,1,0:T(8,128)(2,1)S(1)}, u32[]{:S(2)}, u32[]{:S(2)}) collective-permute-start(bf16[32,16,256]{2,1,0:T(8,128)(2,1)S(1)} %copy-done.8), channel_id=1, source_target_pairs={{0,10},{24,18},{1,11},{25,19},{2,8},{26,16},{3,9},{27,17},{8,2},{1... | collective-permute-start | bytes 786440 | tf_op jit(solution)/shard_map/ppermute | solution.py:100
  48.4 18.3 %collective-permute-start.9 = (bf16[32,16,256]{2,1,0:T(8,128)(2,1)S(1)}, bf16[32,16,256]{2,1,0:T(8,128)(2,1)S(1)}, u32[]{:S(2)}, u32[]{:S(2)}) collective-permute-start(bf16[32,16,256]{2,1,0:T(8,128)(2,1)S(1)} %copy-done.7), channel_id=1, source_target_pairs={{0,11},{24,19},{1,10},{25,18},{2,9},{26,17},{3,8},{27,16},{8,3},{1... | collective-permute-start | bytes 786440 | tf_op jit(solution)/shard_map/ppermute | solution.py:100
  52.4 14.5 %copy-start.2 = (bf16[32,128,256]{2,1,0:T(8,128)(2,1)S(1)}, bf16[32,128,256]{2,1,0:T(8,128)(2,1)}, u32[]{:S(2)}) copy-start(bf16[32,128,256]{2,1,0:T(8,128)(2,1)} %get-tuple-element.45) | copy-start | bytes 6291460
  52.4 14.5 %copy-start.6 = (f32[32,256]{1,0:T(8,128)S(1)}, f32[32,256]{1,0:T(8,128)}, u32[]{:S(2)}) copy-start(f32[32,256]{1,0:T(8,128)} %dynamic-slice_convert_fusion.refs_4_) | copy-start | bytes 98308
  66.8 7.7 %collective-permute-start.10 = (bf16[256,8,256]{2,1,0:T(8,128)(2,1)S(1)}, bf16[256,8,256]{2,1,0:T(8,128)(2,1)S(1)}, u32[]{:S(2)}, u32[]{:S(2)}) collective-permute-start(bf16[256,8,256]{2,1,0:T(8,128)(2,1)S(1)} %slice.289), channel_id=1, source_target_pairs={{0,4},{4,0},{1,5},{5,1},{2,6},{6,2},{3,7},{7,3},{8,12},{12,8},{9,1... | collective-permute-start | bytes 3145736 | tf_op jit(solution)/shard_map/ppermute | solution.py:161
  68.6 12.0 %collective-permute-start.19 = (bf16[32,16,256]{2,1,0:T(8,128)(2,1)S(1)}, bf16[32,16,256]{2,1,0:T(8,128)(2,1)S(1)}, u32[]{:S(2)}, u32[]{:S(2)}) collective-permute-start(bf16[32,16,256]{2,1,0:T(8,128)(2,1)S(1)} %get-tuple-element.67), channel_id=1, source_target_pairs={{0,11},{24,19},{1,10},{25,18},{2,9},{26,17},{3,8},{27,16},{8,3},{1... | collective-permute-start | bytes 786440 | tf_op jit(solution)/shard_map/ppermute | solution.py:100
  70.4 19.3 %collective-permute-start.18 = (bf16[32,16,256]{2,1,0:T(8,128)(2,1)S(1)}, bf16[32,16,256]{2,1,0:T(8,128)(2,1)S(1)}, u32[]{:S(2)}, u32[]{:S(2)}) collective-permute-start(bf16[32,16,256]{2,1,0:T(8,128)(2,1)S(1)} %get-tuple-element.68), channel_id=1, source_target_pairs={{0,10},{24,18},{1,11},{25,19},{2,8},{26,16},{3,9},{27,17},{8,2},{1... | collective-permute-start | bytes 786440 | tf_op jit(solution)/shard_map/ppermute | solution.py:100
  71.8 22.5 %collective-permute-start.17 = (bf16[32,16,256]{2,1,0:T(8,128)(2,1)S(1)}, bf16[32,16,256]{2,1,0:T(8,128)(2,1)S(1)}, u32[]{:S(2)}, u32[]{:S(2)}) collective-permute-start(bf16[32,16,256]{2,1,0:T(8,128)(2,1)S(1)} %get-tuple-element.69), channel_id=1, source_target_pairs={{0,9},{24,17},{1,8},{25,16},{2,11},{26,19},{3,10},{27,18},{8,1},{1... | collective-permute-start | bytes 786440 | tf_op jit(solution)/shard_map/ppermute | solution.py:100
  74.2 24.5 %collective-permute-start.16 = (bf16[32,16,256]{2,1,0:T(8,128)(2,1)S(1)}, bf16[32,16,256]{2,1,0:T(8,128)(2,1)S(1)}, u32[]{:S(2)}, u32[]{:S(2)}) collective-permute-start(bf16[32,16,256]{2,1,0:T(8,128)(2,1)S(1)} %get-tuple-element.70), channel_id=1, source_target_pairs={{0,8},{24,16},{1,9},{25,17},{2,10},{26,18},{3,11},{27,19},{8,0},{1... | collective-permute-start | bytes 786440 | tf_op jit(solution)/shard_map/ppermute | solution.py:100
  74.5 24.2 %collective-permute-start.15 = (bf16[32,16,256]{2,1,0:T(8,128)(2,1)S(1)}, bf16[32,16,256]{2,1,0:T(8,128)(2,1)S(1)}, u32[]{:S(2)}, u32[]{:S(2)}) collective-permute-start(bf16[32,16,256]{2,1,0:T(8,128)(2,1)S(1)} %get-tuple-element.71), channel_id=1, source_target_pairs={{0,3},{24,27},{1,2},{25,26},{2,1},{26,25},{3,0},{27,24},{8,11},{16... | collective-permute-start | bytes 786440 | tf_op jit(solution)/shard_map/ppermute | solution.py:100
  80.5 18.1 %collective-permute-start.14 = (bf16[32,16,256]{2,1,0:T(8,128)(2,1)S(1)}, bf16[32,16,256]{2,1,0:T(8,128)(2,1)S(1)}, u32[]{:S(2)}, u32[]{:S(2)}) collective-permute-start(bf16[32,16,256]{2,1,0:T(8,128)(2,1)S(1)} %get-tuple-element.72), channel_id=1, source_target_pairs={{0,2},{24,26},{1,3},{25,27},{2,0},{26,24},{3,1},{27,25},{8,10},{16... | collective-permute-start | bytes 786440 | tf_op jit(solution)/shard_map/ppermute | solution.py:100
  89.8 10.3 %collective-permute-start.13 = (bf16[32,16,256]{2,1,0:T(8,128)(2,1)S(1)}, bf16[32,16,256]{2,1,0:T(8,128)(2,1)S(1)}, u32[]{:S(2)}, u32[]{:S(2)}) collective-permute-start(bf16[32,16,256]{2,1,0:T(8,128)(2,1)S(1)} %get-tuple-element.73), channel_id=1, source_target_pairs={{0,1},{24,25},{1,0},{25,24},{2,3},{26,27},{3,2},{27,26},{8,9},{16,... | collective-permute-start | bytes 786440 | tf_op jit(solution)/shard_map/ppermute | solution.py:100
  100.2 0.7 copy-start.14
  100.4 9.2 %collective-permute-start.20 = (bf16[256,8,256]{2,1,0:T(8,128)(2,1)S(1)}, bf16[256,8,256]{2,1,0:T(8,128)(2,1)S(1)}, u32[]{:S(2)}, u32[]{:S(2)}) collective-permute-start(bf16[256,8,256]{2,1,0:T(8,128)(2,1)S(1)} %slice.291), channel_id=1, source_target_pairs={{0,4},{4,0},{1,5},{5,1},{2,6},{6,2},{3,7},{7,3},{8,12},{12,8},{9,1... | collective-permute-start | bytes 3145736 | tf_op jit(solution)/shard_map/ppermute | solution.py:161
  102.5 14.1 %collective-permute-start.11 = (bf16[8,256,256]{2,1,0:T(8,128)(2,1)S(1)}, bf16[8,256,256]{2,1,0:T(8,128)(2,1)S(1)}, u32[]{:S(2)}, u32[]{:S(2)}) collective-permute-start(bf16[8,256,256]{2,1,0:T(8,128)(2,1)S(1)} %convolution_convert_fusion.1), channel_id=1, source_target_pairs={{8,16},{16,8},{9,17},{17,9},{10,18},{18,10},{11,19},{19,11},{12,20... | collective-permute-start | bytes 3145736 | tf_op jit(solution)/shard_map/ppermute | solution.py:107
  103.2 29.9 %collective-permute-start.12 = (bf16[8,256,256]{2,1,0:T(8,128)(2,1)S(1)}, bf16[8,256,256]{2,1,0:T(8,128)(2,1)S(1)}, u32[]{:S(2)}, u32[]{:S(2)}) collective-permute-start(bf16[8,256,256]{2,1,0:T(8,128)(2,1)S(1)} %convolution_convert_fusion.1), channel_id=1, source_target_pairs={{0,24},{24,0},{1,25},{25,1},{2,26},{26,2},{3,27},{27,3},{4,28},{28... | collective-permute-start | bytes 3145736 | tf_op jit(solution)/shard_map/ppermute | solution.py:107
  110.7 82.4 %collective-permute-start.39 = (bf16[8,4,16,256]{3,0,2,1:T(8,128)(2,1)S(1)}, bf16[8,4,16,256]{3,0,2,1:T(8,128)(2,1)S(1)}, u32[]{:S(2)}, u32[]{:S(2)}) collective-permute-start(bf16[8,4,16,256]{3,0,2,1:T(8,128)(2,1)S(1)} %bitcast.240), channel_id=1, source_target_pairs={{0,16},{24,8},{8,24},{16,0},{1,17},{25,9},{9,25},{17,1},{2,18},{26... | collective-permute-start | bytes 786440 | tf_op jit(solution)/shard_map/ppermute | solution.py:115
  111.9 83.1 %collective-permute-start.38 = (bf16[8,4,16,256]{3,0,2,1:T(8,128)(2,1)S(1)}, bf16[8,4,16,256]{3,0,2,1:T(8,128)(2,1)S(1)}, u32[]{:S(2)}, u32[]{:S(2)}) collective-permute-start(bf16[8,4,16,256]{3,0,2,1:T(8,128)(2,1)S(1)} %bitcast.241), channel_id=1, source_target_pairs={{0,8},{24,16},{8,0},{16,24},{1,9},{25,17},{9,1},{17,25},{2,10},{26... | collective-permute-start | bytes 786440 | tf_op jit(solution)/shard_map/ppermute | solution.py:115
  112.9 81.7 %collective-permute-start.37 = (bf16[8,4,16,256]{3,0,2,1:T(8,128)(2,1)S(1)}, bf16[8,4,16,256]{3,0,2,1:T(8,128)(2,1)S(1)}, u32[]{:S(2)}, u32[]{:S(2)}) collective-permute-start(bf16[8,4,16,256]{3,0,2,1:T(8,128)(2,1)S(1)} %bitcast.242), channel_id=1, source_target_pairs={{0,24},{24,0},{8,16},{16,8},{1,25},{25,1},{9,17},{17,9},{2,26},{26... | collective-permute-start | bytes 786440 | tf_op jit(solution)/shard_map/ppermute | solution.py:115
  133.8 5.0 %collective-permute-start.21 = (bf16[8,32,256]{2,0,1:T(8,128)(2,1)S(1)}, bf16[8,32,256]{2,0,1:T(8,128)(2,1)S(1)}, u32[]{:S(2)}, u32[]{:S(2)}) collective-permute-start(bf16[8,32,256]{2,0,1:T(8,128)(2,1)S(1)} %bitcast.253), channel_id=1, source_target_pairs={{0,1},{24,25},{1,0},{25,24},{2,3},{26,27},{3,2},{27,26},{8,9},{16,... | collective-permute-start | bytes 393224 | tf_op jit(solution)/shard_map/ppermute | solution.py:100
  134.0 6.0 %collective-permute-start.22 = (bf16[8,32,256]{2,0,1:T(8,128)(2,1)S(1)}, bf16[8,32,256]{2,0,1:T(8,128)(2,1)S(1)}, u32[]{:S(2)}, u32[]{:S(2)}) collective-permute-start(bf16[8,32,256]{2,0,1:T(8,128)(2,1)S(1)} %bitcast.251), channel_id=1, source_target_pairs={{0,2},{24,26},{1,3},{25,27},{2,0},{26,24},{3,1},{27,25},{8,10},{16... | collective-permute-start | bytes 393224 | tf_op jit(solution)/shard_map/ppermute | solution.py:100
  138.8 33.9 %collective-permute-start.23 = (bf16[8,32,256]{2,0,1:T(8,128)(2,1)S(1)}, bf16[8,32,256]{2,0,1:T(8,128)(2,1)S(1)}, u32[]{:S(2)}, u32[]{:S(2)}) collective-permute-start(bf16[8,32,256]{2,0,1:T(8,128)(2,1)S(1)} %bitcast.252), channel_id=1, source_target_pairs={{0,3},{24,27},{1,2},{25,26},{2,1},{26,25},{3,0},{27,24},{8,11},{16... | collective-permute-start | bytes 393224 | tf_op jit(solution)/shard_map/ppermute | solution.py:100
  140.0 37.0 %collective-permute-start.24 = (bf16[8,32,256]{2,0,1:T(8,128)(2,1)S(1)}, bf16[8,32,256]{2,0,1:T(8,128)(2,1)S(1)}, u32[]{:S(2)}, u32[]{:S(2)}) collective-permute-start(bf16[8,32,256]{2,0,1:T(8,128)(2,1)S(1)} %bitcast.250), channel_id=1, source_target_pairs={{0,8},{24,16},{1,9},{25,17},{2,10},{26,18},{3,11},{27,19},{8,0},{1... | collective-permute-start | bytes 393224 | tf_op jit(solution)/shard_map/ppermute | solution.py:100
  172.7 7.5 %collective-permute-start.25 = (bf16[8,32,256]{2,0,1:T(8,128)(2,1)S(1)}, bf16[8,32,256]{2,0,1:T(8,128)(2,1)S(1)}, u32[]{:S(2)}, u32[]{:S(2)}) collective-permute-start(bf16[8,32,256]{2,0,1:T(8,128)(2,1)S(1)} %bitcast.249), channel_id=1, source_target_pairs={{0,9},{24,17},{1,8},{25,16},{2,11},{26,19},{3,10},{27,18},{8,1},{1... | collective-permute-start | bytes 393224 | tf_op jit(solution)/shard_map/ppermute | solution.py:100
  177.1 8.9 %collective-permute-start.26 = (bf16[8,32,256]{2,0,1:T(8,128)(2,1)S(1)}, bf16[8,32,256]{2,0,1:T(8,128)(2,1)S(1)}, u32[]{:S(2)}, u32[]{:S(2)}) collective-permute-start(bf16[8,32,256]{2,0,1:T(8,128)(2,1)S(1)} %bitcast.248), channel_id=1, source_target_pairs={{0,10},{24,18},{1,11},{25,19},{2,8},{26,16},{3,9},{27,17},{8,2},{1... | collective-permute-start | bytes 393224 | tf_op jit(solution)/shard_map/ppermute | solution.py:100
  180.3 11.1 %collective-permute-start.27 = (bf16[8,32,256]{2,0,1:T(8,128)(2,1)S(1)}, bf16[8,32,256]{2,0,1:T(8,128)(2,1)S(1)}, u32[]{:S(2)}, u32[]{:S(2)}) collective-permute-start(bf16[8,32,256]{2,0,1:T(8,128)(2,1)S(1)} %bitcast.247), channel_id=1, source_target_pairs={{0,11},{24,19},{1,10},{25,18},{2,9},{26,17},{3,8},{27,16},{8,3},{1... | collective-permute-start | bytes 393224 | tf_op jit(solution)/shard_map/ppermute | solution.py:100
  186.0 22.9 %collective-permute-start.29 = (bf16[8,4,16,256]{3,0,2,1:T(8,128)(2,1)S(1)}, bf16[8,4,16,256]{3,0,2,1:T(8,128)(2,1)S(1)}, u32[]{:S(2)}, u32[]{:S(2)}) collective-permute-start(bf16[8,4,16,256]{3,0,2,1:T(8,128)(2,1)S(1)} %bitcast.243), channel_id=1, source_target_pairs={{0,8},{24,16},{8,0},{16,24},{1,9},{25,17},{9,1},{17,25},{2,10},{26... | collective-permute-start | bytes 786440 | tf_op jit(solution)/shard_map/ppermute | solution.py:115
  191.4 14.9 %collective-permute-start.30 = (bf16[8,4,16,256]{3,0,2,1:T(8,128)(2,1)S(1)}, bf16[8,4,16,256]{3,0,2,1:T(8,128)(2,1)S(1)}, u32[]{:S(2)}, u32[]{:S(2)}) collective-permute-start(bf16[8,4,16,256]{3,0,2,1:T(8,128)(2,1)S(1)} %bitcast.245), channel_id=1, source_target_pairs={{0,16},{24,8},{8,24},{16,0},{1,17},{25,9},{9,25},{17,1},{2,18},{26... | collective-permute-start | bytes 786440 | tf_op jit(solution)/shard_map/ppermute | solution.py:115
  193.1 15.3 %collective-permute-start.28 = (bf16[8,4,16,256]{3,0,2,1:T(8,128)(2,1)S(1)}, bf16[8,4,16,256]{3,0,2,1:T(8,128)(2,1)S(1)}, u32[]{:S(2)}, u32[]{:S(2)}) collective-permute-start(bf16[8,4,16,256]{3,0,2,1:T(8,128)(2,1)S(1)} %bitcast.244), channel_id=1, source_target_pairs={{0,24},{24,0},{8,16},{16,8},{1,25},{25,1},{9,17},{17,9},{2,26},{26... | collective-permute-start | bytes 786440 | tf_op jit(solution)/shard_map/ppermute | solution.py:115
  195.1 15.6 %collective-permute-start.40 = (bf16[2,8,16,256]{3,1,2,0:T(8,128)(2,1)S(1)}, bf16[2,8,16,256]{3,1,2,0:T(8,128)(2,1)S(1)}, u32[]{:S(2)}, u32[]{:S(2)}) collective-permute-start(bf16[2,8,16,256]{3,1,2,0:T(8,128)(2,1)S(1)} %get-tuple-element.95), channel_id=1, source_target_pairs={{0,1},{1,0},{2,3},{3,2},{4,5},{5,4},{6,7},{7,6},{8,9},{9,8},{10,11... | collective-permute-start | bytes 393224 | tf_op jit(solution)/shard_map/ppermute | solution.py:89
  196.7 15.9 %collective-permute-start.41 = (bf16[2,8,16,256]{3,1,2,0:T(8,128)(2,1)S(1)}, bf16[2,8,16,256]{3,1,2,0:T(8,128)(2,1)S(1)}, u32[]{:S(2)}, u32[]{:S(2)}) collective-permute-start(bf16[2,8,16,256]{3,1,2,0:T(8,128)(2,1)S(1)} %get-tuple-element.96), channel_id=1, source_target_pairs={{0,2},{1,3},{2,0},{3,1},{4,6},{5,7},{6,4},{7,5},{8,10},{9,11},{10,... | collective-permute-start | bytes 393224 | tf_op jit(solution)/shard_map/ppermute | solution.py:89
  206.3 6.4 %collective-permute-start.42 = (bf16[2,8,16,256]{3,1,2,0:T(8,128)(2,1)S(1)}, bf16[2,8,16,256]{3,1,2,0:T(8,128)(2,1)S(1)}, u32[]{:S(2)}, u32[]{:S(2)}) collective-permute-start(bf16[2,8,16,256]{3,1,2,0:T(8,128)(2,1)S(1)} %get-tuple-element.93), channel_id=1, source_target_pairs={{0,3},{1,2},{2,1},{3,0},{4,7},{5,6},{6,5},{7,4},{8,11},{9,10},{10,... | collective-permute-start | bytes 393224 | tf_op jit(solution)/shard_map/ppermute | solution.py:89
  209.0 7.2 %collective-permute-start.31 = (bf16[2,8,16,256]{3,1,2,0:T(8,128)(2,1)S(1)}, bf16[2,8,16,256]{3,1,2,0:T(8,128)(2,1)S(1)}, u32[]{:S(2)}, u32[]{:S(2)}) collective-permute-start(bf16[2,8,16,256]{3,1,2,0:T(8,128)(2,1)S(1)} %get-tuple-element.101), channel_id=1, source_target_pairs={{0,1},{1,0},{2,3},{3,2},{4,5},{5,4},{6,7},{7,6},{8,9},{9,8},{10,11... | collective-permute-start | bytes 393224 | tf_op jit(solution)/shard_map/ppermute | solution.py:89
  210.5 6.8 %collective-permute-start.32 = (bf16[2,8,16,256]{3,1,2,0:T(8,128)(2,1)S(1)}, bf16[2,8,16,256]{3,1,2,0:T(8,128)(2,1)S(1)}, u32[]{:S(2)}, u32[]{:S(2)}) collective-permute-start(bf16[2,8,16,256]{3,1,2,0:T(8,128)(2,1)S(1)} %get-tuple-element.102), channel_id=1, source_target_pairs={{0,2},{1,3},{2,0},{3,1},{4,6},{5,7},{6,4},{7,5},{8,10},{9,11},{10,... | collective-permute-start | bytes 393224 | tf_op jit(solution)/shard_map/ppermute | solution.py:89
  210.7 8.6 %collective-permute-start.33 = (bf16[2,8,16,256]{3,1,2,0:T(8,128)(2,1)S(1)}, bf16[2,8,16,256]{3,1,2,0:T(8,128)(2,1)S(1)}, u32[]{:S(2)}, u32[]{:S(2)}) collective-permute-start(bf16[2,8,16,256]{3,1,2,0:T(8,128)(2,1)S(1)} %get-tuple-element.99), channel_id=1, source_target_pairs={{0,3},{1,2},{2,1},{3,0},{4,7},{5,6},{6,5},{7,4},{8,11},{9,10},{10,... | collective-permute-start | bytes 393224 | tf_op jit(solution)/shard_map/ppermute | solution.py:89
  221.2 8.5 %collective-permute-start.34 = (bf16[16,32,256]{2,1,0:T(8,128)(2,1)S(1)}, bf16[16,32,256]{2,1,0:T(8,128)(2,1)S(1)}, u32[]{:S(2)}, u32[]{:S(2)}) collective-permute-start(bf16[16,32,256]{2,1,0:T(8,128)(2,1)S(1)} %get-tuple-element.83), channel_id=1, source_target_pairs={{0,1},{1,0},{2,3},{3,2},{4,5},{5,4},{6,7},{7,6},{8,9},{9,8},{10,11... | collective-permute-start | bytes 786440 | tf_op jit(solution)/shard_map/ppermute | solution.py:89
  223.4 9.7 %collective-permute-start.35 = (bf16[16,32,256]{2,1,0:T(8,128)(2,1)S(1)}, bf16[16,32,256]{2,1,0:T(8,128)(2,1)S(1)}, u32[]{:S(2)}, u32[]{:S(2)}) collective-permute-start(bf16[16,32,256]{2,1,0:T(8,128)(2,1)S(1)} %get-tuple-element.82), channel_id=1, source_target_pairs={{0,2},{1,3},{2,0},{3,1},{4,6},{5,7},{6,4},{7,5},{8,10},{9,11},{10,... | collective-permute-start | bytes 786440 | tf_op jit(solution)/shard_map/ppermute | solution.py:89
  223.5 9.8 %collective-permute-start.36 = (bf16[16,32,256]{2,1,0:T(8,128)(2,1)S(1)}, bf16[16,32,256]{2,1,0:T(8,128)(2,1)S(1)}, u32[]{:S(2)}, u32[]{:S(2)}) collective-permute-start(bf16[16,32,256]{2,1,0:T(8,128)(2,1)S(1)} %get-tuple-element.81), channel_id=1, source_target_pairs={{0,3},{1,2},{2,1},{3,0},{4,7},{5,6},{6,5},{7,4},{8,11},{9,10},{10,... | collective-permute-start | bytes 786440 | tf_op jit(solution)/shard_map/ppermute | solution.py:89
  224.9 10.5 %collective-permute-start.43 = (bf16[16,32,256]{2,1,0:T(8,128)(2,1)S(1)}, bf16[16,32,256]{2,1,0:T(8,128)(2,1)S(1)}, u32[]{:S(2)}, u32[]{:S(2)}) collective-permute-start(bf16[16,32,256]{2,1,0:T(8,128)(2,1)S(1)} %get-tuple-element.77), channel_id=1, source_target_pairs={{0,1},{1,0},{2,3},{3,2},{4,5},{5,4},{6,7},{7,6},{8,9},{9,8},{10,11... | collective-permute-start | bytes 786440 | tf_op jit(solution)/shard_map/ppermute | solution.py:89
  227.0 11.8 %collective-permute-start.44 = (bf16[16,32,256]{2,1,0:T(8,128)(2,1)S(1)}, bf16[16,32,256]{2,1,0:T(8,128)(2,1)S(1)}, u32[]{:S(2)}, u32[]{:S(2)}) collective-permute-start(bf16[16,32,256]{2,1,0:T(8,128)(2,1)S(1)} %get-tuple-element.76), channel_id=1, source_target_pairs={{0,2},{1,3},{2,0},{3,1},{4,6},{5,7},{6,4},{7,5},{8,10},{9,11},{10,... | collective-permute-start | bytes 786440 | tf_op jit(solution)/shard_map/ppermute | solution.py:89
  227.0 13.4 %copy-start.1 = (bf16[32,128,256]{2,1,0:T(8,128)(2,1)S(1)}, bf16[32,128,256]{2,1,0:T(8,128)(2,1)}, u32[]{:S(2)}) copy-start(bf16[32,128,256]{2,1,0:T(8,128)(2,1)} %param.7) | copy-start | bytes 6291460
  229.7 9.2 %collective-permute-start.45 = (bf16[16,32,256]{2,1,0:T(8,128)(2,1)S(1)}, bf16[16,32,256]{2,1,0:T(8,128)(2,1)S(1)}, u32[]{:S(2)}, u32[]{:S(2)}) collective-permute-start(bf16[16,32,256]{2,1,0:T(8,128)(2,1)S(1)} %get-tuple-element.75), channel_id=1, source_target_pairs={{0,3},{1,2},{2,1},{3,0},{4,7},{5,6},{6,5},{7,4},{8,11},{9,10},{10,... | collective-permute-start | bytes 786440 | tf_op jit(solution)/shard_map/ppermute | solution.py:89
  239.1 1.3 copy-start.3

commit v3 on v2

--- a/solution.py
+++ b/solution.py
@@ -44,7 +44,7 @@
 def norm_and_gate(blocks, mask, gains, gates, sides, count):
     rows, width, columns = blocks[0].shape
     channels, outputs = len(blocks) * width, gates.shape[0]
-    some = min(rows, 8)
+    some = min(rows, 16)
     tall = lambda n: pl.BlockSpec((some, n, columns), lambda i: (i, 0, 0))
     whole = lambda a: pl.BlockSpec(a.shape, lambda i: (0, 0))
     return pl.pallas_call(
@@ -220,7 +220,9 @@
         ).astype(bf16)
         projected = jnp.einsum("hc,hrs->rcs", projection, hidden_normed, preferred_element_type=f32)
         update = (gate[at * step : (at + 1) * step] * projected).astype(bf16)
-        blocks.append([across_gz(update[:, m * local_channels : (m + 1) * local_channels], m) for m in range(planes)])
+        blocks.append(
+            [across_gz(update[:, m * local_channels : (m + 1) * local_channels], m) for m in reversed(range(planes))][::-1]
+        )
     out = jnp.zeros((rows, local_channels, columns), bf16)
     for at in range(pieces):
         for m in range(planes):

time: 241 us -> 241 us (level)
  no operation moved by 1% of the time
where the time goes in v3:
time: 241 us; the launch traced here: 240 us
  starting transfers between devices  103 us (43%)
  waiting for transfers between devices  101 us (42%)
  local copies, waits for them, and re-layouts  12.6 us (5%)
  matrix products  10.3 us (4%)
  other arithmetic  5.96 us (2%)
  Pallas kernels  5.07 us (2%)
    ppermute x21, starting transfers between devices, across_group(): return lax.ppermute(block, ('gx', 'gz'), pairs)  66.9 us
    ppermute x21, waiting for transfers between devices, across_group(): return lax.ppermute(block, ('gx', 'gz'), pairs)  48 us
    ppermute x15, waiting for transfers between devices, across_gz(): lax.ppermute(block, 'gz', [(i, i ^ m) for i in range(planes)])  28.8 us
    ppermute x15, starting transfers between devices, across_gz(): lax.ppermute(block, 'gz', [(i, i ^ m) for i in range(planes)])  21 us
    ppermute x2, waiting for transfers between devices, across_halves(): return lax.ppermute(block, 'gx', [(i, depth - 1 - i) for i in whose])  16.5 us
    ppermute x6, starting transfers between devices, to_plane(): return lax.ppermute(block, 'gx', pairs)  9.05 us
    ppermute x6, waiting for transfers between devices, to_plane(): return lax.ppermute(block, 'gx', pairs)  7.95 us
    unnamed x72, local copies, waits for them, and re-layouts  6.84 us
  transfers between devices with their start and end apart: 46, of which 26 were waited for; matrix products, arithmetic and copies ran while one was open for 10% of the time, Pallas kernels for 0%

profile of v3, /device:TPU:0, one launch (start us, length us, event | category | flops | bytes accessed | tf_op | source)
XLA Modules:
  0.0 240.0 jit_solution(17905212108098374100)
XLA Ops:
  0.0 1.6 copy-done
  1.9 4.0 %collective-permute-start.2 = (bf16[32,32,256]{2,1,0:T(8,128)(2,1)S(1)}, bf16[32,32,256]{2,1,0:T(8,128)(2,1)}, u32[]{:S(2)}, u32[]{:S(2)}) collective-permute-start(bf16[32,32,256]{2,1,0:T(8,128)(2,1)S(1)} %bitcast.236), channel_id=1, source_target_pairs={{0,3},{1,2},{2,1},{3,0},{4,7},{5,6},{6,5},{7,4},{8,11},{9,10},{10,... | collective-permute-start | bytes 1572872 | tf_op jit(solution)/shard_map/ppermute | solution.py:89
  7.3 1.1 copy.125
  9.1 1.1 copy.124
  13.6 1.4 dynamic-slice_convert_fusion.refs_4_
  15.6 13.8 %collective-permute-done.refs_1_ = bf16[32,32,256]{2,1,0:T(8,128)(2,1)} collective-permute-done((bf16[32,32,256]{2,1,0:T(8,128)(2,1)}, bf16[32,32,256]{2,1,0:T(8,128)(2,1)}, u32[]{:S(2)}, u32[]{:S(2)}) %collective-permute-start) | collective-permute-done | bytes 524320 | tf_op jit(solution)/shard_map/ppermute | solution.py:89
  29.5 5.1 %norm_and_gate.1 = (bf16[32,128,256]{2,1,0:T(8,128)(2,1)}, bf16[32,16,256]{2,1,0:T(8,128)(2,1)}, bf16[32,16,256]{2,1,0:T(8,128)(2,1)}, bf16[32,16,256]{2,1,0:T(8...) custom-call(bf16[32,32,256]{2,1,0:T(8,128)(2,1)} %bitcast.238, ...), custom_call_target="tpu_custom_call" | custom-call | flops 536870912 | bytes 8388608 | tf_op jit(solution)/shard_map/norm_and_gate/pallas_call | solution.py:50
  34.6 1.6 collective-permute-start.3
  36.1 1.2 collective-permute-start.4
  38.1 2.4 fusion.78
  40.6 1.6 collective-permute-start.6
  42.2 1.4 collective-permute-start.7
  44.0 2.4 %collective-permute-start.8 = (bf16[32,16,256]{2,1,0:T(8,128)(2,1)S(1)}, bf16[32,16,256]{2,1,0:T(8,128)(2,1)S(1)}, u32[]{:S(2)}, u32[]{:S(2)}) collective-permute-start(bf16[32,16,256]{2,1,0:T(8,128)(2,1)S(1)} %copy-done.8), channel_id=1, source_target_pairs={{0,10},{24,18},{1,11},{25,19},{2,8},{26,16},{3,9},{27,17},{8,2},{1... | collective-permute-start | bytes 786440 | tf_op jit(solution)/shard_map/ppermute | solution.py:100
  46.5 1.6 collective-permute-done.4
  48.0 1.9 collective-permute-start.9
  49.9 2.1 collective-permute-done.5
  52.1 4.3 %collective-permute-done.7 = bf16[32,16,256]{2,1,0:T(8,128)(2,1)S(1)} collective-permute-done((bf16[32,16,256]{2,1,0:T(8,128)(2,1)S(1)}, bf16[32,16,256]{2,1,0:T(8,128)(2,1)S(1)}, u32[]{:S(2)}, u32[]{:S(2)}) %collective-permute-start.7) | collective-permute-done | bytes 262176 | tf_op jit(solution)/shard_map/ppermute | solution.py:100
  56.4 5.6 %collective-permute-done.8 = bf16[32,16,256]{2,1,0:T(8,128)(2,1)S(1)} collective-permute-done((bf16[32,16,256]{2,1,0:T(8,128)(2,1)S(1)}, bf16[32,16,256]{2,1,0:T(8,128)(2,1)S(1)}, u32[]{:S(2)}, u32[]{:S(2)}) %collective-permute-start.8) | collective-permute-done | bytes 262176 | tf_op jit(solution)/shard_map/ppermute | solution.py:100
  62.0 4.4 %collective-permute-done.9 = bf16[32,16,256]{2,1,0:T(8,128)(2,1)S(1)} collective-permute-done((bf16[32,16,256]{2,1,0:T(8,128)(2,1)S(1)}, bf16[32,16,256]{2,1,0:T(8,128)(2,1)S(1)}, u32[]{:S(2)}, u32[]{:S(2)}) %collective-permute-start.9) | collective-permute-done | bytes 262176 | tf_op jit(solution)/shard_map/ppermute | solution.py:100
  66.6 1.4 fusion.12
  68.2 1.9 collective-permute-start.19
  70.1 1.4 collective-permute-start.18
  71.5 2.3 collective-permute-start.17
  75.1 5.1 %collective-permute-done.19 = bf16[32,16,256]{2,1,0:T(8,128)(2,1)S(1)} collective-permute-done((bf16[32,16,256]{2,1,0:T(8,128)(2,1)S(1)}, bf16[32,16,256]{2,1,0:T(8,128)(2,1)S(1)}, u32[]{:S(2)}, u32[]{:S(2)}) %collective-permute-start.19) | collective-permute-done | bytes 262176 | tf_op jit(solution)/shard_map/ppermute | solution.py:100
  80.2 0.9 collective-permute-start.14
  81.1 8.4 %collective-permute-done.18 = bf16[32,16,256]{2,1,0:T(8,128)(2,1)S(1)} collective-permute-done((bf16[32,16,256]{2,1,0:T(8,128)(2,1)S(1)}, bf16[32,16,256]{2,1,0:T(8,128)(2,1)S(1)}, u32[]{:S(2)}, u32[]{:S(2)}) %collective-permute-start.18) | collective-permute-done | bytes 262176 | tf_op jit(solution)/shard_map/ppermute | solution.py:100
  89.4 1.2 collective-permute-start.13
  91.3 2.8 %collective-permute-done.17 = bf16[32,16,256]{2,1,0:T(8,128)(2,1)S(1)} collective-permute-done((bf16[32,16,256]{2,1,0:T(8,128)(2,1)S(1)}, bf16[32,16,256]{2,1,0:T(8,128)(2,1)S(1)}, u32[]{:S(2)}, u32[]{:S(2)}) %collective-permute-start.17) | collective-permute-done | bytes 262176 | tf_op jit(solution)/shard_map/ppermute | solution.py:100
  94.0 4.3 %collective-permute-done.16 = bf16[32,16,256]{2,1,0:T(8,128)(2,1)S(1)} collective-permute-done((bf16[32,16,256]{2,1,0:T(8,128)(2,1)S(1)}, bf16[32,16,256]{2,1,0:T(8,128)(2,1)S(1)}, u32[]{:S(2)}, u32[]{:S(2)}) %collective-permute-start.16) | collective-permute-done | bytes 262176 | tf_op jit(solution)/shard_map/ppermute | solution.py:100
  98.3 1.4 collective-permute-done.13
  100.6 1.5 multiply_bitcast_fusion
  102.9 5.7 %collective-permute-start.12 = (bf16[8,256,256]{2,1,0:T(8,128)(2,1)S(1)}, bf16[8,256,256]{2,1,0:T(8,128)(2,1)S(1)}, u32[]{:S(2)}, u32[]{:S(2)}) collective-permute-start(bf16[8,256,256]{2,1,0:T(8,128)(2,1)S(1)} %convolution_convert_fusion.1), channel_id=1, source_target_pairs={{0,24},{24,0},{1,25},{25,1},{2,26},{26,2},{3,27},{27,3},{4,28},{28... | collective-permute-start | bytes 3145736 | tf_op jit(solution)/shard_map/ppermute | solution.py:107
  111.5 0.8 collective-permute-start.38
  112.5 3.7 %collective-permute-start.37 = (bf16[8,4,16,256]{3,0,2,1:T(8,128)(2,1)S(1)}, bf16[8,4,16,256]{3,0,2,1:T(8,128)(2,1)S(1)}, u32[]{:S(2)}, u32[]{:S(2)}) collective-permute-start(bf16[8,4,16,256]{3,0,2,1:T(8,128)(2,1)S(1)} %bitcast.242), channel_id=1, source_target_pairs={{0,24},{24,0},{8,16},{16,8},{1,25},{25,1},{9,17},{17,9},{2,26},{26... | collective-permute-start | bytes 786440 | tf_op jit(solution)/shard_map/ppermute | solution.py:115
  116.2 16.5 %collective-permute-done.12 = bf16[8,256,256]{2,1,0:T(8,128)(2,1)S(1)} collective-permute-done((bf16[8,256,256]{2,1,0:T(8,128)(2,1)S(1)}, bf16[8,256,256]{2,1,0:T(8,128)(2,1)S(1)}, u32[]{:S(2)}, u32[]{:S(2)}) %collective-permute-start.12) | collective-permute-done | bytes 1048608 | tf_op jit(solution)/shard_map/ppermute | solution.py:107
  133.7 1.7 collective-permute-start.22
  136.5 2.0 collective-permute-done.21
  138.5 1.2 collective-permute-start.23
  139.7 32.7 %collective-permute-start.24 = (bf16[8,32,256]{2,0,1:T(8,128)(2,1)S(1)}, bf16[8,32,256]{2,0,1:T(8,128)(2,1)S(1)}, u32[]{:S(2)}, u32[]{:S(2)}) collective-permute-start(bf16[8,32,256]{2,0,1:T(8,128)(2,1)S(1)} %bitcast.250), channel_id=1, source_target_pairs={{0,8},{24,16},{1,9},{25,17},{2,10},{26,18},{3,11},{27,19},{8,0},{1... | collective-permute-start | bytes 393224 | tf_op jit(solution)/shard_map/ppermute | solution.py:100
  172.4 4.1 %collective-permute-start.25 = (bf16[8,32,256]{2,0,1:T(8,128)(2,1)S(1)}, bf16[8,32,256]{2,0,1:T(8,128)(2,1)S(1)}, u32[]{:S(2)}, u32[]{:S(2)}) collective-permute-start(bf16[8,32,256]{2,0,1:T(8,128)(2,1)S(1)} %bitcast.249), channel_id=1, source_target_pairs={{0,9},{24,17},{1,8},{25,16},{2,11},{26,19},{3,10},{27,18},{8,1},{1... | collective-permute-start | bytes 393224 | tf_op jit(solution)/shard_map/ppermute | solution.py:100
  176.7 2.3 collective-permute-start.26
  179.0 0.9 collective-permute-done.25
  179.9 5.1 %collective-permute-start.27 = (bf16[8,32,256]{2,0,1:T(8,128)(2,1)S(1)}, bf16[8,32,256]{2,0,1:T(8,128)(2,1)S(1)}, u32[]{:S(2)}, u32[]{:S(2)}) collective-permute-start(bf16[8,32,256]{2,0,1:T(8,128)(2,1)S(1)} %bitcast.247), channel_id=1, source_target_pairs={{0,11},{24,19},{1,10},{25,18},{2,9},{26,17},{3,8},{27,16},{8,3},{1... | collective-permute-start | bytes 393224 | tf_op jit(solution)/shard_map/ppermute | solution.py:100
  185.6 1.3 collective-permute-start.29
  187.0 4.1 %collective-permute-done.27 = bf16[8,32,256]{2,0,1:T(8,128)(2,1)S(1)} collective-permute-done((bf16[8,32,256]{2,0,1:T(8,128)(2,1)S(1)}, bf16[8,32,256]{2,0,1:T(8,128)(2,1)S(1)}, u32[]{:S(2)}, u32[]{:S(2)}) %collective-permute-start.27) | collective-permute-done | bytes 131104 | tf_op jit(solution)/shard_map/ppermute | solution.py:100
  191.1 1.7 collective-permute-start.30
  192.8 1.5 collective-permute-start.28
  194.8 1.6 collective-permute-start.40
  196.3 1.7 collective-permute-start.41
  198.0 7.9 %collective-permute-done.30 = bf16[8,4,16,256]{3,0,2,1:T(8,128)(2,1)S(1)} collective-permute-done((bf16[8,4,16,256]{3,0,2,1:T(8,128)(2,1)S(1)}, bf16[8,4,16,256]{3,0,2,1:T(8,128)(2,1)S(1)}, u32[]{:S(2)}, u32[]{:S(2)}) %collective-permute-start.30) | collective-permute-done | bytes 262176 | tf_op jit(solution)/shard_map/ppermute | solution.py:115
  205.9 2.2 collective-permute-start.42
  208.7 1.5 collective-permute-start.31
  210.3 2.0 collective-permute-start.33
  212.6 3.2 %collective-permute-done.31 = bf16[2,8,16,256]{3,1,2,0:T(8,128)(2,1)S(1)} collective-permute-done((bf16[2,8,16,256]{3,1,2,0:T(8,128)(2,1)S(1)}, bf16[2,8,16,256]{3,1,2,0:T(8,128)(2,1)S(1)}, u32[]{:S(2)}, u32[]{:S(2)}) %collective-permute-start.31) | collective-permute-done | bytes 131104 | tf_op jit(solution)/shard_map/ppermute | solution.py:89
  216.9 2.0 collective-permute-done.33
  220.8 2.1 collective-permute-start.34
  223.1 1.5 collective-permute-start.36
  224.6 2.0 collective-permute-start.43
  227.1 2.3 collective-permute-done.34
  229.4 1.6 collective-permute-start.45
  231.1 1.7 collective-permute-done.35
  233.2 1.8 collective-permute-done.43
  235.2 3.2 %collective-permute-done.44 = bf16[16,32,256]{2,1,0:T(8,128)(2,1)S(1)} collective-permute-done((bf16[16,32,256]{2,1,0:T(8,128)(2,1)S(1)}, bf16[16,32,256]{2,1,0:T(8,128)(2,1)S(1)}, u32[]{:S(2)}, u32[]{:S(2)}) %collective-permute-start.44) | collective-permute-done | bytes 262176 | tf_op jit(solution)/shard_map/ppermute | solution.py:89
  238.7 1.3 copy-done.3
  (197 shorter events, 23.2 us)
Async XLA Ops:
  0.0 1.6 copy-start
  1.9 27.6 %collective-permute-start.2 = (bf16[32,32,256]{2,1,0:T(8,128)(2,1)S(1)}, bf16[32,32,256]{2,1,0:T(8,128)(2,1)}, u32[]{:S(2)}, u32[]{:S(2)}) collective-permute-start(bf16[32,32,256]{2,1,0:T(8,128)(2,1)S(1)} %bitcast.236), channel_id=1, source_target_pairs={{0,3},{1,2},{2,1},{3,0},{4,7},{5,6},{6,5},{7,4},{8,11},{9,10},{10,... | collective-permute-start | bytes 1572872 | tf_op jit(solution)/shard_map/ppermute | solution.py:89
  6.5 23.0 %collective-permute-start.1 = (bf16[32,32,256]{2,1,0:T(8,128)(2,1)S(1)}, bf16[32,32,256]{2,1,0:T(8,128)(2,1)}, u32[]{:S(2)}, u32[]{:S(2)}) collective-permute-start(bf16[32,32,256]{2,1,0:T(8,128)(2,1)S(1)} %bitcast.237), channel_id=1, source_target_pairs={{0,2},{1,3},{2,0},{3,1},{4,6},{5,7},{6,4},{7,5},{8,10},{9,11},{10,... | collective-permute-start | bytes 1572872 | tf_op jit(solution)/shard_map/ppermute | solution.py:89
  7.3 3.2 %copy-start.5 = (bf16[4,128,128]{2,1,0:T(8,128)(2,1)S(1)}, bf16[4,128,128]{2,1,0:T(8,128)(2,1)}, u32[]{:S(2)}) copy-start(bf16[4,128,128]{2,1,0:T(8,128)(2,1)} %param.10) | copy-start | bytes 393220
  7.3 3.6 %copy-start.13 = (f32[128]{0:T(128)S(1)}, f32[128]{0:T(128)}, u32[]{:S(2)}) copy-start(f32[128]{0:T(128)} %param.9) | copy-start | bytes 1540
  8.4 6.6 %copy-start.11 = (bf16[128,128]{1,0:T(8,128)(2,1)S(1)}, bf16[128,128]{1,0:T(8,128)(2,1)}, u32[]{:S(2)}) copy-start(bf16[128,128]{1,0:T(8,128)(2,1)} %param.13) | copy-start | bytes 98308
  8.4 21.0 %collective-permute-start = (bf16[32,32,256]{2,1,0:T(8,128)(2,1)}, bf16[32,32,256]{2,1,0:T(8,128)(2,1)}, u32[]{:S(2)}, u32[]{:S(2)}) collective-permute-start(bf16[32,32,256]{2,1,0:T(8,128)(2,1)} %bitcast.216), channel_id=1, source_target_pairs={{0,1},{1,0},{2,3},{3,2},{4,5},{5,4},{6,7},{7,6},{8,9},{9,8},{10,11... | collective-permute-start | bytes 1572872 | tf_op jit(solution)/shard_map/ppermute | solution.py:89
  8.5 6.8 %copy-start.12 = (bf16[128,128]{1,0:T(8,128)(2,1)S(1)}, bf16[128,128]{1,0:T(8,128)(2,1)}, u32[]{:S(2)}) copy-start(bf16[128,128]{1,0:T(8,128)(2,1)} %param.11) | copy-start | bytes 98308
  34.6 9.5 %collective-permute-start.3 = (bf16[32,16,256]{2,1,0:T(8,128)(2,1)}, bf16[32,16,256]{2,1,0:T(8,128)(2,1)S(1)}, u32[]{:S(2)}, u32[]{:S(2)}) collective-permute-start(bf16[32,16,256]{2,1,0:T(8,128)(2,1)} %get-tuple-element.37), channel_id=1, source_target_pairs={{0,1},{24,25},{1,0},{25,24},{2,3},{26,27},{3,2},{27,26},{8,9},{16,... | collective-permute-start | bytes 786440 | tf_op jit(solution)/shard_map/ppermute | solution.py:100
  36.1 11.9 %collective-permute-start.4 = (bf16[32,16,256]{2,1,0:T(8,128)(2,1)}, bf16[32,16,256]{2,1,0:T(8,128)(2,1)S(1)}, u32[]{:S(2)}, u32[]{:S(2)}) collective-permute-start(bf16[32,16,256]{2,1,0:T(8,128)(2,1)} %get-tuple-element.38), channel_id=1, source_target_pairs={{0,2},{24,26},{1,3},{25,27},{2,0},{26,24},{3,1},{27,25},{8,10},{16... | collective-permute-start | bytes 786440 | tf_op jit(solution)/shard_map/ppermute | solution.py:100
  37.3 14.7 %collective-permute-start.5 = (bf16[32,16,256]{2,1,0:T(8,128)(2,1)}, bf16[32,16,256]{2,1,0:T(8,128)(2,1)S(1)}, u32[]{:S(2)}, u32[]{:S(2)}) collective-permute-start(bf16[32,16,256]{2,1,0:T(8,128)(2,1)} %get-tuple-element.39), channel_id=1, source_target_pairs={{0,3},{24,27},{1,2},{25,26},{2,1},{26,25},{3,0},{27,24},{8,11},{16... | collective-permute-start | bytes 786440 | tf_op jit(solution)/shard_map/ppermute | solution.py:100
  38.1 2.4 %copy-start.4 = (bf16[32,16,256]{2,1,0:T(8,128)(2,1)S(1)}, bf16[32,16,256]{2,1,0:T(8,128)(2,1)}, u32[]{:S(2)}) copy-start(bf16[32,16,256]{2,1,0:T(8,128)(2,1)} %get-tuple-element.36) | copy-start | bytes 786436
  38.1 2.4 %copy-start.10 = (bf16[32,16,256]{2,1,0:T(8,128)(2,1)S(1)}, bf16[32,16,256]{2,1,0:T(8,128)(2,1)}, u32[]{:S(2)}) copy-start(bf16[32,16,256]{2,1,0:T(8,128)(2,1)} %get-tuple-element.40) | copy-start | bytes 786436
  38.1 4.1 %copy-start.9 = (bf16[32,16,256]{2,1,0:T(8,128)(2,1)S(1)}, bf16[32,16,256]{2,1,0:T(8,128)(2,1)}, u32[]{:S(2)}) copy-start(bf16[32,16,256]{2,1,0:T(8,128)(2,1)} %get-tuple-element.41) | copy-start | bytes 786436
  38.1 5.9 %copy-start.8 = (bf16[32,16,256]{2,1,0:T(8,128)(2,1)S(1)}, bf16[32,16,256]{2,1,0:T(8,128)(2,1)}, u32[]{:S(2)}) copy-start(bf16[32,16,256]{2,1,0:T(8,128)(2,1)} %get-tuple-element.42) | copy-start | bytes 786436
  38.1 9.9 %copy-start.7 = (bf16[32,16,256]{2,1,0:T(8,128)(2,1)S(1)}, bf16[32,16,256]{2,1,0:T(8,128)(2,1)}, u32[]{:S(2)}) copy-start(bf16[32,16,256]{2,1,0:T(8,128)(2,1)} %get-tuple-element.43) | copy-start | bytes 786436
  40.6 11.5 %collective-permute-start.6 = (bf16[32,16,256]{2,1,0:T(8,128)(2,1)S(1)}, bf16[32,16,256]{2,1,0:T(8,128)(2,1)S(1)}, u32[]{:S(2)}, u32[]{:S(2)}) collective-permute-start(bf16[32,16,256]{2,1,0:T(8,128)(2,1)S(1)} %copy-done.10), channel_id=1, source_target_pairs={{0,8},{24,16},{1,9},{25,17},{2,10},{26,18},{3,11},{27,19},{8,0},{1... | collective-permute-start | bytes 786440 | tf_op jit(solution)/shard_map/ppermute | solution.py:100
  42.2 14.1 %collective-permute-start.7 = (bf16[32,16,256]{2,1,0:T(8,128)(2,1)S(1)}, bf16[32,16,256]{2,1,0:T(8,128)(2,1)S(1)}, u32[]{:S(2)}, u32[]{:S(2)}) collective-permute-start(bf16[32,16,256]{2,1,0:T(8,128)(2,1)S(1)} %copy-done.9), channel_id=1, source_target_pairs={{0,9},{24,17},{1,8},{25,16},{2,11},{26,19},{3,10},{27,18},{8,1},{1... | collective-permute-start | bytes 786440 | tf_op jit(solution)/shard_map/ppermute | solution.py:100
  44.0 17.9 %collective-permute-start.8 = (bf16[32,16,256]{2,1,0:T(8,128)(2,1)S(1)}, bf16[32,16,256]{2,1,0:T(8,128)(2,1)S(1)}, u32[]{:S(2)}, u32[]{:S(2)}) collective-permute-start(bf16[32,16,256]{2,1,0:T(8,128)(2,1)S(1)} %copy-done.8), channel_id=1, source_target_pairs={{0,10},{24,18},{1,11},{25,19},{2,8},{26,16},{3,9},{27,17},{8,2},{1... | collective-permute-start | bytes 786440 | tf_op jit(solution)/shard_map/ppermute | solution.py:100
  48.0 18.3 %collective-permute-start.9 = (bf16[32,16,256]{2,1,0:T(8,128)(2,1)S(1)}, bf16[32,16,256]{2,1,0:T(8,128)(2,1)S(1)}, u32[]{:S(2)}, u32[]{:S(2)}) collective-permute-start(bf16[32,16,256]{2,1,0:T(8,128)(2,1)S(1)} %copy-done.7), channel_id=1, source_target_pairs={{0,11},{24,19},{1,10},{25,18},{2,9},{26,17},{3,8},{27,16},{8,3},{1... | collective-permute-start | bytes 786440 | tf_op jit(solution)/shard_map/ppermute | solution.py:100
  52.0 14.5 %copy-start.2 = (bf16[32,128,256]{2,1,0:T(8,128)(2,1)S(1)}, bf16[32,128,256]{2,1,0:T(8,128)(2,1)}, u32[]{:S(2)}) copy-start(bf16[32,128,256]{2,1,0:T(8,128)(2,1)} %get-tuple-element.45) | copy-start | bytes 6291460
  52.1 14.5 %copy-start.6 = (f32[32,256]{1,0:T(8,128)S(1)}, f32[32,256]{1,0:T(8,128)}, u32[]{:S(2)}) copy-start(f32[32,256]{1,0:T(8,128)} %dynamic-slice_convert_fusion.refs_4_) | copy-start | bytes 98308
  66.5 7.7 %collective-permute-start.10 = (bf16[256,8,256]{2,1,0:T(8,128)(2,1)S(1)}, bf16[256,8,256]{2,1,0:T(8,128)(2,1)S(1)}, u32[]{:S(2)}, u32[]{:S(2)}) collective-permute-start(bf16[256,8,256]{2,1,0:T(8,128)(2,1)S(1)} %slice.289), channel_id=1, source_target_pairs={{0,4},{4,0},{1,5},{5,1},{2,6},{6,2},{3,7},{7,3},{8,12},{12,8},{9,1... | collective-permute-start | bytes 3145736 | tf_op jit(solution)/shard_map/ppermute | solution.py:161
  68.2 12.0 %collective-permute-start.19 = (bf16[32,16,256]{2,1,0:T(8,128)(2,1)S(1)}, bf16[32,16,256]{2,1,0:T(8,128)(2,1)S(1)}, u32[]{:S(2)}, u32[]{:S(2)}) collective-permute-start(bf16[32,16,256]{2,1,0:T(8,128)(2,1)S(1)} %get-tuple-element.67), channel_id=1, source_target_pairs={{0,11},{24,19},{1,10},{25,18},{2,9},{26,17},{3,8},{27,16},{8,3},{1... | collective-permute-start | bytes 786440 | tf_op jit(solution)/shard_map/ppermute | solution.py:100
  70.1 19.4 %collective-permute-start.18 = (bf16[32,16,256]{2,1,0:T(8,128)(2,1)S(1)}, bf16[32,16,256]{2,1,0:T(8,128)(2,1)S(1)}, u32[]{:S(2)}, u32[]{:S(2)}) collective-permute-start(bf16[32,16,256]{2,1,0:T(8,128)(2,1)S(1)} %get-tuple-element.68), channel_id=1, source_target_pairs={{0,10},{24,18},{1,11},{25,19},{2,8},{26,16},{3,9},{27,17},{8,2},{1... | collective-permute-start | bytes 786440 | tf_op jit(solution)/shard_map/ppermute | solution.py:100
  71.5 22.5 %collective-permute-start.17 = (bf16[32,16,256]{2,1,0:T(8,128)(2,1)S(1)}, bf16[32,16,256]{2,1,0:T(8,128)(2,1)S(1)}, u32[]{:S(2)}, u32[]{:S(2)}) collective-permute-start(bf16[32,16,256]{2,1,0:T(8,128)(2,1)S(1)} %get-tuple-element.69), channel_id=1, source_target_pairs={{0,9},{24,17},{1,8},{25,16},{2,11},{26,19},{3,10},{27,18},{8,1},{1... | collective-permute-start | bytes 786440 | tf_op jit(solution)/shard_map/ppermute | solution.py:100
  73.8 24.5 %collective-permute-start.16 = (bf16[32,16,256]{2,1,0:T(8,128)(2,1)S(1)}, bf16[32,16,256]{2,1,0:T(8,128)(2,1)S(1)}, u32[]{:S(2)}, u32[]{:S(2)}) collective-permute-start(bf16[32,16,256]{2,1,0:T(8,128)(2,1)S(1)} %get-tuple-element.70), channel_id=1, source_target_pairs={{0,8},{24,16},{1,9},{25,17},{2,10},{26,18},{3,11},{27,19},{8,0},{1... | collective-permute-start | bytes 786440 | tf_op jit(solution)/shard_map/ppermute | solution.py:100
  74.1 24.2 %collective-permute-start.15 = (bf16[32,16,256]{2,1,0:T(8,128)(2,1)S(1)}, bf16[32,16,256]{2,1,0:T(8,128)(2,1)S(1)}, u32[]{:S(2)}, u32[]{:S(2)}) collective-permute-start(bf16[32,16,256]{2,1,0:T(8,128)(2,1)S(1)} %get-tuple-element.71), channel_id=1, source_target_pairs={{0,3},{24,27},{1,2},{25,26},{2,1},{26,25},{3,0},{27,24},{8,11},{16... | collective-permute-start | bytes 786440 | tf_op jit(solution)/shard_map/ppermute | solution.py:100
  80.2 18.1 %collective-permute-start.14 = (bf16[32,16,256]{2,1,0:T(8,128)(2,1)S(1)}, bf16[32,16,256]{2,1,0:T(8,128)(2,1)S(1)}, u32[]{:S(2)}, u32[]{:S(2)}) collective-permute-start(bf16[32,16,256]{2,1,0:T(8,128)(2,1)S(1)} %get-tuple-element.72), channel_id=1, source_target_pairs={{0,2},{24,26},{1,3},{25,27},{2,0},{26,24},{3,1},{27,25},{8,10},{16... | collective-permute-start | bytes 786440 | tf_op jit(solution)/shard_map/ppermute | solution.py:100
  89.4 10.3 %collective-permute-start.13 = (bf16[32,16,256]{2,1,0:T(8,128)(2,1)S(1)}, bf16[32,16,256]{2,1,0:T(8,128)(2,1)S(1)}, u32[]{:S(2)}, u32[]{:S(2)}) collective-permute-start(bf16[32,16,256]{2,1,0:T(8,128)(2,1)S(1)} %get-tuple-element.73), channel_id=1, source_target_pairs={{0,1},{24,25},{1,0},{25,24},{2,3},{26,27},{3,2},{27,26},{8,9},{16,... | collective-permute-start | bytes 786440 | tf_op jit(solution)/shard_map/ppermute | solution.py:100
  99.8 0.7 copy-start.14
  100.0 9.2 %collective-permute-start.20 = (bf16[256,8,256]{2,1,0:T(8,128)(2,1)S(1)}, bf16[256,8,256]{2,1,0:T(8,128)(2,1)S(1)}, u32[]{:S(2)}, u32[]{:S(2)}) collective-permute-start(bf16[256,8,256]{2,1,0:T(8,128)(2,1)S(1)} %slice.291), channel_id=1, source_target_pairs={{0,4},{4,0},{1,5},{5,1},{2,6},{6,2},{3,7},{7,3},{8,12},{12,8},{9,1... | collective-permute-start | bytes 3145736 | tf_op jit(solution)/shard_map/ppermute | solution.py:161
  102.1 14.1 %collective-permute-start.11 = (bf16[8,256,256]{2,1,0:T(8,128)(2,1)S(1)}, bf16[8,256,256]{2,1,0:T(8,128)(2,1)S(1)}, u32[]{:S(2)}, u32[]{:S(2)}) collective-permute-start(bf16[8,256,256]{2,1,0:T(8,128)(2,1)S(1)} %convolution_convert_fusion.1), channel_id=1, source_target_pairs={{8,16},{16,8},{9,17},{17,9},{10,18},{18,10},{11,19},{19,11},{12,20... | collective-permute-start | bytes 3145736 | tf_op jit(solution)/shard_map/ppermute | solution.py:107
  102.9 29.9 %collective-permute-start.12 = (bf16[8,256,256]{2,1,0:T(8,128)(2,1)S(1)}, bf16[8,256,256]{2,1,0:T(8,128)(2,1)S(1)}, u32[]{:S(2)}, u32[]{:S(2)}) collective-permute-start(bf16[8,256,256]{2,1,0:T(8,128)(2,1)S(1)} %convolution_convert_fusion.1), channel_id=1, source_target_pairs={{0,24},{24,0},{1,25},{25,1},{2,26},{26,2},{3,27},{27,3},{4,28},{28... | collective-permute-start | bytes 3145736 | tf_op jit(solution)/shard_map/ppermute | solution.py:107
  110.4 82.4 %collective-permute-start.39 = (bf16[8,4,16,256]{3,0,2,1:T(8,128)(2,1)S(1)}, bf16[8,4,16,256]{3,0,2,1:T(8,128)(2,1)S(1)}, u32[]{:S(2)}, u32[]{:S(2)}) collective-permute-start(bf16[8,4,16,256]{3,0,2,1:T(8,128)(2,1)S(1)} %bitcast.240), channel_id=1, source_target_pairs={{0,16},{24,8},{8,24},{16,0},{1,17},{25,9},{9,25},{17,1},{2,18},{26... | collective-permute-start | bytes 786440 | tf_op jit(solution)/shard_map/ppermute | solution.py:115
  111.5 83.1 %collective-permute-start.38 = (bf16[8,4,16,256]{3,0,2,1:T(8,128)(2,1)S(1)}, bf16[8,4,16,256]{3,0,2,1:T(8,128)(2,1)S(1)}, u32[]{:S(2)}, u32[]{:S(2)}) collective-permute-start(bf16[8,4,16,256]{3,0,2,1:T(8,128)(2,1)S(1)} %bitcast.241), channel_id=1, source_target_pairs={{0,8},{24,16},{8,0},{16,24},{1,9},{25,17},{9,1},{17,25},{2,10},{26... | collective-permute-start | bytes 786440 | tf_op jit(solution)/shard_map/ppermute | solution.py:115
  112.5 81.7 %collective-permute-start.37 = (bf16[8,4,16,256]{3,0,2,1:T(8,128)(2,1)S(1)}, bf16[8,4,16,256]{3,0,2,1:T(8,128)(2,1)S(1)}, u32[]{:S(2)}, u32[]{:S(2)}) collective-permute-start(bf16[8,4,16,256]{3,0,2,1:T(8,128)(2,1)S(1)} %bitcast.242), channel_id=1, source_target_pairs={{0,24},{24,0},{8,16},{16,8},{1,25},{25,1},{9,17},{17,9},{2,26},{26... | collective-permute-start | bytes 786440 | tf_op jit(solution)/shard_map/ppermute | solution.py:115
  133.4 5.0 %collective-permute-start.21 = (bf16[8,32,256]{2,0,1:T(8,128)(2,1)S(1)}, bf16[8,32,256]{2,0,1:T(8,128)(2,1)S(1)}, u32[]{:S(2)}, u32[]{:S(2)}) collective-permute-start(bf16[8,32,256]{2,0,1:T(8,128)(2,1)S(1)} %bitcast.253), channel_id=1, source_target_pairs={{0,1},{24,25},{1,0},{25,24},{2,3},{26,27},{3,2},{27,26},{8,9},{16,... | collective-permute-start | bytes 393224 | tf_op jit(solution)/shard_map/ppermute | solution.py:100
  133.7 6.0 %collective-permute-start.22 = (bf16[8,32,256]{2,0,1:T(8,128)(2,1)S(1)}, bf16[8,32,256]{2,0,1:T(8,128)(2,1)S(1)}, u32[]{:S(2)}, u32[]{:S(2)}) collective-permute-start(bf16[8,32,256]{2,0,1:T(8,128)(2,1)S(1)} %bitcast.251), channel_id=1, source_target_pairs={{0,2},{24,26},{1,3},{25,27},{2,0},{26,24},{3,1},{27,25},{8,10},{16... | collective-permute-start | bytes 393224 | tf_op jit(solution)/shard_map/ppermute | solution.py:100
  138.5 33.9 %collective-permute-start.23 = (bf16[8,32,256]{2,0,1:T(8,128)(2,1)S(1)}, bf16[8,32,256]{2,0,1:T(8,128)(2,1)S(1)}, u32[]{:S(2)}, u32[]{:S(2)}) collective-permute-start(bf16[8,32,256]{2,0,1:T(8,128)(2,1)S(1)} %bitcast.252), channel_id=1, source_target_pairs={{0,3},{24,27},{1,2},{25,26},{2,1},{26,25},{3,0},{27,24},{8,11},{16... | collective-permute-start | bytes 393224 | tf_op jit(solution)/shard_map/ppermute | solution.py:100
  139.7 37.0 %collective-permute-start.24 = (bf16[8,32,256]{2,0,1:T(8,128)(2,1)S(1)}, bf16[8,32,256]{2,0,1:T(8,128)(2,1)S(1)}, u32[]{:S(2)}, u32[]{:S(2)}) collective-permute-start(bf16[8,32,256]{2,0,1:T(8,128)(2,1)S(1)} %bitcast.250), channel_id=1, source_target_pairs={{0,8},{24,16},{1,9},{25,17},{2,10},{26,18},{3,11},{27,19},{8,0},{1... | collective-permute-start | bytes 393224 | tf_op jit(solution)/shard_map/ppermute | solution.py:100
  172.4 7.5 %collective-permute-start.25 = (bf16[8,32,256]{2,0,1:T(8,128)(2,1)S(1)}, bf16[8,32,256]{2,0,1:T(8,128)(2,1)S(1)}, u32[]{:S(2)}, u32[]{:S(2)}) collective-permute-start(bf16[8,32,256]{2,0,1:T(8,128)(2,1)S(1)} %bitcast.249), channel_id=1, source_target_pairs={{0,9},{24,17},{1,8},{25,16},{2,11},{26,19},{3,10},{27,18},{8,1},{1... | collective-permute-start | bytes 393224 | tf_op jit(solution)/shard_map/ppermute | solution.py:100
  176.7 8.9 %collective-permute-start.26 = (bf16[8,32,256]{2,0,1:T(8,128)(2,1)S(1)}, bf16[8,32,256]{2,0,1:T(8,128)(2,1)S(1)}, u32[]{:S(2)}, u32[]{:S(2)}) collective-permute-start(bf16[8,32,256]{2,0,1:T(8,128)(2,1)S(1)} %bitcast.248), channel_id=1, source_target_pairs={{0,10},{24,18},{1,11},{25,19},{2,8},{26,16},{3,9},{27,17},{8,2},{1... | collective-permute-start | bytes 393224 | tf_op jit(solution)/shard_map/ppermute | solution.py:100
  179.9 11.2 %collective-permute-start.27 = (bf16[8,32,256]{2,0,1:T(8,128)(2,1)S(1)}, bf16[8,32,256]{2,0,1:T(8,128)(2,1)S(1)}, u32[]{:S(2)}, u32[]{:S(2)}) collective-permute-start(bf16[8,32,256]{2,0,1:T(8,128)(2,1)S(1)} %bitcast.247), channel_id=1, source_target_pairs={{0,11},{24,19},{1,10},{25,18},{2,9},{26,17},{3,8},{27,16},{8,3},{1... | collective-permute-start | bytes 393224 | tf_op jit(solution)/shard_map/ppermute | solution.py:100
  185.6 22.9 %collective-permute-start.29 = (bf16[8,4,16,256]{3,0,2,1:T(8,128)(2,1)S(1)}, bf16[8,4,16,256]{3,0,2,1:T(8,128)(2,1)S(1)}, u32[]{:S(2)}, u32[]{:S(2)}) collective-permute-start(bf16[8,4,16,256]{3,0,2,1:T(8,128)(2,1)S(1)} %bitcast.243), channel_id=1, source_target_pairs={{0,8},{24,16},{8,0},{16,24},{1,9},{25,17},{9,1},{17,25},{2,10},{26... | collective-permute-start | bytes 786440 | tf_op jit(solution)/shard_map/ppermute | solution.py:115
  191.1 14.9 %collective-permute-start.30 = (bf16[8,4,16,256]{3,0,2,1:T(8,128)(2,1)S(1)}, bf16[8,4,16,256]{3,0,2,1:T(8,128)(2,1)S(1)}, u32[]{:S(2)}, u32[]{:S(2)}) collective-permute-start(bf16[8,4,16,256]{3,0,2,1:T(8,128)(2,1)S(1)} %bitcast.245), channel_id=1, source_target_pairs={{0,16},{24,8},{8,24},{16,0},{1,17},{25,9},{9,25},{17,1},{2,18},{26... | collective-permute-start | bytes 786440 | tf_op jit(solution)/shard_map/ppermute | solution.py:115
  192.8 15.4 %collective-permute-start.28 = (bf16[8,4,16,256]{3,0,2,1:T(8,128)(2,1)S(1)}, bf16[8,4,16,256]{3,0,2,1:T(8,128)(2,1)S(1)}, u32[]{:S(2)}, u32[]{:S(2)}) collective-permute-start(bf16[8,4,16,256]{3,0,2,1:T(8,128)(2,1)S(1)} %bitcast.244), channel_id=1, source_target_pairs={{0,24},{24,0},{8,16},{16,8},{1,25},{25,1},{9,17},{17,9},{2,26},{26... | collective-permute-start | bytes 786440 | tf_op jit(solution)/shard_map/ppermute | solution.py:115
  194.8 15.6 %collective-permute-start.40 = (bf16[2,8,16,256]{3,1,2,0:T(8,128)(2,1)S(1)}, bf16[2,8,16,256]{3,1,2,0:T(8,128)(2,1)S(1)}, u32[]{:S(2)}, u32[]{:S(2)}) collective-permute-start(bf16[2,8,16,256]{3,1,2,0:T(8,128)(2,1)S(1)} %get-tuple-element.95), channel_id=1, source_target_pairs={{0,1},{1,0},{2,3},{3,2},{4,5},{5,4},{6,7},{7,6},{8,9},{9,8},{10,11... | collective-permute-start | bytes 393224 | tf_op jit(solution)/shard_map/ppermute | solution.py:89
  196.3 16.0 %collective-permute-start.41 = (bf16[2,8,16,256]{3,1,2,0:T(8,128)(2,1)S(1)}, bf16[2,8,16,256]{3,1,2,0:T(8,128)(2,1)S(1)}, u32[]{:S(2)}, u32[]{:S(2)}) collective-permute-start(bf16[2,8,16,256]{3,1,2,0:T(8,128)(2,1)S(1)} %get-tuple-element.96), channel_id=1, source_target_pairs={{0,2},{1,3},{2,0},{3,1},{4,6},{5,7},{6,4},{7,5},{8,10},{9,11},{10,... | collective-permute-start | bytes 393224 | tf_op jit(solution)/shard_map/ppermute | solution.py:89
  205.9 6.4 %collective-permute-start.42 = (bf16[2,8,16,256]{3,1,2,0:T(8,128)(2,1)S(1)}, bf16[2,8,16,256]{3,1,2,0:T(8,128)(2,1)S(1)}, u32[]{:S(2)}, u32[]{:S(2)}) collective-permute-start(bf16[2,8,16,256]{3,1,2,0:T(8,128)(2,1)S(1)} %get-tuple-element.93), channel_id=1, source_target_pairs={{0,3},{1,2},{2,1},{3,0},{4,7},{5,6},{6,5},{7,4},{8,11},{9,10},{10,... | collective-permute-start | bytes 393224 | tf_op jit(solution)/shard_map/ppermute | solution.py:89
  208.7 7.1 %collective-permute-start.31 = (bf16[2,8,16,256]{3,1,2,0:T(8,128)(2,1)S(1)}, bf16[2,8,16,256]{3,1,2,0:T(8,128)(2,1)S(1)}, u32[]{:S(2)}, u32[]{:S(2)}) collective-permute-start(bf16[2,8,16,256]{3,1,2,0:T(8,128)(2,1)S(1)} %get-tuple-element.101), channel_id=1, source_target_pairs={{0,1},{1,0},{2,3},{3,2},{4,5},{5,4},{6,7},{7,6},{8,9},{9,8},{10,11... | collective-permute-start | bytes 393224 | tf_op jit(solution)/shard_map/ppermute | solution.py:89
  210.1 6.8 %collective-permute-start.32 = (bf16[2,8,16,256]{3,1,2,0:T(8,128)(2,1)S(1)}, bf16[2,8,16,256]{3,1,2,0:T(8,128)(2,1)S(1)}, u32[]{:S(2)}, u32[]{:S(2)}) collective-permute-start(bf16[2,8,16,256]{3,1,2,0:T(8,128)(2,1)S(1)} %get-tuple-element.102), channel_id=1, source_target_pairs={{0,2},{1,3},{2,0},{3,1},{4,6},{5,7},{6,4},{7,5},{8,10},{9,11},{10,... | collective-permute-start | bytes 393224 | tf_op jit(solution)/shard_map/ppermute | solution.py:89
  210.3 8.6 %collective-permute-start.33 = (bf16[2,8,16,256]{3,1,2,0:T(8,128)(2,1)S(1)}, bf16[2,8,16,256]{3,1,2,0:T(8,128)(2,1)S(1)}, u32[]{:S(2)}, u32[]{:S(2)}) collective-permute-start(bf16[2,8,16,256]{3,1,2,0:T(8,128)(2,1)S(1)} %get-tuple-element.99), channel_id=1, source_target_pairs={{0,3},{1,2},{2,1},{3,0},{4,7},{5,6},{6,5},{7,4},{8,11},{9,10},{10,... | collective-permute-start | bytes 393224 | tf_op jit(solution)/shard_map/ppermute | solution.py:89
  220.8 8.6 %collective-permute-start.34 = (bf16[16,32,256]{2,1,0:T(8,128)(2,1)S(1)}, bf16[16,32,256]{2,1,0:T(8,128)(2,1)S(1)}, u32[]{:S(2)}, u32[]{:S(2)}) collective-permute-start(bf16[16,32,256]{2,1,0:T(8,128)(2,1)S(1)} %get-tuple-element.83), channel_id=1, source_target_pairs={{0,1},{1,0},{2,3},{3,2},{4,5},{5,4},{6,7},{7,6},{8,9},{9,8},{10,11... | collective-permute-start | bytes 786440 | tf_op jit(solution)/shard_map/ppermute | solution.py:89
  223.0 9.7 %collective-permute-start.35 = (bf16[16,32,256]{2,1,0:T(8,128)(2,1)S(1)}, bf16[16,32,256]{2,1,0:T(8,128)(2,1)S(1)}, u32[]{:S(2)}, u32[]{:S(2)}) collective-permute-start(bf16[16,32,256]{2,1,0:T(8,128)(2,1)S(1)} %get-tuple-element.82), channel_id=1, source_target_pairs={{0,2},{1,3},{2,0},{3,1},{4,6},{5,7},{6,4},{7,5},{8,10},{9,11},{10,... | collective-permute-start | bytes 786440 | tf_op jit(solution)/shard_map/ppermute | solution.py:89
  223.1 9.8 %collective-permute-start.36 = (bf16[16,32,256]{2,1,0:T(8,128)(2,1)S(1)}, bf16[16,32,256]{2,1,0:T(8,128)(2,1)S(1)}, u32[]{:S(2)}, u32[]{:S(2)}) collective-permute-start(bf16[16,32,256]{2,1,0:T(8,128)(2,1)S(1)} %get-tuple-element.81), channel_id=1, source_target_pairs={{0,3},{1,2},{2,1},{3,0},{4,7},{5,6},{6,5},{7,4},{8,11},{9,10},{10,... | collective-permute-start | bytes 786440 | tf_op jit(solution)/shard_map/ppermute | solution.py:89
  224.6 10.5 %collective-permute-start.43 = (bf16[16,32,256]{2,1,0:T(8,128)(2,1)S(1)}, bf16[16,32,256]{2,1,0:T(8,128)(2,1)S(1)}, u32[]{:S(2)}, u32[]{:S(2)}) collective-permute-start(bf16[16,32,256]{2,1,0:T(8,128)(2,1)S(1)} %get-tuple-element.77), channel_id=1, source_target_pairs={{0,1},{1,0},{2,3},{3,2},{4,5},{5,4},{6,7},{7,6},{8,9},{9,8},{10,11... | collective-permute-start | bytes 786440 | tf_op jit(solution)/shard_map/ppermute | solution.py:89
  226.6 11.8 %collective-permute-start.44 = (bf16[16,32,256]{2,1,0:T(8,128)(2,1)S(1)}, bf16[16,32,256]{2,1,0:T(8,128)(2,1)S(1)}, u32[]{:S(2)}, u32[]{:S(2)}) collective-permute-start(bf16[16,32,256]{2,1,0:T(8,128)(2,1)S(1)} %get-tuple-element.76), channel_id=1, source_target_pairs={{0,2},{1,3},{2,0},{3,1},{4,6},{5,7},{6,4},{7,5},{8,10},{9,11},{10,... | collective-permute-start | bytes 786440 | tf_op jit(solution)/shard_map/ppermute | solution.py:89
  226.7 13.3 %copy-start.1 = (bf16[32,128,256]{2,1,0:T(8,128)(2,1)S(1)}, bf16[32,128,256]{2,1,0:T(8,128)(2,1)}, u32[]{:S(2)}) copy-start(bf16[32,128,256]{2,1,0:T(8,128)(2,1)} %param.7) | copy-start | bytes 6291460
  229.4 9.1 %collective-permute-start.45 = (bf16[16,32,256]{2,1,0:T(8,128)(2,1)S(1)}, bf16[16,32,256]{2,1,0:T(8,128)(2,1)S(1)}, u32[]{:S(2)}, u32[]{:S(2)}) collective-permute-start(bf16[16,32,256]{2,1,0:T(8,128)(2,1)S(1)} %get-tuple-element.75), channel_id=1, source_target_pairs={{0,3},{1,2},{2,1},{3,0},{4,7},{5,6},{6,5},{7,4},{8,11},{9,10},{10,... | collective-permute-start | bytes 786440 | tf_op jit(solution)/shard_map/ppermute | solution.py:89
  238.7 1.3 copy-start.3
